TPU v7x, 256 devices: a whole 4x4x8 slice. The times are simulated.
256 devices in a mesh: dp: 8 (over z), expert: 32 (over x, y, core).
Axes of the slice: x: 4, y: 4, z: 8, core: 2. Of those that a mesh axis runs over, the one named last changes fastest.
Arguments:
- tokens: bfloat16 [65536, 2048], P(('dp', 'expert')), may hold values from -6 to 6
- expert_ranks: int32 [32, 65536], P(None, ('dp', 'expert')), may hold values from 0 to 65535, as said below
- capacity: int32 [32], replicated, may hold values from 512 to 1024, as said below
- weight_in: bfloat16 [32, 2048, 8192], P('expert', None, 'dp'), may hold values from -0.125 to 0.125
- weight_out: bfloat16 [32, 8192, 2048], P('expert', 'dp'), may hold values from -0.0625 to 0.0625
- gate_weights: float32 [32, 1024], P('expert', 'dp'), may hold values from 0.05 to 1
Outputs:
- combined: bfloat16 [65536, 2048], P(('dp', 'expert'))
Inputs may be any that keep to these rules, and one draw needn't show every extreme that they name: `expert_ranks`: for each expert the ranks are a permutation of 0 to 65535. Of the 256 tokens of one device, at most 8 have rank under 1024 for one expert; for an expert of capacity 1024, some devices have exactly 8. At least one expert has capacity 1024.
All inputs are finite; a program needn't handle non-finite values.
Results may differ from a plain program's by a relative error of at most 0.0053.
Values may be sent and summed in bfloat16 or wider, within the bound.
No kernel may reach another device: no remote copies, remote signals or barrier semaphores. Data moves between devices by JAX's collectives and lax.ppermute only.
A program may use at most 64 MiB of HBM per device.

v0:
```python
import jax
import jax.numpy as jnp
from jax import lax
from jax.sharding import Mesh
from jax.sharding import PartitionSpec as P

MOST = 8
EXPERT = ("expert_0", "expert_1", "expert_2")
DP_EXPERT = ("dp", "expert_0", "expert_1", "expert_2")


def laid_out(blocks, dim):
    blocks = jnp.moveaxis(blocks, 0, dim)
    dims = blocks.shape
    return blocks.reshape(*dims[:dim], dims[dim] * dims[dim + 1], *dims[dim + 2 :])


def gather_in_order(array, axes, order):
    blocks = array[None]
    for k in order:
        blocks = lax.all_gather(blocks, axes[k], axis=0, tiled=True)
    block = [lax.axis_size(axes[k]) for k in reversed(order)]
    blocks = blocks.reshape(*block, *array.shape)
    turned = sorted(range(len(order)), key=lambda place: order[len(order) - 1 - place])
    return blocks.transpose(*turned, *range(len(order), blocks.ndim)).reshape(-1, *array.shape)


def gather_axes(array, axes, order, dim):
    return laid_out(gather_in_order(array, axes, order), dim)


def on_device(tokens, expert_ranks, capacity, weight_in, weight_out, gate_weights):
    dp_count = lax.axis_size("dp")
    expert_count = lax.axis_size(EXPERT)
    token_count, width = tokens.shape
    slots_all = gate_weights.shape[1] * dp_count
    chosen = expert_ranks < capacity[:, None]
    chosen_int = chosen.astype(jnp.int32)
    counts = jnp.sum(chosen_int, axis=1)
    before = jnp.cumsum(chosen_int, axis=1) - chosen_int
    places = lax.broadcasted_iota(jnp.int32, (expert_count, MOST, token_count), 1)
    pack_table = jnp.logical_and(chosen[:, None, :], before[:, None, :] == places)
    pack_table = pack_table.astype(jnp.bfloat16).reshape(expert_count * MOST, token_count)
    packed = jnp.dot(pack_table, tokens, preferred_element_type=jnp.float32).astype(jnp.bfloat16)
    arrived_rows = lax.all_to_all(
        packed.reshape(expert_count, MOST, width), EXPERT, split_axis=0, concat_axis=0, tiled=True
    )
    own_expert = lax.axis_index(EXPERT)
    expert_mask = (lax.broadcasted_iota(jnp.int32, (expert_count,), 0) == own_expert).astype(
        jnp.int32
    )
    count_table = gather_axes(counts[None, :], DP_EXPERT, (1, 0, 2, 3), 0)
    column = jnp.sum(count_table * expert_mask[None, :], axis=1)
    earlier_sums = jnp.cumsum(column) - column
    row_first = lax.axis_index("dp") * expert_count
    starts = lax.dynamic_slice_in_dim(earlier_sums, row_first, expert_count, 0)
    arrived = lax.dynamic_slice_in_dim(column, row_first, expert_count, 0)
    within = lax.broadcasted_iota(jnp.int32, (expert_count, MOST), 1)
    target = jnp.where(within < arrived[:, None], starts[:, None] + within, -1).reshape(
        expert_count * MOST
    )
    slot_ids = lax.broadcasted_iota(jnp.int32, (expert_count * MOST, slots_all), 1)
    place_table = (target[:, None] == slot_ids).astype(jnp.bfloat16)
    flat_rows = arrived_rows.reshape(expert_count * MOST, width)
    local_rows = lax.dot_general(
        place_table, flat_rows, (((0,), (0,)), ((), ())), preferred_element_type=jnp.float32
    ).astype(jnp.bfloat16)
    first_weight = weight_in[0]
    second_weight = weight_out[0]
    slot_rows = lax.psum(local_rows, "dp").astype(jnp.float32).astype(jnp.bfloat16)
    hidden = jnp.maximum(
        jnp.dot(slot_rows, first_weight, preferred_element_type=jnp.float32), 0.0
    ).astype(jnp.bfloat16)
    out_share = lax.psum_scatter(
        jnp.dot(hidden, second_weight, preferred_element_type=jnp.float32),
        "dp",
        scatter_dimension=0,
        tiled=True,
    )
    scaled = (gate_weights[0][:, None] * out_share).astype(jnp.bfloat16)
    returned = jnp.dot(
        place_table,
        lax.all_gather(scaled, "dp", axis=0, tiled=True),
        preferred_element_type=jnp.float32,
    )
    sent_back = returned.astype(jnp.bfloat16).reshape(expert_count, MOST, width)
    results = lax.all_to_all(sent_back, EXPERT, split_axis=0, concat_axis=0, tiled=True)
    flat_results = results.reshape(expert_count * MOST, width)
    combined = lax.dot_general(
        pack_table, flat_results, (((0,), (0,)), ((), ())), preferred_element_type=jnp.float32
    )
    return combined.astype(jnp.bfloat16)


def solution(mesh):
    split = Mesh(
        mesh.devices.reshape(mesh.shape["dp"], 4, 4, 2), ("dp", "expert_0", "expert_1", "expert_2")
    )
    placed = (
        P(DP_EXPERT, None),
        P(None, DP_EXPERT),
        P(),
        P(EXPERT, None, "dp"),
        P(EXPERT, "dp", None),
        P(EXPERT, "dp"),
    )
    return jax.shard_map(
        on_device, mesh=split, in_specs=placed, out_specs=P(DP_EXPERT, None), check_vma=False
    )
```

profile of v0, /device:TPU:1, one launch (start us, length us, event | category | flops | bytes accessed | tf_op | source)
XLA Modules:
  0.0 387.2 jit_solution(9165938855514273906)
XLA Ops:
  6.6 1.0 convert_reduce_fusion
  7.7 0.6 reduce-window.15
  8.3 0.2 slice_reduce_fusion
  8.6 1.5 fusion.5
  10.0 8.6 %all-to-all-start = ((bf16[32,8,2048]{2,1,0:T(8,128)(2,1)}), bf16[32,8,2048]{2,1,0:T(8,128)(2,1)S(1)}, u32[]{:S(2)}, u32[]{:S(2)}) async-start(bf16[32,8,2048]{2,1,0:T(8,128)(2,1)} %fusion.5), calls=%async_computation | async-start | bytes 2097152 | tf_op jit(solution)/shard_map/all_to_all | solution.py:45
  18.7 0.7 dynamic-slice
  20.1 0.2 dynamic-update-slice
  20.3 15.2 %all-reduce = s32[128]{0:T(128)S(1)} all-reduce(s32[128]{0:T(128)S(1)} %dynamic-update-slice), channel_id=2, replica_groups=mesh['dp'=8,'expert_0'=4,'expert_1'=4,'expert_2'=2] {'expert_0'}, use_global_device_ids=true, to_apply=%add | all-reduce | flops 128 | bytes 1024
  35.6 19.8 %all_gather.16 = s32[32,1,32]{2,1,0:T(1,128)S(1)} all-gather(s32[4,1,32]{2,1,0:T(1,128)S(1)} %bitcast.53), channel_id=1, replica_groups=mesh['dp'=8,'expert_0'=4,'expert_1'=4,'expert_2'=2] {'dp'}, dimensions={0}, use_global_device_ids=true | all-gather | bytes 4608 | tf_op jit(solution)/shard_map/all_gather | solution.py:21
  55.4 9.1 %all_gather.17 = s32[128,1,32]{2,1,0:T(1,128)S(1)} all-gather(s32[32,1,32]{2,1,0:T(1,128)S(1)} %all_gather.16), channel_id=1, replica_groups=mesh['dp'=8,'expert_0'=4,'expert_1'=4,'expert_2'=2] {'expert_1'}, dimensions={0}, use_global_device_ids=true | all-gather | bytes 20480 | tf_op jit(solution)/shard_map/all_gather | solution.py:21
  64.6 12.1 %all_gather.18 = s32[256,1,32]{0,2,1:T(8,128)S(1)} all-gather(s32[128,1,32]{0,2,1:T(8,128)S(1)} %copy.28), channel_id=1, replica_groups=mesh['dp'=8,'expert_0'=4,'expert_1'=4,'expert_2'=2] {'expert_2'}, dimensions={0}, use_global_device_ids=true | all-gather | bytes 49152 | tf_op jit(solution)/shard_map/all_gather | solution.py:21
  76.8 1.2 multiply_reduce_fusion
  78.0 0.3 copy.30
  78.6 0.3 reduce-window.19
  79.7 3.4 convolution_convert_fusion
  83.2 103.9 %all-reduce.3.cloned.1.call-done = bf16[1024,2048]{1,0:T(8,128)(2,1)} async-done(((bf16[1024,2048]{1,0:T(8,128)(2,1)}), bf16[1024,2048]{1,0:T(8,128)(2,1)}) %all-reduce.3.cloned.1.call-update) | async-done | bytes 4194320 | tf_op jit(solution)/shard_map/psum | solution.py:70
  187.1 8.1 %maximum_convert_fusion = bf16[1024,1024]{1,0:T(8,128)(2,1)S(1)} fusion(bf16[1024,2048]{1,0:T(8,128)(2,1)} %all-reduce.3.cloned.1.call-done, bf16[1,2048,1024]{2,1,0:T(8,128)(2,1)} %param.9), kind=kOutput, calls=%fused_computation.4 | convolution fusion | flops 4297064448 | bytes 10485760 | tf_op jit(solution)/shard_map/dot_general | solution.py:72
  195.2 6.7 %fusion = f32[1024,2048]{1,0:T(8,128)} fusion(bf16[1024,1024]{1,0:T(8,128)(2,1)S(1)} %maximum_convert_fusion, bf16[1,1024,2048]{2,1,0:T(8,128)(2,1)S(1)} %copy-done.2), kind=kOutput, calls=%fused_computation | convolution fusion | flops 4294967296 | bytes 14680064 | tf_op jit(solution)/shard_map/dot_general | solution.py:75
  201.9 93.8 %reduce-scatter.2.cloned.1.call-done = f32[128,2048]{1,0:T(8,128)} async-done(((f32[1024,2048]{1,0:T(8,128)}), f32[128,2048]{1,0:T(8,128)}) %reduce-scatter.2.cloned.1.call-update) | async-done | bytes 1048592 | tf_op jit(solution)/shard_map/reduce_scatter | solution.py:74
  295.8 2.1 multiply_convert_fusion
  297.9 53.4 %all-gather.3.cloned.1.call-done = bf16[1024,2048]{1,0:T(8,128)(2,1)} async-done(((bf16[128,2048]{1,0:T(8,128)(2,1)}), bf16[1024,2048]{1,0:T(8,128)(2,1)}) %all-gather.3.cloned.1.call-update) | async-done | bytes 4194320 | tf_op jit(solution)/shard_map/all_gather | solution.py:83
  351.4 3.5 fusion.6
  354.8 24.4 %all_to_all.10 = bf16[32,8,2048]{2,1,0:T(8,128)(2,1)S(1)} all-to-all(bf16[32,8,2048]{2,1,0:T(8,128)(2,1)S(1)} %fusion.6), channel_id=1, replica_groups=mesh['dp'=8,'expert_0'=4,'expert_1'=4,'expert_2'=2] {'expert_0','expert_..., dimensions={0} | all-to-all | bytes 2097152 | tf_op jit(solution)/shard_map/all_to_all | solution.py:87
  379.2 1.5 fusion.4
  (39 shorter events, 1.7 us)
Async XLA Ops:
  6.5 2.0 copy-start
  6.5 12.1 %copy-start.3 = (u32[256]{0:T(256)S(1)}, u32[256]{0:T(256)}, u32[]{:S(2)}) copy-start(u32[256]{0:T(256)} %constant.41) | copy-start | bytes 3076
  10.0 69.7 %all-to-all-start = ((bf16[32,8,2048]{2,1,0:T(8,128)(2,1)}), bf16[32,8,2048]{2,1,0:T(8,128)(2,1)S(1)}, u32[]{:S(2)}, u32[]{:S(2)}) async-start(bf16[32,8,2048]{2,1,0:T(8,128)(2,1)} %fusion.5), calls=%async_computation | async-start | bytes 2097152 | tf_op jit(solution)/shard_map/all_to_all | solution.py:45
  18.6 168.5 %all-reduce.3.cloned.1.call-start = ((), (), s32[]{:S(2)}) async-start(), calls=%async_computation.3 | async-start | bytes 8388608 | tf_op jit(solution)/shard_map/psum | solution.py:70
  83.1 212.6 %reduce-scatter.2.cloned.1.call-start = ((), (), s32[]{:S(2)}) async-start(), calls=%async_computation.4 | async-start | bytes 9437184 | tf_op jit(solution)/shard_map/reduce_scatter | solution.py:74
  187.1 8.1 %copy-start.2 = (bf16[1,1024,2048]{2,1,0:T(8,128)(2,1)S(1)}, bf16[1,1024,2048]{2,1,0:T(8,128)(2,1)}, u32[]{:S(2)}) copy-start(bf16[1,1024,2048]{2,1,0:T(8,128)(2,1)} %param.10) | copy-start | bytes 12582916
  201.8 93.9 %copy-start.1 = (f32[1,128]{1,0:T(1,128)S(1)}, f32[1,128]{1,0:T(1,128)}, u32[]{:S(2)}) copy-start(f32[1,128]{1,0:T(1,128)} %param.11) | copy-start | bytes 1540
  201.9 149.5 %all-gather.3.cloned.1.call-start = ((), (), s32[]{:S(2)}) async-start(), calls=%async_computation.5 | async-start | bytes 4718592 | tf_op jit(solution)/shard_map/all_gather | solution.py:83
Sparse Core Ops, SparseCore 0:
  83.2 103.8 all-reduce.2
  202.0 93.7 reduce-scatter.1
  298.0 53.2 all-gather.2
where the time goes:
time: 388 us; the launch traced here: 387 us
  waiting for transfers between devices  251 us (65%)
  blocking collectives  80.7 us (21%)
  matrix products  24.5 us (6%)
  between operations  14 us (4%)
  starting transfers between devices  8.7 us (2%)
  other arithmetic  5.45 us (1%)
    psum x1, waiting for transfers between devices, on_device(): lax.psum(local_rows, 'dp').astype(jnp.float32).astype(jnp.bfloat16)  104 us
    reduce_scatter x1, waiting for transfers between devices, on_device(): lax.psum_scatter(jnp.dot(hidden, second_weight, preferred_element_type=jn...  93.8 us
    all_gather x1, waiting for transfers between devices, on_device(): lax.all_gather(scaled, 'dp', axis=0, tiled=True)  53.4 us
    all_gather x3, blocking collectives, gather_in_order(): blocks = lax.all_gather(blocks, axes[k], axis=0, tiled=True)  41.1 us
    all_to_all x1, blocking collectives, on_device(): lax.all_to_all(sent_back, EXPERT, split_axis=0, concat_axis=0, tiled=True)  24.4 us
    unnamed x1, blocking collectives  15.2 us
    all_to_all x1, starting transfers between devices, on_device(): lax.all_to_all(packed.reshape(expert_count, MOST, width), EXPERT, split_a...  8.58 us
    dot_general x1, matrix products, on_device(): jnp.dot(slot_rows, first_weight, preferred_element_type=jnp.float32)  8.08 us
  transfers between devices with their start and end apart: 4, of which 3 were waited for; matrix products, arithmetic and copies ran while one was open for 1% of the time, Pallas kernels for 0%

commit v1 on v0

v1 whole, which is shorter than its diff:
```python
import jax
import jax.numpy as jnp
from jax import lax
from jax.sharding import Mesh
from jax.sharding import PartitionSpec as P

MOST = 8
EXPERT = ("expert_0", "expert_1", "expert_2")
DP_EXPERT = ("dp", "expert_0", "expert_1", "expert_2")


def exclusive(values):
    return jnp.cumsum(values) - values


def on_device(tokens, expert_ranks, capacity, weight_in, weight_out, gate_weights):
    dp_count = lax.axis_size("dp")
    expert_count = lax.axis_size(EXPERT)
    token_count, width = tokens.shape
    slots_dp = gate_weights.shape[1]
    rows_all = expert_count * MOST
    own_dp = lax.axis_index("dp")
    own_expert = lax.axis_index(EXPERT)

    chosen = expert_ranks < capacity[:, None]
    chosen_int = chosen.astype(jnp.int32)
    counts = jnp.sum(chosen_int, axis=1)
    before = jnp.cumsum(chosen_int, axis=1) - chosen_int
    places = lax.broadcasted_iota(jnp.int32, (expert_count, MOST, token_count), 1)
    pack_table = jnp.logical_and(chosen[:, None, :], before[:, None, :] == places)
    pack_table = pack_table.astype(jnp.bfloat16).reshape(rows_all, token_count)
    packed = jnp.dot(pack_table, tokens, preferred_element_type=jnp.float32).astype(jnp.bfloat16)
    arrived_rows = lax.all_to_all(
        packed.reshape(expert_count, MOST, width), EXPERT, split_axis=0, concat_axis=0, tiled=True
    ).reshape(rows_all, width)

    device_ids = lax.broadcasted_iota(jnp.int32, (expert_count, expert_count), 0)
    expert_ids = lax.broadcasted_iota(jnp.int32, (expert_count, expert_count), 1)
    table = lax.psum(jnp.where(device_ids == own_expert, counts[None, :], 0), EXPERT)
    plane_ids = lax.broadcasted_iota(jnp.int32, (dp_count, expert_count), 0)
    plane_counts = lax.psum(
        jnp.where(plane_ids == own_dp, jnp.sum(table, axis=0)[None, :], 0), "dp"
    )
    most_rows = jnp.max(plane_counts)
    arrived = jnp.sum(jnp.where(expert_ids == own_expert, table, 0), axis=1)
    earlier = jnp.logical_and(plane_ids < own_dp, expert_ids[:dp_count] == own_expert)
    first_slot = jnp.sum(jnp.where(earlier, plane_counts, 0))
    within = lax.broadcasted_iota(jnp.int32, (expert_count, MOST), 1)
    target = jnp.where(
        within < arrived[:, None], exclusive(arrived)[:, None] + within, -1
    ).reshape(rows_all)
    gates_all = lax.all_gather(gate_weights[0], "dp", axis=0, tiled=True)
    gates_all = jnp.concatenate([gates_all, jnp.zeros((rows_all,), gates_all.dtype)])

    def experts(rows, plane_rows):
        slot_ids = lax.broadcasted_iota(jnp.int32, (rows_all, plane_rows), 1)
        place_table = (target[:, None] == slot_ids).astype(jnp.bfloat16)
        plane = lax.dot_general(
            place_table, rows, (((0,), (0,)), ((), ())), preferred_element_type=jnp.float32
        ).astype(jnp.bfloat16)
        slot_rows = lax.all_gather(plane, "dp", axis=0, tiled=True)
        hidden = jnp.maximum(
            jnp.dot(slot_rows, weight_in[0], preferred_element_type=jnp.float32), 0.0
        ).astype(jnp.bfloat16)
        share = jnp.dot(hidden, weight_out[0], preferred_element_type=jnp.float32)
        out = lax.psum_scatter(
            share.astype(jnp.bfloat16), "dp", scatter_dimension=0, tiled=True
        ).astype(jnp.float32)
        gates = lax.dynamic_slice_in_dim(gates_all, first_slot, plane_rows, 0)
        scaled = (gates[:, None] * out).astype(jnp.bfloat16)
        returned = jnp.dot(place_table, scaled, preferred_element_type=jnp.float32)
        return returned.astype(jnp.bfloat16)

    fair = slots_dp + slots_dp // 4
    sent_back = lax.cond(
        most_rows <= fair,
        lambda rows: experts(rows, fair),
        lambda rows: experts(rows, rows_all),
        arrived_rows,
    )
    results = lax.all_to_all(
        sent_back.reshape(expert_count, MOST, width), EXPERT, split_axis=0, concat_axis=0, tiled=True
    ).reshape(rows_all, width)
    combined = lax.dot_general(
        pack_table, results, (((0,), (0,)), ((), ())), preferred_element_type=jnp.float32
    )
    return combined.astype(jnp.bfloat16)


def solution(mesh):
    split = Mesh(
        mesh.devices.reshape(mesh.shape["dp"], 4, 4, 2), ("dp", "expert_0", "expert_1", "expert_2")
    )
    placed = (
        P(DP_EXPERT, None),
        P(None, DP_EXPERT),
        P(),
        P(EXPERT, None, "dp"),
        P(EXPERT, "dp", None),
        P(EXPERT, "dp"),
    )
    return jax.shard_map(
        on_device, mesh=split, in_specs=placed, out_specs=P(DP_EXPERT, None), check_vma=False
    )
```

time: 388 us -> 360 us (0.928)
  waiting for transfers between devices: 251 us -> 132 us
  blocking collectives: 80.7 us -> 176 us
    psum x0 -> x2, blocking collectives: none -> 141 us  [the longest x1 127 us: on_device(): lax.psum(jnp.where(device_ids == own_expert, counts[None, :], 0), EXPERT)]
    psum x1 -> x0, waiting for transfers between devices: 104 us -> none  [on_device(): lax.psum(local_rows, 'dp').astype(jnp.float32).astype(jnp.bfloat16)]
    reduce_scatter x1, waiting for transfers between devices: 93.8 us -> 61.4 us  [experts(): lax.psum_scatter(share.astype(jnp.bfloat16), 'dp', scatter_dimension=0, t...]
    all_gather x3 -> x1, blocking collectives: 41.1 us -> 10.9 us  [on_device(): gates_all = lax.all_gather(gate_weights[0], 'dp', axis=0, tiled=True)]
    all_gather x1, waiting for transfers between devices: 53.4 us -> 70.5 us  [experts(): slot_rows = lax.all_gather(plane, 'dp', axis=0, tiled=True)]
    unnamed x1 -> x0, blocking collectives: 15.2 us -> none
    dot_general x5 -> x4, matrix products: 23 us -> 21.2 us  [the longest x1 16.9 us: experts(): share = jnp.dot(hidden, weight_out[0], preferred_element_type=jnp.float32)]
  transfers between devices with their start and end apart: 4 -> 3, of which waited for: 3 -> 2; matrix products, arithmetic and copies ran while one was open for 1% -> 1% of each run, Pallas kernels for 0% -> 0%
where the time goes in v1:
time: 360 us
  blocking collectives  176 us (49%)
  waiting for transfers between devices  132 us (37%)
  matrix products  22.7 us (6%)
  between operations  14.1 us (4%)
  starting transfers between devices  8.84 us (2%)
    psum x1, blocking collectives, on_device(): lax.psum(jnp.where(device_ids == own_expert, counts[None, :], 0), EXPERT)  127 us
    all_gather x1, waiting for transfers between devices, experts(): slot_rows = lax.all_gather(plane, 'dp', axis=0, tiled=True)  70.5 us
    reduce_scatter x1, waiting for transfers between devices, experts(): lax.psum_scatter(share.astype(jnp.bfloat16), 'dp', scatter_dimension=0, t...  61.4 us
    all_to_all x1, blocking collectives, on_device(): lax.all_to_all(sent_back.reshape(expert_count, MOST, width), EXPERT, spli...  24.3 us
    dot_general x1, matrix products, experts(): share = jnp.dot(hidden, weight_out[0], preferred_element_type=jnp.float32)  16.9 us
    psum x1, blocking collectives, on_device(): lax.psum(jnp.where(plane_ids == own_dp, jnp.sum(table, axis=0)[None, :],...  13.5 us
    all_gather x1, blocking collectives, on_device(): gates_all = lax.all_gather(gate_weights[0], 'dp', axis=0, tiled=True)  10.9 us
    all_to_all x1, starting transfers between devices, on_device(): lax.all_to_all(packed.reshape(expert_count, MOST, width), EXPERT, split_a...  8.58 us
  transfers between devices with their start and end apart: 3, of which 2 were waited for; matrix products, arithmetic and copies ran while one was open for 1% of the time, Pallas kernels for 0%

profile of v1, /device:TPU:1, one launch (start us, length us, event | category | flops | bytes accessed | tf_op | source)
XLA Modules:
  0.0 359.8 jit_solution(15286796204240877624)
XLA Ops:
  6.5 0.9 convert_bitcast_fusion.1
  7.5 0.6 reduce-window.11
  8.1 0.2 slice_reduce_fusion
  8.3 0.1 iota.68
  8.4 0.1 convert_subtract_fusion
  8.5 1.5 fusion.21
  10.0 8.6 %all-to-all-start = ((bf16[32,8,2048]{2,1,0:T(8,128)(2,1)}), bf16[32,8,2048]{2,1,0:T(8,128)(2,1)S(1)}, u32[]{:S(2)}, u32[]{:S(2)}) async-start(bf16[32,8,2048]{2,1,0:T(8,128)(2,1)} %fusion.21), calls=%async_computation.2 | async-start | bytes 2097152 | tf_op jit(solution)/shard_map/all_to_all | solution.py:33
  18.7 127.2 %psum.14 = s32[32,32]{1,0:T(8,128)S(1)} all-reduce(s32[32,32]{1,0:T(8,128)S(1)} %broadcast_select_fusion), channel_id=1, replica_groups=mesh['dp'=8,'expert_0'=4,'expert_1'=4,'expert_2'=2] {'expert_0','expert_..., use_global_device_ids=true, to_apply=%region_3.4 | all-reduce | flops 1024 | bytes 8192 | tf_op jit(solution)/shard_map/psum | solution.py:39
  145.9 0.1 select_reduce_fusion.2
  146.1 13.5 %psum.15 = s32[8,32]{1,0:T(8,128)S(1)} all-reduce(s32[8,32]{1,0:T(8,128)S(1)} %broadcast_select_fusion.1), channel_id=1, replica_groups=mesh['dp'=8,'expert_0'=4,'expert_1'=4,'expert_2'=2] {'dp'}, use_global_device_ids=true, to_apply=%region_5.6 | all-reduce | flops 256 | bytes 2048 | tf_op jit(solution)/shard_map/psum | solution.py:41
  159.6 0.7 reduce_max.9
  161.0 0.1 copy.25
  161.2 10.9 %all-gather = f32[1,1024]{1,0:T(1,128)S(1)} all-gather(f32[1,128]{1,0:T(1,128)S(1)} %copy-done.1), channel_id=2, replica_groups=mesh['dp'=8,'expert_0'=4,'expert_1'=4,'expert_2'=2] {'dp'}, dimensions={1}, use_global_device_ids=true | all-gather | bytes 4608 | tf_op jit(solution)/shard_map/all_gather | solution.py:52
  172.1 155.2 %conditional.2 = (bf16[256,2048]{1,0:T(8,128)(2,1)S(1)}) conditional(s32[]{:T(128)} %convert_element_type.51, (s32[32]{0:T(128)S(1)}, s32[32,8]{1,0:T(8,128)S(1)}, s32[32,1]{1,0:T(8,128)S(1)}, s32[32,8]{1,0:T(8,128)S(1)}, f32[1024]{0:T(1024)S(1)}, /*index=5*/s32[]{:T(128)}, s32[8]{0:T(128)S(1)}, pred[32]{0:T(512)(128)(4,1)S(1)}, ...), branch_computations={%region_9.12_spmd, %region_12.15_spmd} | conditional | flops 17727356928 | bytes 85999704
  172.3 0.1 eq.45
  172.4 1.3 convolution_convert_fusion.3
  173.7 0.2 reduce-scatter.5.cloned.1.call-start
  174.0 70.5 %all-gather.6.cloned.1.call-done = bf16[1280,2048]{1,0:T(8,128)(2,1)} async-done(((bf16[160,2048]{1,0:T(8,128)(2,1)}), bf16[1280,2048]{1,0:T(8,128)(2,1)}) %all-gather.6.cloned.1.call-update) | async-done | bytes 5242896 | tf_op jit(solution)/shard_map/cond/branch_1_fun/all_gather | solution.py:61
  244.4 16.9 %convolution_convert_fusion.2 = bf16[1280,2048]{1,0:T(8,128)(2,1)} fusion(bf16[1,1024,2048]{2,1,0:T(8,128)(2,1)} %get-tuple-element.129, bf16[1280,2048]{1,0:T(8,128)(2,1)} %all-gather.6.cloned.1.call-done, bf16[1,2048,1024]{2,1,0:T(8,128)(2,1)} %get-tuple-element.128), kind=kOutput, calls=%fused_computation.19 | convolution fusion | flops 10742661120 | bytes 18874368 | tf_op jit(solution)/shard_map/cond/branch_1_fun/dot_general | solution.py:65
  261.4 0.7 select_reduce_fusion.1
  264.1 61.4 %reduce-scatter.5.cloned.1.call-done = bf16[160,2048]{1,0:T(8,128)(2,1)} async-done(((bf16[1280,2048]{1,0:T(8,128)(2,1)}), bf16[160,2048]{1,0:T(8,128)(2,1)}) %reduce-scatter.5.cloned.1.call-update) | async-done | bytes 655376 | tf_op jit(solution)/shard_map/cond/branch_1_fun/reduce_scatter | solution.py:66
  325.4 1.6 fusion.15
  327.3 24.3 %all_to_all.10 = bf16[32,8,2048]{2,1,0:T(8,128)(2,1)S(1)} all-to-all(bf16[32,8,2048]{2,1,0:T(8,128)(2,1)S(1)} %bitcast.60), channel_id=1, replica_groups=mesh['dp'=8,'expert_0'=4,'expert_1'=4,'expert_2'=2] {'expert_0','expert_..., dimensions={0} | all-to-all | bytes 2097152 | tf_op jit(solution)/shard_map/all_to_all | solution.py:81
  351.5 1.5 fusion.20
  (25 shorter events, 0.6 us)
Async XLA Ops:
  6.5 2.0 copy-start
  6.5 154.6 %copy-start.1 = (f32[1,128]{1,0:T(1,128)S(1)}, f32[1,128]{1,0:T(1,128)}, u32[]{:S(2)}) copy-start(f32[1,128]{1,0:T(1,128)} %param.13) | copy-start | bytes 1540
  10.0 162.1 %all-to-all-start = ((bf16[32,8,2048]{2,1,0:T(8,128)(2,1)}), bf16[32,8,2048]{2,1,0:T(8,128)(2,1)S(1)}, u32[]{:S(2)}, u32[]{:S(2)}) async-start(bf16[32,8,2048]{2,1,0:T(8,128)(2,1)} %fusion.21), calls=%async_computation.2 | async-start | bytes 2097152 | tf_op jit(solution)/shard_map/all_to_all | solution.py:33
  172.1 72.3 %all-gather.6.cloned.1.call-start = ((), (), s32[]{:S(2)}) async-start(), calls=%async_computation.6 | async-start | bytes 5898240 | tf_op jit(solution)/shard_map/cond/branch_1_fun/all_gather | solution.py:61
  173.7 151.7 %reduce-scatter.5.cloned.1.call-start = ((), (), s32[]{:S(2)}) async-start(), calls=%async_computation.7 | async-start | bytes 5898240 | tf_op jit(solution)/shard_map/cond/branch_1_fun/reduce_scatter | solution.py:66
Sparse Core Ops, SparseCore 0:
  174.7 69.7 all-gather.5
  261.5 63.9 reduce-scatter.4

commit v2 on v1

--- a/solution.py
+++ b/solution.py
@@ -5,6 +5,7 @@
 from jax.sharding import PartitionSpec as P
 
 MOST = 8
+LANES = 128
 EXPERT = ("expert_0", "expert_1", "expert_2")
 DP_EXPERT = ("dp", "expert_0", "expert_1", "expert_2")
 
@@ -36,21 +37,30 @@
 
     device_ids = lax.broadcasted_iota(jnp.int32, (expert_count, expert_count), 0)
     expert_ids = lax.broadcasted_iota(jnp.int32, (expert_count, expert_count), 1)
-    table = lax.psum(jnp.where(device_ids == own_expert, counts[None, :], 0), EXPERT)
-    plane_ids = lax.broadcasted_iota(jnp.int32, (dp_count, expert_count), 0)
-    plane_counts = lax.psum(
-        jnp.where(plane_ids == own_dp, jnp.sum(table, axis=0)[None, :], 0), "dp"
+    table = jnp.where(device_ids == own_expert, counts[None, :], 0)
+    table = lax.psum(table.reshape(-1, LANES), EXPERT).reshape(expert_count, expert_count)
+    arrived = jnp.sum(jnp.where(expert_ids == own_expert, table, 0), axis=1)
+    plane_ids = lax.broadcasted_iota(jnp.int32, (dp_count, LANES), 0)
+    lane_ids = lax.broadcasted_iota(jnp.int32, (dp_count, LANES), 1)
+    plane_row = jnp.pad(jnp.sum(table, axis=0).astype(jnp.float32), (0, LANES - expert_count))
+    both = jnp.concatenate(
+        [
+            jnp.where(plane_ids == own_dp, plane_row[None, :], 0.0),
+            jnp.where(plane_ids == own_dp, gate_weights.reshape(-1, LANES), 0.0),
+        ]
     )
+    both = lax.psum(both, "dp")
+    plane_counts = both[:dp_count].astype(jnp.int32)
     most_rows = jnp.max(plane_counts)
-    arrived = jnp.sum(jnp.where(expert_ids == own_expert, table, 0), axis=1)
-    earlier = jnp.logical_and(plane_ids < own_dp, expert_ids[:dp_count] == own_expert)
+    earlier = jnp.logical_and(plane_ids < own_dp, lane_ids == own_expert)
     first_slot = jnp.sum(jnp.where(earlier, plane_counts, 0))
+    gates_all = jnp.concatenate(
+        [both[dp_count:].reshape(-1), jnp.zeros((rows_all,), jnp.float32)]
+    )
     within = lax.broadcasted_iota(jnp.int32, (expert_count, MOST), 1)
     target = jnp.where(
         within < arrived[:, None], exclusive(arrived)[:, None] + within, -1
     ).reshape(rows_all)
-    gates_all = lax.all_gather(gate_weights[0], "dp", axis=0, tiled=True)
-    gates_all = jnp.concatenate([gates_all, jnp.zeros((rows_all,), gates_all.dtype)])
 
     def experts(rows, plane_rows):
         slot_ids = lax.broadcasted_iota(jnp.int32, (rows_all, plane_rows), 1)

time: 360 us -> 349 us (0.969)
  blocking collectives: 176 us -> 168 us
    all_gather x1 -> x0, blocking collectives: 10.9 us -> none  [on_device(): gates_all = lax.all_gather(gate_weights[0], 'dp', axis=0, tiled=True)]
where the time goes in v2:
time: 349 us
  blocking collectives  168 us (48%)
  waiting for transfers between devices  129 us (37%)
  matrix products  22.7 us (7%)
  between operations  14.2 us (4%)
  starting transfers between devices  8.84 us (3%)
    psum x1, blocking collectives, on_device(): lax.psum(table.reshape(-1, LANES), EXPERT)  127 us
    all_gather x1, waiting for transfers between devices, experts(): slot_rows = lax.all_gather(plane, 'dp', axis=0, tiled=True)  67.1 us
    reduce_scatter x1, waiting for transfers between devices, experts(): lax.psum_scatter(share.astype(jnp.bfloat16), 'dp', scatter_dimension=0, t...  62.3 us
    all_to_all x1, blocking collectives, on_device(): lax.all_to_all(sent_back.reshape(expert_count, MOST, width), EXPERT, spli...  24.3 us
    dot_general x1, matrix products, experts(): share = jnp.dot(hidden, weight_out[0], preferred_element_type=jnp.float32)  16.9 us
    psum x1, blocking collectives, on_device(): both = lax.psum(both, 'dp')  16.5 us
    all_to_all x1, starting transfers between devices, on_device(): lax.all_to_all(packed.reshape(expert_count, MOST, width), EXPERT, split_a...  8.58 us
  transfers between devices with their start and end apart: 3, of which 2 were waited for; matrix products, arithmetic and copies ran while one was open for 1% of the time, Pallas kernels for 0%

profile of v2, /device:TPU:1, one launch (start us, length us, event | category | flops | bytes accessed | tf_op | source)
XLA Modules:
  0.0 348.8 jit_solution(17893966849262882347)
XLA Ops:
  6.5 0.9 convert_bitcast_fusion.1
  7.5 0.6 reduce-window.18
  8.1 0.2 slice_reduce_fusion
  8.3 0.1 iota.90
  8.4 0.1 convert_subtract_fusion
  8.5 1.5 fusion.19
  10.0 8.6 %all-to-all-start = ((bf16[32,8,2048]{2,1,0:T(8,128)(2,1)}), bf16[32,8,2048]{2,1,0:T(8,128)(2,1)S(1)}, u32[]{:S(2)}, u32[]{:S(2)}) async-start(bf16[32,8,2048]{2,1,0:T(8,128)(2,1)} %fusion.19), calls=%async_computation.2 | async-start | bytes 2097152 | tf_op jit(solution)/shard_map/all_to_all | solution.py:34
  18.7 0.1 iota.80
  18.9 127.0 %psum.14 = s32[32,32]{1,0:T(8,128)S(1)} all-reduce(s32[32,32]{1,0:T(8,128)S(1)} %reshape.73), channel_id=1, replica_groups=mesh['dp'=8,'expert_0'=4,'expert_1'=4,'expert_2'=2] {'expert_0','expert_..., use_global_device_ids=true, to_apply=%region_3.4 | all-reduce | flops 1024 | bytes 8192 | tf_op jit(solution)/shard_map/psum | solution.py:41
  145.9 0.1 select_reduce_fusion
  146.1 16.5 %psum.15 = f32[16,128]{1,0:T(8,128)S(1)} all-reduce(f32[16,128]{1,0:T(8,128)S(1)} %pad_maximum_fusion), channel_id=1, replica_groups=mesh['dp'=8,'expert_0'=4,'expert_1'=4,'expert_2'=2] {'dp'}, use_global_device_ids=true, to_apply=%region_5.6 | all-reduce | flops 2048 | bytes 16384 | tf_op jit(solution)/shard_map/psum | solution.py:52
  162.7 0.8 select_reduce_fusion.1
  164.2 0.1 copy.19
  164.3 0.1 reduce.1
  164.5 151.7 %conditional.2 = (bf16[256,2048]{1,0:T(8,128)(2,1)S(1)}) conditional(s32[]{:T(128)} %convert_element_type.61, (s32[32,8]{1,0:T(8,128)S(1)}, s32[]{:T(128)}, f32[1280]{0:T(1024)S(1)}, bf16[256,2048]{1,0:T(8,128)(2,1)S(1)}, bf16[1,2048,1024]{2,1,0:T(8,128)(2,1)}, /*index=5*/bf16[1,1024,2048]{2,1,0:T(8,128)(2,1)}) %tuple.30, (s32[32,8]{1,0:T(8,128)S(1)}, ...), branch_computations={%region_10.12_spmd, %region_12.14_spmd} | conditional | flops 17727356928 | bytes 85990520
  164.6 0.1 eq.49
  164.7 1.3 convolution_convert_fusion.3
  166.0 0.2 reduce-scatter.5.cloned.1.call-start
  166.2 67.1 %all-gather.5.cloned.1.call-done = bf16[1280,2048]{1,0:T(8,128)(2,1)} async-done(((bf16[160,2048]{1,0:T(8,128)(2,1)}), bf16[1280,2048]{1,0:T(8,128)(2,1)}) %all-gather.5.cloned.1.call-update) | async-done | bytes 5242896 | tf_op jit(solution)/shard_map/cond/branch_1_fun/all_gather | solution.py:71
  233.4 16.9 %convolution_convert_fusion.2 = bf16[1280,2048]{1,0:T(8,128)(2,1)} fusion(bf16[1,1024,2048]{2,1,0:T(8,128)(2,1)} %get-tuple-element.45, bf16[1280,2048]{1,0:T(8,128)(2,1)} %all-gather.5.cloned.1.call-done, bf16[1,2048,1024]{2,1,0:T(8,128)(2,1)} %get-tuple-element.44), kind=kOutput, calls=%fused_computation.13 | convolution fusion | flops 10742661120 | bytes 18874368 | tf_op jit(solution)/shard_map/cond/branch_1_fun/dot_general | solution.py:75
  252.0 62.3 %reduce-scatter.5.cloned.1.call-done = bf16[160,2048]{1,0:T(8,128)(2,1)} async-done(((bf16[1280,2048]{1,0:T(8,128)(2,1)}), bf16[160,2048]{1,0:T(8,128)(2,1)}) %reduce-scatter.5.cloned.1.call-update) | async-done | bytes 655376 | tf_op jit(solution)/shard_map/cond/branch_1_fun/reduce_scatter | solution.py:76
  314.4 1.6 fusion.13
  316.2 24.3 %all_to_all.10 = bf16[32,8,2048]{2,1,0:T(8,128)(2,1)S(1)} all-to-all(bf16[32,8,2048]{2,1,0:T(8,128)(2,1)S(1)} %bitcast.57), channel_id=1, replica_groups=mesh['dp'=8,'expert_0'=4,'expert_1'=4,'expert_2'=2] {'expert_0','expert_..., dimensions={0} | all-to-all | bytes 2097152 | tf_op jit(solution)/shard_map/all_to_all | solution.py:91
  340.5 1.5 fusion.18
  (32 shorter events, 0.7 us)
Async XLA Ops:
  6.5 2.0 copy-start
  6.5 139.5 %copy-start.1 = (f32[1,128]{1,0:T(1,128)S(1)}, f32[1,128]{1,0:T(1,128)}, u32[]{:S(2)}) copy-start(f32[1,128]{1,0:T(1,128)} %param.13) | copy-start | bytes 1540
  10.0 154.5 %all-to-all-start = ((bf16[32,8,2048]{2,1,0:T(8,128)(2,1)}), bf16[32,8,2048]{2,1,0:T(8,128)(2,1)S(1)}, u32[]{:S(2)}, u32[]{:S(2)}) async-start(bf16[32,8,2048]{2,1,0:T(8,128)(2,1)} %fusion.19), calls=%async_computation.2 | async-start | bytes 2097152 | tf_op jit(solution)/shard_map/all_to_all | solution.py:34
  164.5 68.8 %all-gather.5.cloned.1.call-start = ((), (), s32[]{:S(2)}) async-start(), calls=%async_computation.6 | async-start | bytes 5898240 | tf_op jit(solution)/shard_map/cond/branch_1_fun/all_gather | solution.py:71
  166.0 148.4 %reduce-scatter.5.cloned.1.call-start = ((), (), s32[]{:S(2)}) async-start(), calls=%async_computation.7 | async-start | bytes 5898240 | tf_op jit(solution)/shard_map/cond/branch_1_fun/reduce_scatter | solution.py:76
Sparse Core Ops, SparseCore 0:
  167.1 66.1 all-gather.4
  250.4 63.9 reduce-scatter.4

commit v3 on v1

v3 whole, which is shorter than its diff:
```python
import jax
import jax.numpy as jnp
from jax import lax
from jax.experimental import pallas as pl
from jax.experimental.pallas import tpu as pltpu
from jax.sharding import Mesh
from jax.sharding import PartitionSpec as P


MOST = 8
LANES = 128
NOTE = 8
HIDDEN_BLOCK = 256
VMEM_LIMIT = 20 * 1024 * 1024
EXPERT = ("expert_0", "expert_1", "expert_2")
DP_EXPERT = ("dp", "expert_0", "expert_1", "expert_2")


def narrow(rows):
    return rows.astype(jnp.bfloat16)


def wide(rows):
    return rows.astype(jnp.float32)


def expert_kernel(*refs):
    *refs, rows_ref, sums_ref = refs
    count = (len(refs) - 2) // 2
    pieces, (first_ref, second_ref), outs = refs[:count], refs[count : count + 2], refs[count + 2 :]
    half = outs[0].shape[0]
    step = pl.program_id(0)

    @pl.when(step == 0)
    def _():
        for i, piece in enumerate(pieces):
            rows_ref[i * half : (i + 1) * half] = piece[piece.shape[0] - half :]

    hidden = jnp.dot(rows_ref[...], first_ref[...], preferred_element_type=jnp.float32)
    hidden = jnp.maximum(hidden, 0.0).astype(jnp.bfloat16)
    sums = jnp.dot(hidden, second_ref[...], preferred_element_type=jnp.float32)

    @pl.when(step == 0)
    def _():
        sums_ref[...] = sums

    @pl.when(jnp.logical_and(step > 0, step < pl.num_programs(0) - 1))
    def _():
        sums_ref[...] += sums

    @pl.when(step == pl.num_programs(0) - 1)
    def _():
        for i, out in enumerate(outs):
            part = slice(i * half, (i + 1) * half)
            out[...] = (sums_ref[part] + sums[part]).astype(out.dtype)


def expert_rows(pieces, first_weight, second_weight, half, kinds):
    width, hidden = first_weight.shape
    count = len(pieces) * half
    return pl.pallas_call(
        expert_kernel,
        grid=(hidden // HIDDEN_BLOCK,),
        in_specs=[
            *[pl.BlockSpec(piece.shape, lambda i: (0, 0)) for piece in pieces],
            pl.BlockSpec((width, HIDDEN_BLOCK), lambda i: (0, i)),
            pl.BlockSpec((HIDDEN_BLOCK, width), lambda i: (i, 0)),
        ],
        out_specs=[pl.BlockSpec((half, width), lambda i: (0, 0)) for _ in pieces],
        out_shape=[pltpu.HBM((half, width), kind) for kind in kinds],
        scratch_shapes=[pltpu.VMEM((count, width), jnp.bfloat16), pltpu.VMEM((count, width), jnp.float32)],
        compiler_params=pltpu.CompilerParams(
            dimension_semantics=("arbitrary",), vmem_limit_bytes=VMEM_LIMIT
        ),
        cost_estimate=pl.CostEstimate(
            flops=4 * count * width * hidden,
            transcendentals=0,
            bytes_accessed=4 * width * hidden + 6 * count * width,
        ),
        name="expert_rows",
    )(*pieces, first_weight, second_weight)


def ring_experts(note, plane, first_weight, second_weight, dp_count):
    far = dp_count // 2
    half = plane.shape[0] // 2
    upward = [(i, (i + 1) % dp_count) for i in range(dp_count)]
    downward = [(i, (i - 1) % dp_count) for i in range(dp_count)]

    def hop(up_rows, down_rows):
        up_rows = lax.ppermute(up_rows, "dp", upward)
        down_rows = lax.ppermute(down_rows, "dp", downward)
        return up_rows, down_rows

    def mlp(*pieces, sent=()):
        kinds = [jnp.bfloat16 if i in sent else jnp.float32 for i in range(len(pieces))]
        return expert_rows(pieces, first_weight, second_weight, half, kinds)

    def after(rows, *others):
        return lax.optimization_barrier((rows, others))[0]

    top, bottom = jnp.concatenate([note, plane[:half]]), plane[half:]
    kept = 4 * LANES
    notes = {0: note[:1, :kept]}
    firsts = hop(top, bottom)
    seconds = hop(bottom, top)
    outs, done = {}, ()
    for k in range(1, far):
        firsts = after(firsts, *done)
        seconds = after(seconds, *firsts)
        notes[-k % dp_count], notes[k] = firsts[0][:1, :kept], seconds[1][:1, :kept]
        next_firsts = hop(*firsts)
        if k < far - 1:
            next_seconds = hop(*seconds)
        outs[k] = mlp(firsts[0], seconds[0], seconds[1], firsts[1], sent=(0, 3) if k == far - 1 else ())
        done = *outs[k], notes[-k % dp_count], notes[k]
        firsts, seconds = next_firsts, next_seconds

    below_top, below_bottom, above_top, above_bottom = outs[far - 1]
    seconds = hop(above_bottom, below_top)
    firsts = after(firsts, above_bottom, below_top, *done)
    notes[far] = firsts[0][:1, :kept]
    last = mlp(firsts[0], top, bottom, firsts[1], sent=(0, 3))
    sends = last[0], last[3]
    firsts = hop(*sends)
    for k in range(far - 1, 0, -1):
        if k > 1:
            below_top, _, _, above_bottom = outs[k - 1]
            seconds = after(seconds, *sends)
            sends = narrow(wide(seconds[0]) + above_bottom), narrow(wide(seconds[1]) + below_top)
            seconds = hop(*sends)
        _, below_bottom, above_top, _ = outs[k]
        firsts = after(firsts, *sends)
        sends = narrow(wide(firsts[0]) + above_top), narrow(wide(firsts[1]) + below_bottom)
        firsts = hop(*sends)
    sums = jnp.concatenate(
        [last[1] + wide(firsts[0]) + wide(seconds[1]), last[2] + wide(seconds[0]) + wide(firsts[1])]
    )
    return sums, after([notes[j] for j in range(dp_count)], *sends)


def on_device(tokens, expert_ranks, capacity, weight_in, weight_out, gate_weights):
    dp_count = lax.axis_size("dp")
    expert_count = lax.axis_size(EXPERT)
    token_count, width = tokens.shape
    slots_dp = gate_weights.shape[1]
    rows_all = expert_count * MOST
    round_rows = slots_dp + slots_dp // 4
    own_dp = lax.axis_index("dp")

    chosen = expert_ranks < capacity[:, None]
    chosen_int = chosen.astype(jnp.int32)
    before = jnp.cumsum(chosen_int, axis=1) - chosen_int
    places = lax.broadcasted_iota(jnp.int32, (expert_count, MOST, token_count), 1)
    pack_table = jnp.logical_and(chosen[:, None, :], before[:, None, :] == places)
    pack_table = pack_table.astype(jnp.bfloat16).reshape(rows_all, token_count)
    marked = jnp.concatenate([tokens, jnp.ones((token_count, LANES), jnp.bfloat16)], axis=1)
    packed = jnp.dot(pack_table, marked, preferred_element_type=jnp.float32).astype(jnp.bfloat16)
    arrived = lax.all_to_all(
        packed.reshape(expert_count, MOST, width + LANES), EXPERT, split_axis=0, concat_axis=0, tiled=True
    ).reshape(rows_all, width + LANES)
    arrived_rows, taken = arrived[:, :width], arrived[:, width:]

    earlier = lax.broadcasted_iota(jnp.int32, (rows_all, rows_all), 1) < lax.broadcasted_iota(
        jnp.int32, (rows_all, rows_all), 0
    )
    place = jnp.dot(earlier.astype(jnp.bfloat16), taken, preferred_element_type=jnp.float32)
    target = jnp.where(taken > 0, place, -1.0)
    plane_count = (place + wide(taken))[rows_all - 1 :]

    gate_high = lax.reduce_precision(gate_weights, 8, 7)
    gate_left = gate_weights - gate_high
    gate_middle = lax.reduce_precision(gate_left, 8, 7)
    gate_low = gate_left - gate_middle
    note = jnp.concatenate([gate_high, gate_middle, gate_low, plane_count], axis=1).astype(jnp.bfloat16)
    note = jnp.pad(note, ((0, NOTE - 1), (0, width - note.shape[1])))

    def experts(state):
        step, _, sent_back = state
        first = step * round_rows
        slot_ids = first + lax.broadcasted_iota(jnp.int32, (rows_all, round_rows), 1)
        place_table = (target[:, :1] == slot_ids.astype(jnp.float32)).astype(jnp.bfloat16)
        plane = lax.dot_general(
            place_table, arrived_rows, (((0,), (0,)), ((), ())), preferred_element_type=jnp.float32
        ).astype(jnp.bfloat16)
        sums, notes = ring_experts(note, plane, weight_in[0], weight_out[0], dp_count)
        table = jnp.concatenate(notes).astype(jnp.float32)
        table = lax.dynamic_slice_in_dim(
            jnp.concatenate([table, table]), (dp_count - own_dp) % dp_count, dp_count, 0
        )
        gates = table[:, :slots_dp] + table[:, slots_dp : 2 * slots_dp] + table[:, 2 * slots_dp : 3 * slots_dp]
        plane_counts = table[:, 3 * slots_dp].astype(jnp.int32)
        first_slot = jnp.sum(
            jnp.where(lax.broadcasted_iota(jnp.int32, (dp_count,), 0) < own_dp, plane_counts, 0)
        )
        gates = jnp.pad(gates.reshape(-1), (0, 2 * rows_all))
        gates = lax.dynamic_slice_in_dim(gates, first_slot + first, round_rows, 0)
        scaled = (gates[:, None] * sums).astype(jnp.bfloat16)
        returned = jnp.dot(place_table, scaled, preferred_element_type=jnp.float32)
        return step + 1, jnp.max(plane_counts), sent_back + returned.astype(jnp.bfloat16)

    _, _, sent_back = lax.while_loop(
        lambda state: state[0] * round_rows < state[1],
        experts,
        (jnp.int32(0), jnp.int32(1), jnp.zeros((rows_all, width), jnp.bfloat16)),
    )
    results = lax.all_to_all(
        sent_back.reshape(expert_count, MOST, width), EXPERT, split_axis=0, concat_axis=0, tiled=True
    ).reshape(rows_all, width)
    combined = lax.dot_general(
        pack_table, results, (((0,), (0,)), ((), ())), preferred_element_type=jnp.float32
    )
    return combined.astype(jnp.bfloat16)


def solution(mesh):
    split = Mesh(
        mesh.devices.reshape(mesh.shape["dp"], 4, 4, 2), ("dp", "expert_0", "expert_1", "expert_2")
    )
    placed = (
        P(DP_EXPERT, None),
        P(None, DP_EXPERT),
        P(),
        P(EXPERT, None, "dp"),
        P(EXPERT, "dp", None),
        P(EXPERT, "dp"),
    )
    return jax.shard_map(
        on_device, mesh=split, in_specs=placed, out_specs=P(DP_EXPERT, None), check_vma=False
    )
```

time: 360 us -> 185 us (0.51)
  blocking collectives: 176 us -> 28.7 us
  waiting for transfers between devices: 132 us -> 51.5 us
  Pallas kernels: 0 us -> 37.8 us
  starting transfers between devices: 8.84 us -> 44.8 us
  matrix products: 22.7 us -> 5.61 us
  between operations: 14.1 us -> 0.11 us
  other arithmetic: 3.51 us -> 12.5 us
    psum x2 -> x0, blocking collectives: 141 us -> none  [the longest x1 127 us: on_device(): lax.psum(jnp.where(device_ids == own_expert, counts[None, :], 0), EXPERT)]
    all_gather x1 -> x0, waiting for transfers between devices: 70.5 us -> none  [experts(): slot_rows = lax.all_gather(plane, 'dp', axis=0, tiled=True)]
    reduce_scatter x1 -> x0, waiting for transfers between devices: 61.4 us -> none  [experts(): lax.psum_scatter(share.astype(jnp.bfloat16), 'dp', scatter_dimension=0, t...]
    pallas_call x0 -> x4, Pallas kernels: none -> 37.8 us  [expert_rows(): pl.pallas_call(expert_kernel, grid=(hidden // HIDDEN_BLOCK,), in_specs=[*...]
    ppermute x0 -> x28, starting transfers between devices: none -> 36.1 us  [the longest x14 31.1 us: hop(): down_rows = lax.ppermute(down_rows, 'dp', downward)]
    ppermute x0 -> x28, waiting for transfers between devices: none -> 33.9 us  [the longest x14 20.9 us: hop(): up_rows = lax.ppermute(up_rows, 'dp', upward)]
    all_to_all x1, waiting for transfers between devices: 0.01 us -> 17.6 us  [on_device(): lax.all_to_all(packed.reshape(expert_count, MOST, width + LANES), EXPERT,...]
    dot_general x3, matrix products: 19.6 us -> 3.4 us  [the longest x1 2.77 us: on_device(): jnp.dot(pack_table, marked, preferred_element_type=jnp.float32)]
  transfers between devices with their start and end apart: 3 -> 29, of which waited for: 2 -> 13; matrix products, arithmetic and copies ran while one was open for 1% -> 5% of each run, Pallas kernels for 0% -> 20%
where the time goes in v3:
time: 185 us; the launch traced here: 184 us
  waiting for transfers between devices  51.5 us (28%)
  starting transfers between devices  44.8 us (24%)
  Pallas kernels  37.8 us (20%)
  blocking collectives  28.7 us (16%)
  other arithmetic  12.5 us (7%)
  matrix products  5.61 us (3%)
    pallas_call x4, Pallas kernels, expert_rows(): pl.pallas_call(expert_kernel, grid=(hidden // HIDDEN_BLOCK,), in_specs=[*...  37.8 us
    ppermute x14, starting transfers between devices, hop(): down_rows = lax.ppermute(down_rows, 'dp', downward)  31.1 us
    all_to_all x1, blocking collectives, on_device(): lax.all_to_all(sent_back.reshape(expert_count, MOST, width), EXPERT, spli...  28.7 us
    ppermute x14, waiting for transfers between devices, hop(): up_rows = lax.ppermute(up_rows, 'dp', upward)  20.9 us
    all_to_all x1, waiting for transfers between devices, on_device(): lax.all_to_all(packed.reshape(expert_count, MOST, width + LANES), EXPERT,...  17.6 us
    ppermute x14, waiting for transfers between devices, hop(): down_rows = lax.ppermute(down_rows, 'dp', downward)  13.1 us
    all_to_all x1, starting transfers between devices, on_device(): lax.all_to_all(packed.reshape(expert_count, MOST, width + LANES), EXPERT,...  8.71 us
    convert_element_type x10, other arithmetic, narrow(): return rows.astype(jnp.bfloat16)  7.17 us
  transfers between devices with their start and end apart: 29, of which 13 were waited for; matrix products, arithmetic and copies ran while one was open for 5% of the time, Pallas kernels for 20%

profile of v3, /device:TPU:1, one launch (start us, length us, event | category | flops | bytes accessed | tf_op | source)
XLA Modules:
  0.0 184.3 jit_solution(5900191017633845741)
XLA Ops:
  1.8 2.8 %fusion.15 = bf16[32,8,2176]{2,1,0:T(8,128)(2,1)} fusion(bf16[256,2048]{1,0:T(8,128)(2,1)} %param.8, s32[256]{0:T(256)S(1)} %iota.42, s32[32,256]{1,0:T(8,128)S(1)} %convert_subtract_fusion, pred[32,256]{1,0:T(8,128)(4,1)S(1)} %get-tuple-element.226), kind=kOutput, calls=%fused_computation.38 | convolution fusion | flops 285900800 | bytes 2204672 | tf_op jit(solution)/shard_map/dot_general | solution.py:158
  4.6 8.7 %all-to-all-start = ((bf16[32,8,2176]{2,1,0:T(8,128)(2,1)}), bf16[32,8,2176]{2,1,0:T(8,128)(2,1)S(1)}, u32[]{:S(2)}, u32[]{:S(2)}) async-start(bf16[32,8,2176]{2,1,0:T(8,128)(2,1)} %fusion.15), calls=%async_computation | async-start | bytes 2228224 | tf_op jit(solution)/shard_map/all_to_all | solution.py:159
  13.4 17.6 %all-to-all-done = bf16[32,8,2176]{2,1,0:T(8,128)(2,1)S(1)} async-done(((bf16[32,8,2176]{2,1,0:T(8,128)(2,1)}), bf16[32,8,2176]{2,1,0:T(8,128)(2,1)S(1)}, u32[]{:S(2)}, u32[]{:S(2)}) %all-to-all-start) | async-done | bytes 1114144 | tf_op jit(solution)/shard_map/all_to_all | solution.py:159
  31.6 122.5 %while.14 = (s32[]{:T(128)}, s32[]{:T(128)}, bf16[256,2048]{1,0:T(8,128)(2,1)S(1)}, bf16[8,2048]{1,0:T(8,128)(2,1)S(1)}, f32[256,128]{0,1:T(8,128)S(1)}, /*index...) while((s32[]{:T(128)}, s32[]{:T(128)}, ...), condition=%wide.region_5.6_spmd, body=%wide.region_2.5_spmd.sunk | while | flops 11082356736 | bytes 174625696 | solution.py:202
  34.5 4.0 %collective-permute-start.3 = (bf16[80,2048]{1,0:T(8,128)(2,1)S(1)}, bf16[80,2048]{1,0:T(8,128)(2,1)S(1)}, u32[]{:S(2)}, u32[]{:S(2)}) collective-permute-start(bf16[80,2048]{1,0:T(8,128)(2,1)S(1)} %get-tuple-element.346.refs_2_), channel_id=1, source_target_pairs={{0,224},{32,0},{64,32},{96,64},{128,96},{160,128},{192,160},{224,1... | collective-permute-start | bytes 983048 | tf_op jit(solution)/shard_map/while/body/ppermute | solution.py:92
  40.0 5.5 %collective-permute-done.3.refs_3_ = bf16[80,2048]{1,0:T(8,128)(2,1)S(1)} collective-permute-done((bf16[80,2048]{1,0:T(8,128)(2,1)S(1)}, bf16[80,2048]{1,0:T(8,128)(2,1)S(1)}, u32[]{:S(2)}, u32[]{:S(2)}) %collective-permute-start.3) | collective-permute-done | bytes 327712 | tf_op jit(solution)/shard_map/while/body/ppermute | solution.py:92
  47.1 2.7 %collective-permute-start.7 = (bf16[80,2048]{1,0:T(8,128)(2,1)S(1)}, bf16[80,2048]{1,0:T(8,128)(2,1)S(1)}, u32[]{:S(2)}, u32[]{:S(2)}) collective-permute-start(bf16[80,2048]{1,0:T(8,128)(2,1)S(1)} %collective-permute-done.3.refs_3_), channel_id=1, source_target_pairs={{0,224},{32,0},{64,32},{96,64},{128,96},{160,128},{192,160},{224,1... | collective-permute-start | bytes 983048 | tf_op jit(solution)/shard_map/while/body/ppermute | solution.py:92
  49.8 4.3 %collective-permute-done.refs_1_ = bf16[80,2048]{1,0:T(8,128)(2,1)S(1)} collective-permute-done((bf16[80,2048]{1,0:T(8,128)(2,1)S(1)}, bf16[80,2048]{1,0:T(8,128)(2,1)S(1)}, u32[]{:S(2)}, u32[]{:S(2)}) %collective-permute-start) | collective-permute-done | bytes 327712 | tf_op jit(solution)/shard_map/while/body/ppermute | solution.py:91
  54.2 2.5 %collective-permute-start.5 = (bf16[88,2048]{1,0:T(8,128)(2,1)S(1)}, bf16[88,2048]{1,0:T(8,128)(2,1)S(1)}, u32[]{:S(2)}, u32[]{:S(2)}) collective-permute-start(bf16[88,2048]{1,0:T(8,128)(2,1)S(1)} %collective-permute-done.1.refs_2_), channel_id=1, source_target_pairs={{0,224},{32,0},{64,32},{96,64},{128,96},{160,128},{192,160},{224,1... | collective-permute-start | bytes 1081352 | tf_op jit(solution)/shard_map/while/body/ppermute | solution.py:92
  56.7 10.4 %expert_rows.16 = (f32[80,2048]{1,0:T(8,128)}, f32[80,2048]{1,0:T(8,128)}, f32[80,2048]{1,0:T(8,128)}, f32[80,2048]{1,0:T(8,128)}) custom-call(bf16[88,2048]{1,0:T(8,128)(2,1)S(1)} %collective-permute-done.2.refs_0_, bf16[80,2048]{1,0:T(8,128)(2,1)S(1)} %collective-permute-done.refs_1_, bf16[88,2048]{1,0:T(8,128)(2,1)S(1)} %collective-permute-done.1.refs_2_, ...), custom_call_target="tpu_custom_call" | custom-call | flops 2684354560 | bytes 12320768 | tf_op jit(solution)/shard_map/while/body/expert_rows/pallas_call | solution.py:61
  67.2 2.7 %collective-permute-start.11 = (bf16[80,2048]{1,0:T(8,128)(2,1)S(1)}, bf16[80,2048]{1,0:T(8,128)(2,1)S(1)}, u32[]{:S(2)}, u32[]{:S(2)}) collective-permute-start(bf16[80,2048]{1,0:T(8,128)(2,1)S(1)} %collective-permute-done.7.refs_3_), channel_id=1, source_target_pairs={{0,224},{32,0},{64,32},{96,64},{128,96},{160,128},{192,160},{224,1... | collective-permute-start | bytes 983048 | tf_op jit(solution)/shard_map/while/body/ppermute | solution.py:92
  71.5 9.2 %expert_rows.17 = (f32[80,2048]{1,0:T(8,128)}, f32[80,2048]{1,0:T(8,128)}, f32[80,2048]{1,0:T(8,128)}, f32[80,2048]{1,0:T(8,128)}) custom-call(bf16[88,2048]{1,0:T(8,128)(2,1)S(1)} %collective-permute-done.6.refs_0_, bf16[80,2048]{1,0:T(8,128)(2,1)S(1)} %collective-permute-done.4.refs_1_, bf16[88,2048]{1,0:T(8,128)(2,1)S(1)} %collective-permute-done.5.refs_2_, ...), custom_call_target="tpu_custom_call" | custom-call | flops 2684354560 | bytes 12320768 | tf_op jit(solution)/shard_map/while/body/expert_rows/pallas_call | solution.py:61
  81.2 2.3 %collective-permute-start.13 = (bf16[80,2048]{1,0:T(8,128)(2,1)S(1)}, bf16[80,2048]{1,0:T(8,128)(2,1)S(1)}, u32[]{:S(2)}, u32[]{:S(2)}) collective-permute-start(bf16[80,2048]{1,0:T(8,128)(2,1)S(1)} %collective-permute-done.11.refs_3_), channel_id=1, source_target_pairs={{0,224},{32,0},{64,32},{96,64},{128,96},{160,128},{192,160},{224,1... | collective-permute-start | bytes 983048 | tf_op jit(solution)/shard_map/while/body/ppermute | solution.py:92
  83.6 9.0 %expert_rows.18 = (bf16[80,2048]{1,0:T(8,128)(2,1)}, f32[80,2048]{1,0:T(8,128)}, f32[80,2048]{1,0:T(8,128)}, bf16[80,2048]{1,0:T(8,128)(2,1)}) custom-call(bf16[88,2048]{1,0:T(8,128)(2,1)S(1)} %collective-permute-done.10.refs_0_, bf16[80,2048]{1,0:T(8,128)(2,1)S(1)} %collective-permute-done.8.refs_1_, bf16[88,2048]{1,0:T(8,128)(2,1)S(1)} %collective-permute-done.9.refs_2_, ...), custom_call_target="tpu_custom_call" | custom-call | flops 2684354560 | bytes 12320768 | tf_op jit(solution)/shard_map/while/body/expert_rows/pallas_call | solution.py:61
  95.4 9.1 %expert_rows.19 = (bf16[80,2048]{1,0:T(8,128)(2,1)}, f32[80,2048]{1,0:T(8,128)}, f32[80,2048]{1,0:T(8,128)}, bf16[80,2048]{1,0:T(8,128)(2,1)}) custom-call(bf16[88,2048]{1,0:T(8,128)(2,1)S(1)} %collective-permute-done.12.refs_0_, bf16[88,2048]{1,0:T(8,128)(2,1)S(1)} %pad_maximum_fusion.2.refs_1_, bf16[80,2048]{1,0:T(8,128)(2,1)S(1)} %get-tuple-element.346.refs_2_, ...), custom_call_target="tpu_custom_call" | custom-call | flops 2684354560 | bytes 12320768 | tf_op jit(solution)/shard_map/while/body/expert_rows/pallas_call | solution.py:61
  104.4 2.7 %collective-permute-start.15 = (bf16[80,2048]{1,0:T(8,128)(2,1)}, bf16[80,2048]{1,0:T(8,128)(2,1)S(1)}, u32[]{:S(2)}, u32[]{:S(2)}) collective-permute-start(bf16[80,2048]{1,0:T(8,128)(2,1)} %get-tuple-element.375), channel_id=1, source_target_pairs={{0,224},{32,0},{64,32},{96,64},{128,96},{160,128},{192,160},{224,1... | collective-permute-start | bytes 983048 | tf_op jit(solution)/shard_map/while/body/ppermute | solution.py:92
  108.9 2.9 %collective-permute-done.14 = bf16[80,2048]{1,0:T(8,128)(2,1)S(1)} collective-permute-done((bf16[80,2048]{1,0:T(8,128)(2,1)}, bf16[80,2048]{1,0:T(8,128)(2,1)S(1)}, u32[]{:S(2)}, u32[]{:S(2)}) %collective-permute-start.14) | collective-permute-done | bytes 327712 | tf_op jit(solution)/shard_map/while/body/ppermute | solution.py:91
  111.9 2.8 %collective-permute-start.19 = (bf16[80,2048]{1,0:T(8,128)(2,1)S(1)}, bf16[80,2048]{1,0:T(8,128)(2,1)S(1)}, u32[]{:S(2)}, u32[]{:S(2)}) collective-permute-start(bf16[80,2048]{1,0:T(8,128)(2,1)S(1)} %add_convert_fusion.26), channel_id=1, source_target_pairs={{0,224},{32,0},{64,32},{96,64},{128,96},{160,128},{192,160},{224,1... | collective-permute-start | bytes 983048 | tf_op jit(solution)/shard_map/while/body/ppermute | solution.py:92
  119.3 4.4 %collective-permute-done.19 = bf16[80,2048]{1,0:T(8,128)(2,1)S(1)} collective-permute-done((bf16[80,2048]{1,0:T(8,128)(2,1)S(1)}, bf16[80,2048]{1,0:T(8,128)(2,1)S(1)}, u32[]{:S(2)}, u32[]{:S(2)}) %collective-permute-start.19) | collective-permute-done | bytes 327712 | tf_op jit(solution)/shard_map/while/body/ppermute | solution.py:92
  128.8 2.7 %collective-permute-start.26 = (bf16[80,2048]{1,0:T(8,128)(2,1)}, bf16[80,2048]{1,0:T(8,128)(2,1)}, u32[]{:S(2)}, u32[]{:S(2)}) collective-permute-start(bf16[80,2048]{1,0:T(8,128)(2,1)} %add_convert_fusion.28), channel_id=1, source_target_pairs={{0,224},{32,0},{64,32},{96,64},{128,96},{160,128},{192,160},{224,1... | collective-permute-start | bytes 983048 | tf_op jit(solution)/shard_map/while/body/ppermute | solution.py:92
  132.7 3.5 %collective-permute-done.22 = bf16[80,2048]{1,0:T(8,128)(2,1)} collective-permute-done((bf16[80,2048]{1,0:T(8,128)(2,1)}, bf16[80,2048]{1,0:T(8,128)(2,1)}, u32[]{:S(2)}, u32[]{:S(2)}) %collective-permute-start.22) | collective-permute-done | bytes 327712 | tf_op jit(solution)/shard_map/while/body/ppermute | solution.py:91
  139.9 2.7 %collective-permute-start.24 = (bf16[80,2048]{1,0:T(8,128)(2,1)}, bf16[80,2048]{1,0:T(8,128)(2,1)}, u32[]{:S(2)}, u32[]{:S(2)}) collective-permute-start(bf16[80,2048]{1,0:T(8,128)(2,1)} %add_convert_fusion.32), channel_id=1, source_target_pairs={{0,224},{32,0},{64,32},{96,64},{128,96},{160,128},{192,160},{224,1... | collective-permute-start | bytes 983048 | tf_op jit(solution)/shard_map/while/body/ppermute | solution.py:92
  144.9 5.4 %collective-permute-done.27 = bf16[80,2048]{1,0:T(8,128)(2,1)} collective-permute-done((bf16[80,2048]{1,0:T(8,128)(2,1)}, bf16[80,2048]{1,0:T(8,128)(2,1)}, u32[]{:S(2)}, u32[]{:S(2)}) %collective-permute-start.27) | collective-permute-done | bytes 327712 | tf_op jit(solution)/shard_map/while/body/ppermute | solution.py:91
  154.1 28.7 %all_to_all.10 = bf16[32,8,2048]{2,1,0:T(8,128)(2,1)S(1)} all-to-all(bf16[32,8,2048]{2,1,0:T(8,128)(2,1)S(1)} %bitcast.45), channel_id=1, replica_groups=mesh['dp'=8,'expert_0'=4,'expert_1'=4,'expert_2'=2] {'expert_0','expert_..., dimensions={0} | all-to-all | bytes 2097152 | tf_op jit(solution)/shard_map/all_to_all | solution.py:207
  (123 shorter events, 36.0 us)
Async XLA Ops:
  4.6 26.4 %all-to-all-start = ((bf16[32,8,2176]{2,1,0:T(8,128)(2,1)}), bf16[32,8,2176]{2,1,0:T(8,128)(2,1)S(1)}, u32[]{:S(2)}, u32[]{:S(2)}) async-start(bf16[32,8,2176]{2,1,0:T(8,128)(2,1)} %fusion.15), calls=%async_computation | async-start | bytes 2228224 | tf_op jit(solution)/shard_map/all_to_all | solution.py:159
  32.8 14.3 %collective-permute-start.2 = (bf16[88,2048]{1,0:T(8,128)(2,1)S(1)}, bf16[88,2048]{1,0:T(8,128)(2,1)S(1)}, u32[]{:S(2)}, u32[]{:S(2)}) collective-permute-start(bf16[88,2048]{1,0:T(8,128)(2,1)S(1)} %pad_maximum_fusion.2.refs_1_), channel_id=1, source_target_pairs={{0,32},{32,64},{64,96},{96,128},{128,160},{160,192},{192,224},{224... | collective-permute-start | bytes 1081352 | tf_op jit(solution)/shard_map/while/body/ppermute | solution.py:91
  34.5 11.0 %collective-permute-start.3 = (bf16[80,2048]{1,0:T(8,128)(2,1)S(1)}, bf16[80,2048]{1,0:T(8,128)(2,1)S(1)}, u32[]{:S(2)}, u32[]{:S(2)}) collective-permute-start(bf16[80,2048]{1,0:T(8,128)(2,1)S(1)} %get-tuple-element.346.refs_2_), channel_id=1, source_target_pairs={{0,224},{32,0},{64,32},{96,64},{128,96},{160,128},{192,160},{224,1... | collective-permute-start | bytes 983048 | tf_op jit(solution)/shard_map/while/body/ppermute | solution.py:92
  38.5 15.6 %collective-permute-start.1 = (bf16[88,2048]{1,0:T(8,128)(2,1)S(1)}, bf16[88,2048]{1,0:T(8,128)(2,1)S(1)}, u32[]{:S(2)}, u32[]{:S(2)}) collective-permute-start(bf16[88,2048]{1,0:T(8,128)(2,1)S(1)} %pad_maximum_fusion.2.refs_1_), channel_id=1, source_target_pairs={{0,224},{32,0},{64,32},{96,64},{128,96},{160,128},{192,160},{224,1... | collective-permute-start | bytes 1081352 | tf_op jit(solution)/shard_map/while/body/ppermute | solution.py:92
  39.9 14.2 %collective-permute-start = (bf16[80,2048]{1,0:T(8,128)(2,1)S(1)}, bf16[80,2048]{1,0:T(8,128)(2,1)S(1)}, u32[]{:S(2)}, u32[]{:S(2)}) collective-permute-start(bf16[80,2048]{1,0:T(8,128)(2,1)S(1)} %get-tuple-element.346.refs_2_), channel_id=1, source_target_pairs={{0,32},{32,64},{64,96},{96,128},{128,160},{160,192},{192,224},{224... | collective-permute-start | bytes 983048 | tf_op jit(solution)/shard_map/while/body/ppermute | solution.py:91
  47.1 20.0 %collective-permute-start.6 = (bf16[88,2048]{1,0:T(8,128)(2,1)S(1)}, bf16[88,2048]{1,0:T(8,128)(2,1)S(1)}, u32[]{:S(2)}, u32[]{:S(2)}) collective-permute-start(bf16[88,2048]{1,0:T(8,128)(2,1)S(1)} %collective-permute-done.2.refs_0_), channel_id=1, source_target_pairs={{0,32},{32,64},{64,96},{96,128},{128,160},{160,192},{192,224},{224... | collective-permute-start | bytes 1081352 | tf_op jit(solution)/shard_map/while/body/ppermute | solution.py:91
  47.1 20.0 %collective-permute-start.7 = (bf16[80,2048]{1,0:T(8,128)(2,1)S(1)}, bf16[80,2048]{1,0:T(8,128)(2,1)S(1)}, u32[]{:S(2)}, u32[]{:S(2)}) collective-permute-start(bf16[80,2048]{1,0:T(8,128)(2,1)S(1)} %collective-permute-done.3.refs_3_), channel_id=1, source_target_pairs={{0,224},{32,0},{64,32},{96,64},{128,96},{160,128},{192,160},{224,1... | collective-permute-start | bytes 983048 | tf_op jit(solution)/shard_map/while/body/ppermute | solution.py:92
  54.2 15.8 %collective-permute-start.5 = (bf16[88,2048]{1,0:T(8,128)(2,1)S(1)}, bf16[88,2048]{1,0:T(8,128)(2,1)S(1)}, u32[]{:S(2)}, u32[]{:S(2)}) collective-permute-start(bf16[88,2048]{1,0:T(8,128)(2,1)S(1)} %collective-permute-done.1.refs_2_), channel_id=1, source_target_pairs={{0,224},{32,0},{64,32},{96,64},{128,96},{160,128},{192,160},{224,1... | collective-permute-start | bytes 1081352 | tf_op jit(solution)/shard_map/while/body/ppermute | solution.py:92
  56.6 13.3 %collective-permute-start.4 = (bf16[80,2048]{1,0:T(8,128)(2,1)S(1)}, bf16[80,2048]{1,0:T(8,128)(2,1)S(1)}, u32[]{:S(2)}, u32[]{:S(2)}) collective-permute-start(bf16[80,2048]{1,0:T(8,128)(2,1)S(1)} %collective-permute-done.refs_1_), channel_id=1, source_target_pairs={{0,32},{32,64},{64,96},{96,128},{128,160},{160,192},{192,224},{224... | collective-permute-start | bytes 983048 | tf_op jit(solution)/shard_map/while/body/ppermute | solution.py:91
  67.1 13.6 %collective-permute-start.10 = (bf16[88,2048]{1,0:T(8,128)(2,1)S(1)}, bf16[88,2048]{1,0:T(8,128)(2,1)S(1)}, u32[]{:S(2)}, u32[]{:S(2)}) collective-permute-start(bf16[88,2048]{1,0:T(8,128)(2,1)S(1)} %collective-permute-done.6.refs_0_), channel_id=1, source_target_pairs={{0,32},{32,64},{64,96},{96,128},{128,160},{160,192},{192,224},{224... | collective-permute-start | bytes 1081352 | tf_op jit(solution)/shard_map/while/body/ppermute | solution.py:91
  67.2 13.5 %collective-permute-start.11 = (bf16[80,2048]{1,0:T(8,128)(2,1)S(1)}, bf16[80,2048]{1,0:T(8,128)(2,1)S(1)}, u32[]{:S(2)}, u32[]{:S(2)}) collective-permute-start(bf16[80,2048]{1,0:T(8,128)(2,1)S(1)} %collective-permute-done.7.refs_3_), channel_id=1, source_target_pairs={{0,224},{32,0},{64,32},{96,64},{128,96},{160,128},{192,160},{224,1... | collective-permute-start | bytes 983048 | tf_op jit(solution)/shard_map/while/body/ppermute | solution.py:92
  70.0 13.6 %collective-permute-start.9 = (bf16[88,2048]{1,0:T(8,128)(2,1)S(1)}, bf16[88,2048]{1,0:T(8,128)(2,1)S(1)}, u32[]{:S(2)}, u32[]{:S(2)}) collective-permute-start(bf16[88,2048]{1,0:T(8,128)(2,1)S(1)} %collective-permute-done.5.refs_2_), channel_id=1, source_target_pairs={{0,224},{32,0},{64,32},{96,64},{128,96},{160,128},{192,160},{224,1... | collective-permute-start | bytes 1081352 | tf_op jit(solution)/shard_map/while/body/ppermute | solution.py:92
  71.4 12.2 %collective-permute-start.8 = (bf16[80,2048]{1,0:T(8,128)(2,1)S(1)}, bf16[80,2048]{1,0:T(8,128)(2,1)S(1)}, u32[]{:S(2)}, u32[]{:S(2)}) collective-permute-start(bf16[80,2048]{1,0:T(8,128)(2,1)S(1)} %collective-permute-done.4.refs_1_), channel_id=1, source_target_pairs={{0,32},{32,64},{64,96},{96,128},{128,160},{160,192},{192,224},{224... | collective-permute-start | bytes 983048 | tf_op jit(solution)/shard_map/while/body/ppermute | solution.py:91
  80.7 14.6 %collective-permute-start.12 = (bf16[88,2048]{1,0:T(8,128)(2,1)S(1)}, bf16[88,2048]{1,0:T(8,128)(2,1)S(1)}, u32[]{:S(2)}, u32[]{:S(2)}) collective-permute-start(bf16[88,2048]{1,0:T(8,128)(2,1)S(1)} %collective-permute-done.10.refs_0_), channel_id=1, source_target_pairs={{0,32},{32,64},{64,96},{96,128},{128,160},{160,192},{192,224},{224... | collective-permute-start | bytes 1081352 | tf_op jit(solution)/shard_map/while/body/ppermute | solution.py:91
  81.2 14.2 %collective-permute-start.13 = (bf16[80,2048]{1,0:T(8,128)(2,1)S(1)}, bf16[80,2048]{1,0:T(8,128)(2,1)S(1)}, u32[]{:S(2)}, u32[]{:S(2)}) collective-permute-start(bf16[80,2048]{1,0:T(8,128)(2,1)S(1)} %collective-permute-done.11.refs_3_), channel_id=1, source_target_pairs={{0,224},{32,0},{64,32},{96,64},{128,96},{160,128},{192,160},{224,1... | collective-permute-start | bytes 983048 | tf_op jit(solution)/shard_map/while/body/ppermute | solution.py:92
  92.6 14.5 %collective-permute-start.16 = (bf16[80,2048]{1,0:T(8,128)(2,1)}, bf16[80,2048]{1,0:T(8,128)(2,1)S(1)}, u32[]{:S(2)}, u32[]{:S(2)}) collective-permute-start(bf16[80,2048]{1,0:T(8,128)(2,1)} %get-tuple-element.368), channel_id=1, source_target_pairs={{0,32},{32,64},{64,96},{96,128},{128,160},{160,192},{192,224},{224... | collective-permute-start | bytes 983048 | tf_op jit(solution)/shard_map/while/body/ppermute | solution.py:91
  93.6 13.5 %collective-permute-start.17 = (bf16[80,2048]{1,0:T(8,128)(2,1)}, bf16[80,2048]{1,0:T(8,128)(2,1)S(1)}, u32[]{:S(2)}, u32[]{:S(2)}) collective-permute-start(bf16[80,2048]{1,0:T(8,128)(2,1)} %get-tuple-element.369), channel_id=1, source_target_pairs={{0,224},{32,0},{64,32},{96,64},{128,96},{160,128},{192,160},{224,1... | collective-permute-start | bytes 983048 | tf_op jit(solution)/shard_map/while/body/ppermute | solution.py:92
  107.4 10.3 %collective-permute-start.20 = (bf16[80,2048]{1,0:T(8,128)(2,1)S(1)}, bf16[80,2048]{1,0:T(8,128)(2,1)S(1)}, u32[]{:S(2)}, u32[]{:S(2)}) collective-permute-start(bf16[80,2048]{1,0:T(8,128)(2,1)S(1)} %add_convert_fusion.23), channel_id=1, source_target_pairs={{0,32},{32,64},{64,96},{96,128},{128,160},{160,192},{192,224},{224... | collective-permute-start | bytes 983048 | tf_op jit(solution)/shard_map/while/body/ppermute | solution.py:91
  111.9 11.9 %collective-permute-start.19 = (bf16[80,2048]{1,0:T(8,128)(2,1)S(1)}, bf16[80,2048]{1,0:T(8,128)(2,1)S(1)}, u32[]{:S(2)}, u32[]{:S(2)}) collective-permute-start(bf16[80,2048]{1,0:T(8,128)(2,1)S(1)} %add_convert_fusion.26), channel_id=1, source_target_pairs={{0,224},{32,0},{64,32},{96,64},{128,96},{160,128},{192,160},{224,1... | collective-permute-start | bytes 983048 | tf_op jit(solution)/shard_map/while/body/ppermute | solution.py:92
  114.7 11.0 %collective-permute-start.18 = (bf16[80,2048]{1,0:T(8,128)(2,1)S(1)}, bf16[80,2048]{1,0:T(8,128)(2,1)S(1)}, u32[]{:S(2)}, u32[]{:S(2)}) collective-permute-start(bf16[80,2048]{1,0:T(8,128)(2,1)S(1)} %add_convert_fusion.25), channel_id=1, source_target_pairs={{0,32},{32,64},{64,96},{96,128},{128,160},{160,192},{192,224},{224... | collective-permute-start | bytes 983048 | tf_op jit(solution)/shard_map/while/body/ppermute | solution.py:91
  128.8 16.1 %collective-permute-start.26 = (bf16[80,2048]{1,0:T(8,128)(2,1)}, bf16[80,2048]{1,0:T(8,128)(2,1)}, u32[]{:S(2)}, u32[]{:S(2)}) collective-permute-start(bf16[80,2048]{1,0:T(8,128)(2,1)} %add_convert_fusion.28), channel_id=1, source_target_pairs={{0,224},{32,0},{64,32},{96,64},{128,96},{160,128},{192,160},{224,1... | collective-permute-start | bytes 983048 | tf_op jit(solution)/shard_map/while/body/ppermute | solution.py:92
  131.5 19.9 %collective-permute-start.25 = (bf16[80,2048]{1,0:T(8,128)(2,1)}, bf16[80,2048]{1,0:T(8,128)(2,1)}, u32[]{:S(2)}, u32[]{:S(2)}) collective-permute-start(bf16[80,2048]{1,0:T(8,128)(2,1)} %add_convert_fusion.27), channel_id=1, source_target_pairs={{0,32},{32,64},{64,96},{96,128},{128,160},{160,192},{192,224},{224... | collective-permute-start | bytes 983048 | tf_op jit(solution)/shard_map/while/body/ppermute | solution.py:91
  139.9 10.3 %collective-permute-start.27 = (bf16[80,2048]{1,0:T(8,128)(2,1)}, bf16[80,2048]{1,0:T(8,128)(2,1)}, u32[]{:S(2)}, u32[]{:S(2)}) collective-permute-start(bf16[80,2048]{1,0:T(8,128)(2,1)} %add_convert_fusion.31), channel_id=1, source_target_pairs={{0,32},{32,64},{64,96},{96,128},{128,160},{160,192},{192,224},{224... | collective-permute-start | bytes 983048 | tf_op jit(solution)/shard_map/while/body/ppermute | solution.py:91
  139.9 11.5 %collective-permute-start.24 = (bf16[80,2048]{1,0:T(8,128)(2,1)}, bf16[80,2048]{1,0:T(8,128)(2,1)}, u32[]{:S(2)}, u32[]{:S(2)}) collective-permute-start(bf16[80,2048]{1,0:T(8,128)(2,1)} %add_convert_fusion.32), channel_id=1, source_target_pairs={{0,224},{32,0},{64,32},{96,64},{128,96},{160,128},{192,160},{224,1... | collective-permute-start | bytes 983048 | tf_op jit(solution)/shard_map/while/body/ppermute | solution.py:92
  (21 other events, 189.2 us)

commit v4 on v3

--- a/solution.py
+++ b/solution.py
@@ -10,7 +10,8 @@
 MOST = 8
 LANES = 128
 NOTE = 8
-HIDDEN_BLOCK = 256
+HIDDEN_BLOCK = 512
+OUT_BLOCK = 512
 VMEM_LIMIT = 20 * 1024 * 1024
 EXPERT = ("expert_0", "expert_1", "expert_2")
 DP_EXPERT = ("dp", "expert_0", "expert_1", "expert_2")
@@ -25,34 +26,28 @@
 
 
 def expert_kernel(*refs):
-    *refs, rows_ref, sums_ref = refs
+    *refs, rows_ref, hidden_ref = refs
     count = (len(refs) - 2) // 2
     pieces, (first_ref, second_ref), outs = refs[:count], refs[count : count + 2], refs[count + 2 :]
-    half = outs[0].shape[0]
-    step = pl.program_id(0)
-
-    @pl.when(step == 0)
-    def _():
-        for i, piece in enumerate(pieces):
-            rows_ref[i * half : (i + 1) * half] = piece[piece.shape[0] - half :]
-
-    hidden = jnp.dot(rows_ref[...], first_ref[...], preferred_element_type=jnp.float32)
-    hidden = jnp.maximum(hidden, 0.0).astype(jnp.bfloat16)
-    sums = jnp.dot(hidden, second_ref[...], preferred_element_type=jnp.float32)
-
-    @pl.when(step == 0)
-    def _():
-        sums_ref[...] = sums
-
-    @pl.when(jnp.logical_and(step > 0, step < pl.num_programs(0) - 1))
-    def _():
-        sums_ref[...] += sums
-
-    @pl.when(step == pl.num_programs(0) - 1)
-    def _():
-        for i, out in enumerate(outs):
-            part = slice(i * half, (i + 1) * half)
-            out[...] = (sums_ref[part] + sums[part]).astype(out.dtype)
+    half, width = outs[0].shape
+    for i, piece in enumerate(pieces):
+        rows_ref[i * half : (i + 1) * half] = piece[piece.shape[0] - half :]
+
+    def hidden_block(i, _):
+        block = pl.ds(pl.multiple_of(i * HIDDEN_BLOCK, HIDDEN_BLOCK), HIDDEN_BLOCK)
+        hidden = jnp.dot(rows_ref[...], first_ref[:, block], preferred_element_type=jnp.float32)
+        hidden_ref[:, block] = jnp.maximum(hidden, 0.0).astype(jnp.bfloat16)
+        return 0
+
+    def out_block(i, _):
+        block = pl.ds(pl.multiple_of(i * OUT_BLOCK, OUT_BLOCK), OUT_BLOCK)
+        sums = jnp.dot(hidden_ref[...], second_ref[:, block], preferred_element_type=jnp.float32)
+        for j, out in enumerate(outs):
+            out[:, block] = sums[j * half : (j + 1) * half].astype(out.dtype)
+        return 0
+
+    lax.fori_loop(0, hidden_ref.shape[1] // HIDDEN_BLOCK, hidden_block, 0)
+    lax.fori_loop(0, width // OUT_BLOCK, out_block, 0)
 
 
 def expert_rows(pieces, first_weight, second_weight, half, kinds):
@@ -60,18 +55,9 @@
     count = len(pieces) * half
     return pl.pallas_call(
         expert_kernel,
-        grid=(hidden // HIDDEN_BLOCK,),
-        in_specs=[
-            *[pl.BlockSpec(piece.shape, lambda i: (0, 0)) for piece in pieces],
-            pl.BlockSpec((width, HIDDEN_BLOCK), lambda i: (0, i)),
-            pl.BlockSpec((HIDDEN_BLOCK, width), lambda i: (i, 0)),
-        ],
-        out_specs=[pl.BlockSpec((half, width), lambda i: (0, 0)) for _ in pieces],
-        out_shape=[pltpu.HBM((half, width), kind) for kind in kinds],
-        scratch_shapes=[pltpu.VMEM((count, width), jnp.bfloat16), pltpu.VMEM((count, width), jnp.float32)],
-        compiler_params=pltpu.CompilerParams(
-            dimension_semantics=("arbitrary",), vmem_limit_bytes=VMEM_LIMIT
-        ),
+        out_shape=[jax.ShapeDtypeStruct((half, width), kind) for kind in kinds],
+        scratch_shapes=[pltpu.VMEM((count, width), jnp.bfloat16), pltpu.VMEM((count, hidden), jnp.bfloat16)],
+        compiler_params=pltpu.CompilerParams(vmem_limit_bytes=VMEM_LIMIT),
         cost_estimate=pl.CostEstimate(
             flops=4 * count * width * hidden,
             transcendentals=0,

time: 185 us -> 176 us (0.951)
  Pallas kernels: 37.8 us -> 18.9 us
  waiting for transfers between devices: 51.5 us -> 64.1 us
  blocking collectives: 28.7 us -> 24.8 us
  other arithmetic: 12.5 us -> 9.9 us
  matrix products: 5.61 us -> 7.68 us
    pallas_call x4, Pallas kernels: 37.8 us -> 18.9 us  [expert_rows(): pl.pallas_call(expert_kernel, out_shape=[jax.ShapeDtypeStruct((half, widt...]
    ppermute x14, waiting for transfers between devices: 20.9 us -> 27.6 us  [hop(): up_rows = lax.ppermute(up_rows, 'dp', upward)]
    ppermute x14, waiting for transfers between devices: 13.1 us -> 19 us  [hop(): down_rows = lax.ppermute(down_rows, 'dp', downward)]
    all_to_all x1, blocking collectives: 28.7 us -> 24.8 us  [on_device(): lax.all_to_all(sent_back.reshape(expert_count, MOST, width), EXPERT, spli...]
    ppermute x14, starting transfers between devices: 31.1 us -> 33.9 us  [hop(): down_rows = lax.ppermute(down_rows, 'dp', downward)]
    convert_element_type x10, other arithmetic: 7.17 us -> 4.73 us  [narrow(): return rows.astype(jnp.bfloat16)]
    dot_general x1, matrix products: 0.74 us -> 2.8 us  [experts(): returned = jnp.dot(place_table, scaled, preferred_element_type=jnp.float32)]
  transfers between devices with their start and end apart: 29 -> 29, of which waited for: 13 -> 15; matrix products, arithmetic and copies ran while one was open for 5% -> 4% of each run, Pallas kernels for 20% -> 11%
where the time goes in v4:
time: 176 us; the launch traced here: 175 us
  waiting for transfers between devices  64.1 us (36%)
  starting transfers between devices  45.9 us (26%)
  blocking collectives  24.8 us (14%)
  Pallas kernels  18.9 us (11%)
  other arithmetic  9.9 us (6%)
  matrix products  7.68 us (4%)
  local copies, waits for them, and re-layouts  2.36 us (1%)
    ppermute x14, starting transfers between devices, hop(): down_rows = lax.ppermute(down_rows, 'dp', downward)  33.9 us
    ppermute x14, waiting for transfers between devices, hop(): up_rows = lax.ppermute(up_rows, 'dp', upward)  27.6 us
    all_to_all x1, blocking collectives, on_device(): lax.all_to_all(sent_back.reshape(expert_count, MOST, width), EXPERT, spli...  24.8 us
    ppermute x14, waiting for transfers between devices, hop(): down_rows = lax.ppermute(down_rows, 'dp', downward)  19 us
    pallas_call x4, Pallas kernels, expert_rows(): pl.pallas_call(expert_kernel, out_shape=[jax.ShapeDtypeStruct((half, widt...  18.9 us
    all_to_all x1, waiting for transfers between devices, on_device(): lax.all_to_all(packed.reshape(expert_count, MOST, width + LANES), EXPERT,...  17.6 us
    all_to_all x1, starting transfers between devices, on_device(): lax.all_to_all(packed.reshape(expert_count, MOST, width + LANES), EXPERT,...  8.71 us
    convert_element_type x10, other arithmetic, narrow(): return rows.astype(jnp.bfloat16)  4.73 us
  transfers between devices with their start and end apart: 29, of which 15 were waited for; matrix products, arithmetic and copies ran while one was open for 4% of the time, Pallas kernels for 11%

profile of v4, /device:TPU:1, one launch (start us, length us, event | category | flops | bytes accessed | tf_op | source)
XLA Modules:
  0.0 175.3 jit_solution(9525048558273663270)
XLA Ops:
  1.8 2.8 %fusion.15 = bf16[32,8,2176]{2,1,0:T(8,128)(2,1)} fusion(bf16[256,2048]{1,0:T(8,128)(2,1)} %param.8, s32[256]{0:T(256)S(1)} %iota.42, s32[32,256]{1,0:T(8,128)S(1)} %convert_subtract_fusion, pred[32,256]{1,0:T(8,128)(4,1)S(1)} %get-tuple-element.226), kind=kOutput, calls=%fused_computation.38 | convolution fusion | flops 285900800 | bytes 2204672 | tf_op jit(solution)/shard_map/dot_general | solution.py:144
  4.6 8.7 %all-to-all-start = ((bf16[32,8,2176]{2,1,0:T(8,128)(2,1)}), bf16[32,8,2176]{2,1,0:T(8,128)(2,1)S(1)}, u32[]{:S(2)}, u32[]{:S(2)}) async-start(bf16[32,8,2176]{2,1,0:T(8,128)(2,1)} %fusion.15), calls=%async_computation | async-start | bytes 2228224 | tf_op jit(solution)/shard_map/all_to_all | solution.py:145
  13.4 17.6 %all-to-all-done = bf16[32,8,2176]{2,1,0:T(8,128)(2,1)S(1)} async-done(((bf16[32,8,2176]{2,1,0:T(8,128)(2,1)}), bf16[32,8,2176]{2,1,0:T(8,128)(2,1)S(1)}, u32[]{:S(2)}, u32[]{:S(2)}) %all-to-all-start) | async-done | bytes 1114144 | tf_op jit(solution)/shard_map/all_to_all | solution.py:145
  32.5 116.5 %while.14 = (s32[]{:T(128)}, s32[]{:T(128)}, bf16[256,2048]{1,0:T(8,128)(2,1)}, bf16[8,2048]{1,0:T(8,128)(2,1)S(1)}, f32[256,128]{0,1:T(8,128)S(1)}, /*index=5*/...) while((s32[]{:T(128)}, s32[]{:T(128)}, ...), condition=%wide.region_5.6_spmd, body=%wide.region_2.5_spmd.sunk | while | flops 11082356736 | bytes 153129600 | solution.py:188
  35.3 4.0 %collective-permute-start.3 = (bf16[80,2048]{1,0:T(8,128)(2,1)S(1)}, bf16[80,2048]{1,0:T(8,128)(2,1)S(1)}, u32[]{:S(2)}, u32[]{:S(2)}) collective-permute-start(bf16[80,2048]{1,0:T(8,128)(2,1)S(1)} %get-tuple-element.346.refs_2_), channel_id=1, source_target_pairs={{0,224},{32,0},{64,32},{96,64},{128,96},{160,128},{192,160},{224,1... | collective-permute-start | bytes 983048 | tf_op jit(solution)/shard_map/while/body/ppermute | solution.py:78
  40.8 5.5 %collective-permute-done.3.refs_3_ = bf16[80,2048]{1,0:T(8,128)(2,1)S(1)} collective-permute-done((bf16[80,2048]{1,0:T(8,128)(2,1)S(1)}, bf16[80,2048]{1,0:T(8,128)(2,1)S(1)}, u32[]{:S(2)}, u32[]{:S(2)}) %collective-permute-start.3) | collective-permute-done | bytes 327712 | tf_op jit(solution)/shard_map/while/body/ppermute | solution.py:78
  47.9 2.7 %collective-permute-start.7 = (bf16[80,2048]{1,0:T(8,128)(2,1)S(1)}, bf16[80,2048]{1,0:T(8,128)(2,1)S(1)}, u32[]{:S(2)}, u32[]{:S(2)}) collective-permute-start(bf16[80,2048]{1,0:T(8,128)(2,1)S(1)} %collective-permute-done.3.refs_3_), channel_id=1, source_target_pairs={{0,224},{32,0},{64,32},{96,64},{128,96},{160,128},{192,160},{224,1... | collective-permute-start | bytes 983048 | tf_op jit(solution)/shard_map/while/body/ppermute | solution.py:78
  50.6 4.3 %collective-permute-done.refs_1_ = bf16[80,2048]{1,0:T(8,128)(2,1)S(1)} collective-permute-done((bf16[80,2048]{1,0:T(8,128)(2,1)S(1)}, bf16[80,2048]{1,0:T(8,128)(2,1)S(1)}, u32[]{:S(2)}, u32[]{:S(2)}) %collective-permute-start) | collective-permute-done | bytes 327712 | tf_op jit(solution)/shard_map/while/body/ppermute | solution.py:77
  57.5 7.4 %expert_rows.16 = (f32[80,2048]{1,0:T(8,128)S(1)}, f32[80,2048]{1,0:T(8,128)S(1)}, f32[80,2048]{1,0:T(8,128)S(1)}, f32[80,2048]{1,0:T(8,128)S(1)}) custom-call(bf16[88,2048]{1,0:T(8,128)(2,1)S(1)} %collective-permute-done.2.refs_0_, bf16[80,2048]{1,0:T(8,128)(2,1)S(1)} %collective-permute-done.refs_1_, bf16[88,2048]{1,0:T(8,128)(2,1)S(1)} %collective-permute-done.1.refs_2_, ...), custom_call_target="tpu_custom_call" | custom-call | flops 2684354560 | bytes 12320768 | tf_op jit(solution)/shard_map/while/body/expert_rows/pallas_call | solution.py:56
  65.0 2.7 %collective-permute-start.11 = (bf16[80,2048]{1,0:T(8,128)(2,1)S(1)}, bf16[80,2048]{1,0:T(8,128)(2,1)S(1)}, u32[]{:S(2)}, u32[]{:S(2)}) collective-permute-start(bf16[80,2048]{1,0:T(8,128)(2,1)S(1)} %collective-permute-done.7.refs_3_), channel_id=1, source_target_pairs={{0,224},{32,0},{64,32},{96,64},{128,96},{160,128},{192,160},{224,1... | collective-permute-start | bytes 983048 | tf_op jit(solution)/shard_map/while/body/ppermute | solution.py:78
  69.3 2.8 %collective-permute-start.9 = (bf16[88,2048]{1,0:T(8,128)(2,1)S(1)}, bf16[88,2048]{1,0:T(8,128)(2,1)S(1)}, u32[]{:S(2)}, u32[]{:S(2)}) collective-permute-start(bf16[88,2048]{1,0:T(8,128)(2,1)S(1)} %collective-permute-done.5.refs_2_), channel_id=1, source_target_pairs={{0,224},{32,0},{64,32},{96,64},{128,96},{160,128},{192,160},{224,1... | collective-permute-start | bytes 1081352 | tf_op jit(solution)/shard_map/while/body/ppermute | solution.py:78
  72.2 3.8 %expert_rows.17 = (f32[80,2048]{1,0:T(8,128)S(1)}, f32[80,2048]{1,0:T(8,128)S(1)}, f32[80,2048]{1,0:T(8,128)S(1)}, f32[80,2048]{1,0:T(8,128)S(1)}) custom-call(bf16[88,2048]{1,0:T(8,128)(2,1)S(1)} %collective-permute-done.6.refs_0_, bf16[80,2048]{1,0:T(8,128)(2,1)S(1)} %collective-permute-done.4.refs_1_, ...), custom_call_target="tpu_custom_call" | custom-call | flops 2684354560 | bytes 12320768 | tf_op jit(solution)/shard_map/while/body/expert_rows/pallas_call | solution.py:56
  76.5 2.7 %collective-permute-start.13 = (bf16[80,2048]{1,0:T(8,128)(2,1)S(1)}, bf16[80,2048]{1,0:T(8,128)(2,1)S(1)}, u32[]{:S(2)}, u32[]{:S(2)}) collective-permute-start(bf16[80,2048]{1,0:T(8,128)(2,1)S(1)} %collective-permute-done.11.refs_3_), channel_id=1, source_target_pairs={{0,224},{32,0},{64,32},{96,64},{128,96},{160,128},{192,160},{224,1... | collective-permute-start | bytes 983048 | tf_op jit(solution)/shard_map/while/body/ppermute | solution.py:78
  79.2 4.3 %collective-permute-done.8.refs_1_ = bf16[80,2048]{1,0:T(8,128)(2,1)S(1)} collective-permute-done((bf16[80,2048]{1,0:T(8,128)(2,1)S(1)}, bf16[80,2048]{1,0:T(8,128)(2,1)S(1)}, u32[]{:S(2)}, u32[]{:S(2)}) %collective-permute-start.8) | collective-permute-done | bytes 327712 | tf_op jit(solution)/shard_map/while/body/ppermute | solution.py:77
  83.5 3.8 %expert_rows.18 = (bf16[80,2048]{1,0:T(8,128)(2,1)S(1)}, f32[80,2048]{1,0:T(8,128)S(1)}, f32[80,2048]{1,0:T(8,128)S(1)}, bf16[80,2048]{1,0:T(8,128)(2,1)S(1)}) custom-call(bf16[88,2048]{1,0:T(8,128)(2,1)S(1)} %collective-permute-done.10.refs_0_, bf16[80,2048]{1,0:T(8,128)(2,1)S(1)} %collective-permute-done.8.refs_1_, ...), custom_call_target="tpu_custom_call" | custom-call | flops 2684354560 | bytes 12320768 | tf_op jit(solution)/shard_map/while/body/expert_rows/pallas_call | solution.py:56
  91.2 3.8 %expert_rows.19 = (bf16[80,2048]{1,0:T(8,128)(2,1)S(1)}, f32[80,2048]{1,0:T(8,128)S(1)}, f32[80,2048]{1,0:T(8,128)S(1)}, bf16[80,2048]{1,0:T(8,128)(2,1)S(1)}) custom-call(bf16[88,2048]{1,0:T(8,128)(2,1)S(1)} %collective-permute-done.12.refs_0_, bf16[88,2048]{1,0:T(8,128)(2,1)S(1)} %pad_maximum_fusion.2.refs_1_, ...), custom_call_target="tpu_custom_call" | custom-call | flops 2684354560 | bytes 12320768 | tf_op jit(solution)/shard_map/while/body/expert_rows/pallas_call | solution.py:56
  99.6 4.1 %collective-permute-done.14 = bf16[80,2048]{1,0:T(8,128)(2,1)S(1)} collective-permute-done((bf16[80,2048]{1,0:T(8,128)(2,1)S(1)}, bf16[80,2048]{1,0:T(8,128)(2,1)S(1)}, u32[]{:S(2)}, u32[]{:S(2)}) %collective-permute-start.14) | collective-permute-done | bytes 327712 | tf_op jit(solution)/shard_map/while/body/ppermute | solution.py:77
  106.5 4.9 %collective-permute-done.21 = bf16[80,2048]{1,0:T(8,128)(2,1)S(1)} collective-permute-done((bf16[80,2048]{1,0:T(8,128)(2,1)S(1)}, bf16[80,2048]{1,0:T(8,128)(2,1)S(1)}, u32[]{:S(2)}, u32[]{:S(2)}) %collective-permute-start.21) | collective-permute-done | bytes 327712 | tf_op jit(solution)/shard_map/while/body/ppermute | solution.py:78
  112.3 6.2 %collective-permute-done.19 = bf16[80,2048]{1,0:T(8,128)(2,1)S(1)} collective-permute-done((bf16[80,2048]{1,0:T(8,128)(2,1)S(1)}, bf16[80,2048]{1,0:T(8,128)(2,1)S(1)}, u32[]{:S(2)}, u32[]{:S(2)}) %collective-permute-start.19) | collective-permute-done | bytes 327712 | tf_op jit(solution)/shard_map/while/body/ppermute | solution.py:78
  121.8 2.7 %collective-permute-start.26 = (bf16[80,2048]{1,0:T(8,128)(2,1)}, bf16[80,2048]{1,0:T(8,128)(2,1)}, u32[]{:S(2)}, u32[]{:S(2)}) collective-permute-start(bf16[80,2048]{1,0:T(8,128)(2,1)} %add_convert_fusion.28), channel_id=1, source_target_pairs={{0,224},{32,0},{64,32},{96,64},{128,96},{160,128},{192,160},{224,1... | collective-permute-start | bytes 983048 | tf_op jit(solution)/shard_map/while/body/ppermute | solution.py:78
  126.4 2.9 %collective-permute-done.22 = bf16[80,2048]{1,0:T(8,128)(2,1)} collective-permute-done((bf16[80,2048]{1,0:T(8,128)(2,1)}, bf16[80,2048]{1,0:T(8,128)(2,1)}, u32[]{:S(2)}, u32[]{:S(2)}) %collective-permute-start.22) | collective-permute-done | bytes 327712 | tf_op jit(solution)/shard_map/while/body/ppermute | solution.py:77
  136.4 7.0 %collective-permute-done.27 = bf16[80,2048]{1,0:T(8,128)(2,1)S(1)} collective-permute-done((bf16[80,2048]{1,0:T(8,128)(2,1)S(1)}, bf16[80,2048]{1,0:T(8,128)(2,1)S(1)}, u32[]{:S(2)}, u32[]{:S(2)}) %collective-permute-start.27) | collective-permute-done | bytes 327712 | tf_op jit(solution)/shard_map/while/body/ppermute | solution.py:77
  145.6 2.8 %fusion.65 = bf16[256,2048]{1,0:T(8,128)(2,1)} fusion(bf16[256,2048]{1,0:T(8,128)(2,1)} %get-tuple-element.414, f32[80,2048]{1,0:T(8,128)S(1)} %convert_add_fusion.4, f32[80,2048]{1,0:T(8,128)S(1)} %convert_add_fusion.5, f32[160]{0:T(256)S(1)} %pad_dynamic-slice_fusion.2, f32[160]{0:T(256)S(1)} %add_convert_fusion.22, f32[256]{0:T(256)S(1)} %bitcast.49), kind=kOutput, calls=%fused_computation.1.clone.1 | convolution fusion | flops 169844736 | bytes 3410176 | tf_op jit(solution)/shard_map/while/body/dot_general | solution.py:185
  149.1 24.8 %all_to_all.10 = bf16[32,8,2048]{2,1,0:T(8,128)(2,1)S(1)} all-to-all(bf16[32,8,2048]{2,1,0:T(8,128)(2,1)} %bitcast.8), channel_id=1, replica_groups=mesh['dp'=8,'expert_0'=4,'expert_1'=4,'expert_2'=2] {'expert_0','expert_..., dimensions={0} | all-to-all | bytes 2097152 | tf_op jit(solution)/shard_map/all_to_all | solution.py:193
  (101 shorter events, 41.0 us)
Async XLA Ops:
  4.6 26.4 %all-to-all-start = ((bf16[32,8,2176]{2,1,0:T(8,128)(2,1)}), bf16[32,8,2176]{2,1,0:T(8,128)(2,1)S(1)}, u32[]{:S(2)}, u32[]{:S(2)}) async-start(bf16[32,8,2176]{2,1,0:T(8,128)(2,1)} %fusion.15), calls=%async_computation | async-start | bytes 2228224 | tf_op jit(solution)/shard_map/all_to_all | solution.py:145
  33.6 14.3 %collective-permute-start.2 = (bf16[88,2048]{1,0:T(8,128)(2,1)S(1)}, bf16[88,2048]{1,0:T(8,128)(2,1)S(1)}, u32[]{:S(2)}, u32[]{:S(2)}) collective-permute-start(bf16[88,2048]{1,0:T(8,128)(2,1)S(1)} %pad_maximum_fusion.2.refs_1_), channel_id=1, source_target_pairs={{0,32},{32,64},{64,96},{96,128},{128,160},{160,192},{192,224},{224... | collective-permute-start | bytes 1081352 | tf_op jit(solution)/shard_map/while/body/ppermute | solution.py:77
  35.3 11.0 %collective-permute-start.3 = (bf16[80,2048]{1,0:T(8,128)(2,1)S(1)}, bf16[80,2048]{1,0:T(8,128)(2,1)S(1)}, u32[]{:S(2)}, u32[]{:S(2)}) collective-permute-start(bf16[80,2048]{1,0:T(8,128)(2,1)S(1)} %get-tuple-element.346.refs_2_), channel_id=1, source_target_pairs={{0,224},{32,0},{64,32},{96,64},{128,96},{160,128},{192,160},{224,1... | collective-permute-start | bytes 983048 | tf_op jit(solution)/shard_map/while/body/ppermute | solution.py:78
  39.3 15.6 %collective-permute-start.1 = (bf16[88,2048]{1,0:T(8,128)(2,1)S(1)}, bf16[88,2048]{1,0:T(8,128)(2,1)S(1)}, u32[]{:S(2)}, u32[]{:S(2)}) collective-permute-start(bf16[88,2048]{1,0:T(8,128)(2,1)S(1)} %pad_maximum_fusion.2.refs_1_), channel_id=1, source_target_pairs={{0,224},{32,0},{64,32},{96,64},{128,96},{160,128},{192,160},{224,1... | collective-permute-start | bytes 1081352 | tf_op jit(solution)/shard_map/while/body/ppermute | solution.py:78
  40.7 14.2 %collective-permute-start = (bf16[80,2048]{1,0:T(8,128)(2,1)S(1)}, bf16[80,2048]{1,0:T(8,128)(2,1)S(1)}, u32[]{:S(2)}, u32[]{:S(2)}) collective-permute-start(bf16[80,2048]{1,0:T(8,128)(2,1)S(1)} %get-tuple-element.346.refs_2_), channel_id=1, source_target_pairs={{0,32},{32,64},{64,96},{96,128},{128,160},{160,192},{192,224},{224... | collective-permute-start | bytes 983048 | tf_op jit(solution)/shard_map/while/body/ppermute | solution.py:77
  47.9 17.0 %collective-permute-start.6 = (bf16[88,2048]{1,0:T(8,128)(2,1)S(1)}, bf16[88,2048]{1,0:T(8,128)(2,1)S(1)}, u32[]{:S(2)}, u32[]{:S(2)}) collective-permute-start(bf16[88,2048]{1,0:T(8,128)(2,1)S(1)} %collective-permute-done.2.refs_0_), channel_id=1, source_target_pairs={{0,32},{32,64},{64,96},{96,128},{128,160},{160,192},{192,224},{224... | collective-permute-start | bytes 1081352 | tf_op jit(solution)/shard_map/while/body/ppermute | solution.py:77
  47.9 17.0 %collective-permute-start.7 = (bf16[80,2048]{1,0:T(8,128)(2,1)S(1)}, bf16[80,2048]{1,0:T(8,128)(2,1)S(1)}, u32[]{:S(2)}, u32[]{:S(2)}) collective-permute-start(bf16[80,2048]{1,0:T(8,128)(2,1)S(1)} %collective-permute-done.3.refs_3_), channel_id=1, source_target_pairs={{0,224},{32,0},{64,32},{96,64},{128,96},{160,128},{192,160},{224,1... | collective-permute-start | bytes 983048 | tf_op jit(solution)/shard_map/while/body/ppermute | solution.py:78
  54.9 14.4 %collective-permute-start.5 = (bf16[88,2048]{1,0:T(8,128)(2,1)S(1)}, bf16[88,2048]{1,0:T(8,128)(2,1)S(1)}, u32[]{:S(2)}, u32[]{:S(2)}) collective-permute-start(bf16[88,2048]{1,0:T(8,128)(2,1)S(1)} %collective-permute-done.1.refs_2_), channel_id=1, source_target_pairs={{0,224},{32,0},{64,32},{96,64},{128,96},{160,128},{192,160},{224,1... | collective-permute-start | bytes 1081352 | tf_op jit(solution)/shard_map/while/body/ppermute | solution.py:78
  57.4 11.9 %collective-permute-start.4 = (bf16[80,2048]{1,0:T(8,128)(2,1)S(1)}, bf16[80,2048]{1,0:T(8,128)(2,1)S(1)}, u32[]{:S(2)}, u32[]{:S(2)}) collective-permute-start(bf16[80,2048]{1,0:T(8,128)(2,1)S(1)} %collective-permute-done.refs_1_), channel_id=1, source_target_pairs={{0,32},{32,64},{64,96},{96,128},{128,160},{160,192},{192,224},{224... | collective-permute-start | bytes 983048 | tf_op jit(solution)/shard_map/while/body/ppermute | solution.py:77
  64.9 11.6 %collective-permute-start.10 = (bf16[88,2048]{1,0:T(8,128)(2,1)S(1)}, bf16[88,2048]{1,0:T(8,128)(2,1)S(1)}, u32[]{:S(2)}, u32[]{:S(2)}) collective-permute-start(bf16[88,2048]{1,0:T(8,128)(2,1)S(1)} %collective-permute-done.6.refs_0_), channel_id=1, source_target_pairs={{0,32},{32,64},{64,96},{96,128},{128,160},{160,192},{192,224},{224... | collective-permute-start | bytes 1081352 | tf_op jit(solution)/shard_map/while/body/ppermute | solution.py:77
  65.0 11.0 %collective-permute-start.11 = (bf16[80,2048]{1,0:T(8,128)(2,1)S(1)}, bf16[80,2048]{1,0:T(8,128)(2,1)S(1)}, u32[]{:S(2)}, u32[]{:S(2)}) collective-permute-start(bf16[80,2048]{1,0:T(8,128)(2,1)S(1)} %collective-permute-done.7.refs_3_), channel_id=1, source_target_pairs={{0,224},{32,0},{64,32},{96,64},{128,96},{160,128},{192,160},{224,1... | collective-permute-start | bytes 983048 | tf_op jit(solution)/shard_map/while/body/ppermute | solution.py:78
  69.3 14.2 %collective-permute-start.9 = (bf16[88,2048]{1,0:T(8,128)(2,1)S(1)}, bf16[88,2048]{1,0:T(8,128)(2,1)S(1)}, u32[]{:S(2)}, u32[]{:S(2)}) collective-permute-start(bf16[88,2048]{1,0:T(8,128)(2,1)S(1)} %collective-permute-done.5.refs_2_), channel_id=1, source_target_pairs={{0,224},{32,0},{64,32},{96,64},{128,96},{160,128},{192,160},{224,1... | collective-permute-start | bytes 1081352 | tf_op jit(solution)/shard_map/while/body/ppermute | solution.py:78
  72.2 11.4 %collective-permute-start.8 = (bf16[80,2048]{1,0:T(8,128)(2,1)S(1)}, bf16[80,2048]{1,0:T(8,128)(2,1)S(1)}, u32[]{:S(2)}, u32[]{:S(2)}) collective-permute-start(bf16[80,2048]{1,0:T(8,128)(2,1)S(1)} %collective-permute-done.4.refs_1_), channel_id=1, source_target_pairs={{0,32},{32,64},{64,96},{96,128},{128,160},{160,192},{192,224},{224... | collective-permute-start | bytes 983048 | tf_op jit(solution)/shard_map/while/body/ppermute | solution.py:77
  76.5 14.7 %collective-permute-start.12 = (bf16[88,2048]{1,0:T(8,128)(2,1)S(1)}, bf16[88,2048]{1,0:T(8,128)(2,1)S(1)}, u32[]{:S(2)}, u32[]{:S(2)}) collective-permute-start(bf16[88,2048]{1,0:T(8,128)(2,1)S(1)} %collective-permute-done.10.refs_0_), channel_id=1, source_target_pairs={{0,32},{32,64},{64,96},{96,128},{128,160},{160,192},{192,224},{224... | collective-permute-start | bytes 1081352 | tf_op jit(solution)/shard_map/while/body/ppermute | solution.py:77
  76.5 13.6 %collective-permute-start.13 = (bf16[80,2048]{1,0:T(8,128)(2,1)S(1)}, bf16[80,2048]{1,0:T(8,128)(2,1)S(1)}, u32[]{:S(2)}, u32[]{:S(2)}) collective-permute-start(bf16[80,2048]{1,0:T(8,128)(2,1)S(1)} %collective-permute-done.11.refs_3_), channel_id=1, source_target_pairs={{0,224},{32,0},{64,32},{96,64},{128,96},{160,128},{192,160},{224,1... | collective-permute-start | bytes 983048 | tf_op jit(solution)/shard_map/while/body/ppermute | solution.py:78
  87.3 10.5 %collective-permute-start.16 = (bf16[80,2048]{1,0:T(8,128)(2,1)S(1)}, bf16[80,2048]{1,0:T(8,128)(2,1)S(1)}, u32[]{:S(2)}, u32[]{:S(2)}) collective-permute-start(bf16[80,2048]{1,0:T(8,128)(2,1)S(1)} %get-tuple-element.368), channel_id=1, source_target_pairs={{0,32},{32,64},{64,96},{96,128},{128,160},{160,192},{192,224},{224... | collective-permute-start | bytes 983048 | tf_op jit(solution)/shard_map/while/body/ppermute | solution.py:77
  97.9 13.5 %collective-permute-start.21 = (bf16[80,2048]{1,0:T(8,128)(2,1)S(1)}, bf16[80,2048]{1,0:T(8,128)(2,1)S(1)}, u32[]{:S(2)}, u32[]{:S(2)}) collective-permute-start(bf16[80,2048]{1,0:T(8,128)(2,1)S(1)} %add_convert_fusion.24), channel_id=1, source_target_pairs={{0,224},{32,0},{64,32},{96,64},{128,96},{160,128},{192,160},{224,1... | collective-permute-start | bytes 983048 | tf_op jit(solution)/shard_map/while/body/ppermute | solution.py:78
  98.6 12.8 %collective-permute-start.20 = (bf16[80,2048]{1,0:T(8,128)(2,1)S(1)}, bf16[80,2048]{1,0:T(8,128)(2,1)S(1)}, u32[]{:S(2)}, u32[]{:S(2)}) collective-permute-start(bf16[80,2048]{1,0:T(8,128)(2,1)S(1)} %add_convert_fusion.23), channel_id=1, source_target_pairs={{0,32},{32,64},{64,96},{96,128},{128,160},{160,192},{192,224},{224... | collective-permute-start | bytes 983048 | tf_op jit(solution)/shard_map/while/body/ppermute | solution.py:77
  104.4 14.0 %collective-permute-start.19 = (bf16[80,2048]{1,0:T(8,128)(2,1)S(1)}, bf16[80,2048]{1,0:T(8,128)(2,1)S(1)}, u32[]{:S(2)}, u32[]{:S(2)}) collective-permute-start(bf16[80,2048]{1,0:T(8,128)(2,1)S(1)} %add_convert_fusion.26), channel_id=1, source_target_pairs={{0,224},{32,0},{64,32},{96,64},{128,96},{160,128},{192,160},{224,1... | collective-permute-start | bytes 983048 | tf_op jit(solution)/shard_map/while/body/ppermute | solution.py:78
  106.4 12.0 %collective-permute-start.18 = (bf16[80,2048]{1,0:T(8,128)(2,1)S(1)}, bf16[80,2048]{1,0:T(8,128)(2,1)S(1)}, u32[]{:S(2)}, u32[]{:S(2)}) collective-permute-start(bf16[80,2048]{1,0:T(8,128)(2,1)S(1)} %add_convert_fusion.25), channel_id=1, source_target_pairs={{0,32},{32,64},{64,96},{96,128},{128,160},{160,192},{192,224},{224... | collective-permute-start | bytes 983048 | tf_op jit(solution)/shard_map/while/body/ppermute | solution.py:77
  121.8 14.6 %collective-permute-start.26 = (bf16[80,2048]{1,0:T(8,128)(2,1)}, bf16[80,2048]{1,0:T(8,128)(2,1)}, u32[]{:S(2)}, u32[]{:S(2)}) collective-permute-start(bf16[80,2048]{1,0:T(8,128)(2,1)} %add_convert_fusion.28), channel_id=1, source_target_pairs={{0,224},{32,0},{64,32},{96,64},{128,96},{160,128},{192,160},{224,1... | collective-permute-start | bytes 983048 | tf_op jit(solution)/shard_map/while/body/ppermute | solution.py:78
  124.6 19.9 %collective-permute-start.25 = (bf16[80,2048]{1,0:T(8,128)(2,1)S(1)}, bf16[80,2048]{1,0:T(8,128)(2,1)}, u32[]{:S(2)}, u32[]{:S(2)}) collective-permute-start(bf16[80,2048]{1,0:T(8,128)(2,1)S(1)} %add_convert_fusion.27), channel_id=1, source_target_pairs={{0,32},{32,64},{64,96},{96,128},{128,160},{160,192},{192,224},{224... | collective-permute-start | bytes 983048 | tf_op jit(solution)/shard_map/while/body/ppermute | solution.py:77
  131.4 12.1 %collective-permute-start.27 = (bf16[80,2048]{1,0:T(8,128)(2,1)S(1)}, bf16[80,2048]{1,0:T(8,128)(2,1)S(1)}, u32[]{:S(2)}, u32[]{:S(2)}) collective-permute-start(bf16[80,2048]{1,0:T(8,128)(2,1)S(1)} %add_convert_fusion.31), channel_id=1, source_target_pairs={{0,32},{32,64},{64,96},{96,128},{128,160},{160,192},{192,224},{224... | collective-permute-start | bytes 983048 | tf_op jit(solution)/shard_map/while/body/ppermute | solution.py:77
  131.5 13.1 %collective-permute-start.24 = (bf16[80,2048]{1,0:T(8,128)(2,1)S(1)}, bf16[80,2048]{1,0:T(8,128)(2,1)S(1)}, u32[]{:S(2)}, u32[]{:S(2)}) collective-permute-start(bf16[80,2048]{1,0:T(8,128)(2,1)S(1)} %add_convert_fusion.32), channel_id=1, source_target_pairs={{0,224},{32,0},{64,32},{96,64},{128,96},{160,128},{192,160},{224,1... | collective-permute-start | bytes 983048 | tf_op jit(solution)/shard_map/while/body/ppermute | solution.py:78
  (10 other events, 84.9 us)

commit v5 on v4

--- a/solution.py
+++ b/solution.py
@@ -10,8 +10,7 @@
 MOST = 8
 LANES = 128
 NOTE = 8
-HIDDEN_BLOCK = 512
-OUT_BLOCK = 512
+BLOCK = 512
 VMEM_LIMIT = 20 * 1024 * 1024
 EXPERT = ("expert_0", "expert_1", "expert_2")
 DP_EXPERT = ("dp", "expert_0", "expert_1", "expert_2")
@@ -25,38 +24,91 @@
     return rows.astype(jnp.float32)
 
 
-def expert_kernel(*refs):
-    *refs, rows_ref, hidden_ref = refs
-    count = (len(refs) - 2) // 2
-    pieces, (first_ref, second_ref), outs = refs[:count], refs[count : count + 2], refs[count + 2 :]
-    half, width = outs[0].shape
+def gather_rows(pieces, rows_ref, half):
     for i, piece in enumerate(pieces):
         rows_ref[i * half : (i + 1) * half] = piece[piece.shape[0] - half :]
 
+
+def expert_sums(first_ref, second_ref, outs, rows_ref, hidden_ref, first_block, second_block):
+    half, width = outs[0].shape
+
     def hidden_block(i, _):
-        block = pl.ds(pl.multiple_of(i * HIDDEN_BLOCK, HIDDEN_BLOCK), HIDDEN_BLOCK)
+        block = first_block(i)
         hidden = jnp.dot(rows_ref[...], first_ref[:, block], preferred_element_type=jnp.float32)
         hidden_ref[:, block] = jnp.maximum(hidden, 0.0).astype(jnp.bfloat16)
         return 0
 
     def out_block(i, _):
-        block = pl.ds(pl.multiple_of(i * OUT_BLOCK, OUT_BLOCK), OUT_BLOCK)
+        block = second_block(i)
         sums = jnp.dot(hidden_ref[...], second_ref[:, block], preferred_element_type=jnp.float32)
         for j, out in enumerate(outs):
             out[:, block] = sums[j * half : (j + 1) * half].astype(out.dtype)
         return 0
 
-    lax.fori_loop(0, hidden_ref.shape[1] // HIDDEN_BLOCK, hidden_block, 0)
-    lax.fori_loop(0, width // OUT_BLOCK, out_block, 0)
-
-
-def expert_rows(pieces, first_weight, second_weight, half, kinds):
+    lax.fori_loop(0, hidden_ref.shape[1] // BLOCK, hidden_block, 0)
+    lax.fori_loop(0, width // BLOCK, out_block, 0)
+
+
+def columns(i):
+    return pl.ds(pl.multiple_of(i * BLOCK, BLOCK), BLOCK)
+
+
+def split_refs(refs):
+    count = (len(refs) - 2) // 2
+    return refs[:count], refs[count], refs[count + 1], refs[count + 2 :]
+
+
+def expert_kernel(*refs):
+    *refs, rows_ref, hidden_ref = refs
+    pieces, first_ref, second_ref, outs = split_refs(refs)
+    gather_rows(pieces, rows_ref, outs[0].shape[0])
+    expert_sums(first_ref, second_ref, outs, rows_ref, hidden_ref, columns, columns)
+
+
+def staged_expert_kernel(*refs):
+    *refs, rows_ref, hidden_ref, first_ref, second_ref, first_sems, second_sems = refs
+    pieces, first_far, second_far, outs = split_refs(refs)
+
+    def first_copy(i):
+        return pltpu.make_async_copy(first_far.at[:, columns(i)], first_ref.at[:, columns(i)], first_sems.at[i])
+
+    def second_copy(i):
+        return pltpu.make_async_copy(second_far.at[:, columns(i)], second_ref.at[:, columns(i)], second_sems.at[i])
+
+    def first_block(i):
+        first_copy(i).wait()
+        return columns(i)
+
+    def second_block(i):
+        second_copy(i).wait()
+        return columns(i)
+
+    for i in range(first_ref.shape[1] // BLOCK):
+        first_copy(i).start()
+    for i in range(second_ref.shape[1] // BLOCK):
+        second_copy(i).start()
+    gather_rows(pieces, rows_ref, outs[0].shape[0])
+    expert_sums(first_ref, second_ref, outs, rows_ref, hidden_ref, first_block, second_block)
+
+
+def expert_rows(pieces, first_weight, second_weight, half, kinds, staged):
     width, hidden = first_weight.shape
     count = len(pieces) * half
+    scratch = [pltpu.VMEM((count, width), jnp.bfloat16), pltpu.VMEM((count, hidden), jnp.bfloat16)]
+    specs = {}
+    if staged:
+        scratch += [
+            pltpu.VMEM(first_weight.shape, jnp.bfloat16),
+            pltpu.VMEM(second_weight.shape, jnp.bfloat16),
+            pltpu.SemaphoreType.DMA((hidden // BLOCK,)),
+            pltpu.SemaphoreType.DMA((width // BLOCK,)),
+        ]
+        near, far = pl.BlockSpec(memory_space=pltpu.VMEM), pl.BlockSpec(memory_space=pl.ANY)
+        specs = {"in_specs": [near] * len(pieces) + [far] * 2}
     return pl.pallas_call(
-        expert_kernel,
+        staged_expert_kernel if staged else expert_kernel,
         out_shape=[jax.ShapeDtypeStruct((half, width), kind) for kind in kinds],
-        scratch_shapes=[pltpu.VMEM((count, width), jnp.bfloat16), pltpu.VMEM((count, hidden), jnp.bfloat16)],
+        scratch_shapes=scratch,
         compiler_params=pltpu.CompilerParams(vmem_limit_bytes=VMEM_LIMIT),
         cost_estimate=pl.CostEstimate(
             flops=4 * count * width * hidden,
@@ -64,7 +116,74 @@
             bytes_accessed=4 * width * hidden + 6 * count * width,
         ),
         name="expert_rows",
+        **specs,
     )(*pieces, first_weight, second_weight)
+
+
+def pack_kernel(tokens_ref, ranks_ref, capacity_ref, packed_ref, table_ref, blank_ref):
+    experts, count = ranks_ref.shape
+    width = tokens_ref.shape[1]
+    chosen = ranks_ref[...] < capacity_ref[...]
+    earlier = lax.broadcasted_iota(jnp.int32, (count, count), 0) < lax.broadcasted_iota(
+        jnp.int32, (count, count), 1
+    )
+    before = jnp.dot(
+        jnp.where(chosen, 1.0, 0.0).astype(jnp.bfloat16),
+        jnp.where(earlier, 1.0, 0.0).astype(jnp.bfloat16),
+        preferred_element_type=jnp.float32,
+    )
+    place = jnp.where(chosen, before, -1.0)
+    row = lax.broadcasted_iota(jnp.int32, (MOST, count), 0).astype(jnp.float32)
+    for e in range(experts):
+        table_ref[e * MOST : (e + 1) * MOST] = jnp.where(place[e : e + 1] == row, 1.0, 0.0).astype(jnp.bfloat16)
+    table = table_ref[...]
+    packed = jnp.dot(table, tokens_ref[...], preferred_element_type=jnp.float32)
+    packed_ref[:, :width] = packed.astype(jnp.bfloat16)
+    blank_ref[...] = jnp.zeros(blank_ref.shape, blank_ref.dtype)
+    ones = jnp.ones((count, LANES), jnp.bfloat16)
+    packed_ref[:, width:] = jnp.dot(table, ones, preferred_element_type=jnp.float32).astype(jnp.bfloat16)
+
+
+def pack(tokens, expert_ranks, capacity):
+    count, width = tokens.shape
+    rows_all = expert_ranks.shape[0] * MOST
+    return pl.pallas_call(
+        pack_kernel,
+        out_shape=[
+            jax.ShapeDtypeStruct((rows_all, width + LANES), jnp.bfloat16),
+            pltpu.HBM((rows_all, count), jnp.bfloat16),
+            pltpu.HBM((rows_all, width), jnp.bfloat16),
+        ],
+        compiler_params=pltpu.CompilerParams(vmem_limit_bytes=VMEM_LIMIT),
+        name="pack",
+    )(tokens, expert_ranks, capacity[:, None])
+
+
+def finish_kernel(*refs):
+    *parts, gates_ref, target_ref, kept_ref, out_ref, scaled_ref = refs
+    half = parts[0].shape[0]
+    for i, (own, one, other) in enumerate((parts[:3], parts[3:])):
+        rows = slice(i * half, (i + 1) * half)
+        sums = own[...] + wide(one[...]) + wide(other[...])
+        scaled_ref[rows] = narrow(gates_ref[rows] * sums)
+    target = target_ref[:, :1]
+    count = 2 * half
+    slots = lax.broadcasted_iota(jnp.int32, (target.shape[0], count), 1).astype(jnp.float32)
+    table = jnp.where(target == slots, 1.0, 0.0).astype(jnp.bfloat16)
+    returned = jnp.dot(table, scaled_ref[...], preferred_element_type=jnp.float32)
+    here = jnp.logical_and(target >= 0.0, target < count)
+    out_ref[...] = narrow(jnp.where(here, returned, wide(kept_ref[...])))
+
+
+def finish(parts, gates, target, kept):
+    half, width = parts[0].shape
+    return pl.pallas_call(
+        finish_kernel,
+        out_shape=jax.ShapeDtypeStruct(kept.shape, kept.dtype),
+        scratch_shapes=[pltpu.VMEM((2 * half, width), jnp.bfloat16)],
+        compiler_params=pltpu.CompilerParams(vmem_limit_bytes=VMEM_LIMIT),
+        name="finish",
+    )(*parts, gates, target, kept)
 
 
 def ring_experts(note, plane, first_weight, second_weight, dp_count):
@@ -78,9 +197,9 @@
         down_rows = lax.ppermute(down_rows, "dp", downward)
         return up_rows, down_rows
 
-    def mlp(*pieces, sent=()):
+    def mlp(*pieces, sent=(), staged=False):
         kinds = [jnp.bfloat16 if i in sent else jnp.float32 for i in range(len(pieces))]
-        return expert_rows(pieces, first_weight, second_weight, half, kinds)
+        return expert_rows(pieces, first_weight, second_weight, half, kinds, staged)
 
     def after(rows, *others):
         return lax.optimization_barrier((rows, others))[0]
@@ -98,7 +217,7 @@
         next_firsts = hop(*firsts)
         if k < far - 1:
             next_seconds = hop(*seconds)
-        outs[k] = mlp(firsts[0], seconds[0], seconds[1], firsts[1], sent=(0, 3) if k == far - 1 else ())
+        outs[k] = mlp(firsts[0], seconds[0], seconds[1], firsts[1], sent=(0, 3) if k == far - 1 else (), staged=k == 1)
         done = *outs[k], notes[-k % dp_count], notes[k]
         firsts, seconds = next_firsts, next_seconds
 
@@ -119,33 +238,24 @@
         firsts = after(firsts, *sends)
         sends = narrow(wide(firsts[0]) + above_top), narrow(wide(firsts[1]) + below_bottom)
         firsts = hop(*sends)
-    sums = jnp.concatenate(
-        [last[1] + wide(firsts[0]) + wide(seconds[1]), last[2] + wide(seconds[0]) + wide(firsts[1])]
-    )
-    return sums, after([notes[j] for j in range(dp_count)], *sends)
+    parts = last[1], firsts[0], seconds[1], last[2], seconds[0], firsts[1]
+    return parts, after([notes[j] for j in range(dp_count)], *sends)
 
 
 def on_device(tokens, expert_ranks, capacity, weight_in, weight_out, gate_weights):
     dp_count = lax.axis_size("dp")
     expert_count = lax.axis_size(EXPERT)
-    token_count, width = tokens.shape
+    width = tokens.shape[1]
     slots_dp = gate_weights.shape[1]
     rows_all = expert_count * MOST
     round_rows = slots_dp + slots_dp // 4
     own_dp = lax.axis_index("dp")
 
-    chosen = expert_ranks < capacity[:, None]
-    chosen_int = chosen.astype(jnp.int32)
-    before = jnp.cumsum(chosen_int, axis=1) - chosen_int
-    places = lax.broadcasted_iota(jnp.int32, (expert_count, MOST, token_count), 1)
-    pack_table = jnp.logical_and(chosen[:, None, :], before[:, None, :] == places)
-    pack_table = pack_table.astype(jnp.bfloat16).reshape(rows_all, token_count)
-    marked = jnp.concatenate([tokens, jnp.ones((token_count, LANES), jnp.bfloat16)], axis=1)
-    packed = jnp.dot(pack_table, marked, preferred_element_type=jnp.float32).astype(jnp.bfloat16)
+    packed, pack_table, blank = pack(tokens, expert_ranks, capacity)
     arrived = lax.all_to_all(
         packed.reshape(expert_count, MOST, width + LANES), EXPERT, split_axis=0, concat_axis=0, tiled=True
     ).reshape(rows_all, width + LANES)
-    arrived_rows, taken = arrived[:, :width], arrived[:, width:]
+    taken = arrived[:, width:]
 
     earlier = lax.broadcasted_iota(jnp.int32, (rows_all, rows_all), 1) < lax.broadcasted_iota(
         jnp.int32, (rows_all, rows_all), 0
@@ -164,12 +274,13 @@
     def experts(state):
         step, _, sent_back = state
         first = step * round_rows
-        slot_ids = first + lax.broadcasted_iota(jnp.int32, (rows_all, round_rows), 1)
-        place_table = (target[:, :1] == slot_ids.astype(jnp.float32)).astype(jnp.bfloat16)
+        here = target - first.astype(jnp.float32)
+        slot_ids = lax.broadcasted_iota(jnp.int32, (rows_all, round_rows), 1)
+        place_table = (here[:, :1] == slot_ids.astype(jnp.float32)).astype(jnp.bfloat16)
         plane = lax.dot_general(
-            place_table, arrived_rows, (((0,), (0,)), ((), ())), preferred_element_type=jnp.float32
+            place_table, arrived[:, :width], (((0,), (0,)), ((), ())), preferred_element_type=jnp.float32
         ).astype(jnp.bfloat16)
-        sums, notes = ring_experts(note, plane, weight_in[0], weight_out[0], dp_count)
+        parts, notes = ring_experts(note, plane, weight_in[0], weight_out[0], dp_count)
         table = jnp.concatenate(notes).astype(jnp.float32)
         table = lax.dynamic_slice_in_dim(
             jnp.concatenate([table, table]), (dp_count - own_dp) % dp_count, dp_count, 0
@@ -181,14 +292,13 @@
         )
         gates = jnp.pad(gates.reshape(-1), (0, 2 * rows_all))
         gates = lax.dynamic_slice_in_dim(gates, first_slot + first, round_rows, 0)
-        scaled = (gates[:, None] * sums).astype(jnp.bfloat16)
-        returned = jnp.dot(place_table, scaled, preferred_element_type=jnp.float32)
-        return step + 1, jnp.max(plane_counts), sent_back + returned.astype(jnp.bfloat16)
+        sent_back = finish(parts, gates[:, None], here, sent_back)
+        return step + 1, jnp.max(plane_counts), sent_back
 
     _, _, sent_back = lax.while_loop(
         lambda state: state[0] * round_rows < state[1],
         experts,
-        (jnp.int32(0), jnp.int32(1), jnp.zeros((rows_all, width), jnp.bfloat16)),
+        (jnp.int32(0), jnp.int32(1), blank),
     )
     results = lax.all_to_all(
         sent_back.reshape(expert_count, MOST, width), EXPERT, split_axis=0, concat_axis=0, tiled=True

time: 176 us -> 180 us (1.023)
  local copies, waits for them, and re-layouts: 2.36 us -> 6.93 us
  waiting for transfers between devices: 64.1 us -> 60.1 us
  Pallas kernels: 18.9 us -> 22.1 us
  matrix products: 7.68 us -> 4.88 us
  blocking collectives: 24.8 us -> 26.7 us
    dot_general x3 -> x1, matrix products: 6.03 us -> 1.68 us  [experts(): lax.dot_general(place_table, arrived[:, :width], (((0,), (0,)), ((), ()))...]
    pallas_call x4 -> x6, Pallas kernels: 18.9 us -> 22.1 us  [the longest x4 17.7 us: expert_rows(): pl.pallas_call(staged_expert_kernel if staged else expert_kernel, out_sha...]
    convert_element_type x10, other arithmetic: 4.73 us -> 7.09 us  [narrow(): return rows.astype(jnp.bfloat16)]
    ppermute x14, waiting for transfers between devices: 19 us -> 16.7 us  [hop(): down_rows = lax.ppermute(down_rows, 'dp', downward)]
    add x2 -> x0, other arithmetic: 2.13 us -> none  [the longest x1 1.07 us: ring_experts(): last[2] + wide(seconds[0]) + wide(firsts[1])]
    unnamed x2 -> x8, local copies, waits for them, and re-layouts: 0.01 us -> 1.99 us
    all_to_all x1, blocking collectives: 24.8 us -> 26.7 us  [on_device(): lax.all_to_all(sent_back.reshape(expert_count, MOST, width), EXPERT, spli...]
  transfers between devices with their start and end apart: 29 -> 29, of which waited for: 15 -> 16; matrix products, arithmetic and copies ran while one was open for 4% -> 6% of each run, Pallas kernels for 11% -> 10%
where the time goes in v5:
time: 180 us; the launch traced here: 179 us
  waiting for transfers between devices  60.1 us (33%)
  starting transfers between devices  45.9 us (26%)
  blocking collectives  26.7 us (15%)
  Pallas kernels  22.1 us (12%)
  other arithmetic  10.9 us (6%)
  local copies, waits for them, and re-layouts  6.93 us (4%)
  matrix products  4.88 us (3%)
    ppermute x14, starting transfers between devices, hop(): down_rows = lax.ppermute(down_rows, 'dp', downward)  34 us
    all_to_all x1, blocking collectives, on_device(): lax.all_to_all(sent_back.reshape(expert_count, MOST, width), EXPERT, spli...  26.7 us
    ppermute x14, waiting for transfers between devices, hop(): up_rows = lax.ppermute(up_rows, 'dp', upward)  25.8 us
    pallas_call x4, Pallas kernels, expert_rows(): pl.pallas_call(staged_expert_kernel if staged else expert_kernel, out_sha...  17.7 us
    all_to_all x1, waiting for transfers between devices, on_device(): lax.all_to_all(packed.reshape(expert_count, MOST, width + LANES), EXPERT,...  17.7 us
    ppermute x14, waiting for transfers between devices, hop(): down_rows = lax.ppermute(down_rows, 'dp', downward)  16.7 us
    all_to_all x1, starting transfers between devices, on_device(): lax.all_to_all(packed.reshape(expert_count, MOST, width + LANES), EXPERT,...  8.76 us
    convert_element_type x10, other arithmetic, narrow(): return rows.astype(jnp.bfloat16)  7.09 us
  transfers between devices with their start and end apart: 29, of which 16 were waited for; matrix products, arithmetic and copies ran while one was open for 6% of the time, Pallas kernels for 10%

profile of v5, /device:TPU:1, one launch (start us, length us, event | category | flops | bytes accessed | tf_op | source)
XLA Modules:
  0.0 179.3 jit_solution(16062152010153628227)
XLA Ops:
  4.6 8.8 %all-to-all-start = ((bf16[32,8,2176]{2,1,0:T(8,128)(2,1)}), bf16[32,8,2176]{2,1,0:T(8,128)(2,1)}, u32[]{:S(2)}, u32[]{:S(2)}) async-start(bf16[32,8,2176]{2,1,0:T(8,128)(2,1)} %bitcast.5), calls=%async_computation | async-start | bytes 2228224 | tf_op jit(solution)/shard_map/all_to_all | solution.py:255
  13.4 17.7 %all-to-all-done = bf16[32,8,2176]{2,1,0:T(8,128)(2,1)} async-done(((bf16[32,8,2176]{2,1,0:T(8,128)(2,1)}), bf16[32,8,2176]{2,1,0:T(8,128)(2,1)}, u32[]{:S(2)}, u32[]{:S(2)}) %all-to-all-start) | async-done | bytes 1114144 | tf_op jit(solution)/shard_map/all_to_all | solution.py:255
  34.3 116.8 %while.14 = (s32[]{:T(128)}, s32[]{:T(128)}, bf16[256,2048]{1,0:T(8,128)(2,1)}, bf16[8,2048]{1,0:T(8,128)(2,1)}, f32[256,128]{1,0:T(8,128)}, /*index=5*/bf16[256...) while((s32[]{:T(128)}, s32[]{:T(128)}, ...), condition=%wide.region_3.4_spmd, body=%wide.region_0.3_spmd.sunk | while | flops 10911234048 | bytes 146574976 | solution.py:298
  39.6 4.0 %collective-permute-start.3 = (bf16[80,2048]{1,0:T(8,128)(2,1)S(1)}, bf16[80,2048]{1,0:T(8,128)(2,1)S(1)}, u32[]{:S(2)}, u32[]{:S(2)}) collective-permute-start(bf16[80,2048]{1,0:T(8,128)(2,1)S(1)} %get-tuple-element.328.refs_2_), channel_id=1, source_target_pairs={{0,224},{32,0},{64,32},{96,64},{128,96},{160,128},{192,160},{224,1... | collective-permute-start | bytes 983048 | tf_op jit(solution)/shard_map/while/body/ppermute | solution.py:197
  45.1 5.5 %collective-permute-done.3.refs_3_ = bf16[80,2048]{1,0:T(8,128)(2,1)S(1)} collective-permute-done((bf16[80,2048]{1,0:T(8,128)(2,1)S(1)}, bf16[80,2048]{1,0:T(8,128)(2,1)S(1)}, u32[]{:S(2)}, u32[]{:S(2)}) %collective-permute-start.3) | collective-permute-done | bytes 327712 | tf_op jit(solution)/shard_map/while/body/ppermute | solution.py:197
  52.2 2.7 %collective-permute-start.7 = (bf16[80,2048]{1,0:T(8,128)(2,1)S(1)}, bf16[80,2048]{1,0:T(8,128)(2,1)S(1)}, u32[]{:S(2)}, u32[]{:S(2)}) collective-permute-start(bf16[80,2048]{1,0:T(8,128)(2,1)S(1)} %collective-permute-done.3.refs_3_), channel_id=1, source_target_pairs={{0,224},{32,0},{64,32},{96,64},{128,96},{160,128},{192,160},{224,1... | collective-permute-start | bytes 983048 | tf_op jit(solution)/shard_map/while/body/ppermute | solution.py:197
  54.9 4.3 %collective-permute-done.refs_1_ = bf16[80,2048]{1,0:T(8,128)(2,1)S(1)} collective-permute-done((bf16[80,2048]{1,0:T(8,128)(2,1)S(1)}, bf16[80,2048]{1,0:T(8,128)(2,1)S(1)}, u32[]{:S(2)}, u32[]{:S(2)}) %collective-permute-start) | collective-permute-done | bytes 327712 | tf_op jit(solution)/shard_map/while/body/ppermute | solution.py:196
  61.8 6.3 %expert_rows.16 = (f32[80,2048]{1,0:T(8,128)S(1)}, f32[80,2048]{1,0:T(8,128)S(1)}, f32[80,2048]{1,0:T(8,128)S(1)}, f32[80,2048]{1,0:T(8,128)S(1)}) custom-call(bf16[88,2048]{1,0:T(8,128)(2,1)S(1)} %collective-permute-done.2.refs_0_, bf16[80,2048]{1,0:T(8,128)(2,1)S(1)} %collective-permute-done.refs_1_, bf16[88,2048]{1,0:T(8,128)(2,1)S(1)} %collective-permute-done.1.refs_2_, ...), custom_call_target="tpu_custom_call" | custom-call | flops 2684354560 | bytes 12320768 | tf_op jit(solution)/shard_map/while/body/expert_rows/pallas_call | solution.py:108
  68.9 2.7 %collective-permute-start.11 = (bf16[80,2048]{1,0:T(8,128)(2,1)S(1)}, bf16[80,2048]{1,0:T(8,128)(2,1)S(1)}, u32[]{:S(2)}, u32[]{:S(2)}) collective-permute-start(bf16[80,2048]{1,0:T(8,128)(2,1)S(1)} %collective-permute-done.7.refs_3_), channel_id=1, source_target_pairs={{0,224},{32,0},{64,32},{96,64},{128,96},{160,128},{192,160},{224,1... | collective-permute-start | bytes 983048 | tf_op jit(solution)/shard_map/while/body/ppermute | solution.py:197
  73.6 2.8 %collective-permute-start.9 = (bf16[88,2048]{1,0:T(8,128)(2,1)S(1)}, bf16[88,2048]{1,0:T(8,128)(2,1)S(1)}, u32[]{:S(2)}, u32[]{:S(2)}) collective-permute-start(bf16[88,2048]{1,0:T(8,128)(2,1)S(1)} %collective-permute-done.5.refs_2_), channel_id=1, source_target_pairs={{0,224},{32,0},{64,32},{96,64},{128,96},{160,128},{192,160},{224,1... | collective-permute-start | bytes 1081352 | tf_op jit(solution)/shard_map/while/body/ppermute | solution.py:197
  76.5 3.8 %expert_rows.17 = (f32[80,2048]{1,0:T(8,128)S(1)}, f32[80,2048]{1,0:T(8,128)S(1)}, f32[80,2048]{1,0:T(8,128)S(1)}, f32[80,2048]{1,0:T(8,128)S(1)}) custom-call(bf16[88,2048]{1,0:T(8,128)(2,1)S(1)} %collective-permute-done.6.refs_0_, bf16[80,2048]{1,0:T(8,128)(2,1)S(1)} %collective-permute-done.4.refs_1_, ...), custom_call_target="tpu_custom_call" | custom-call | flops 2684354560 | bytes 12320768 | tf_op jit(solution)/shard_map/while/body/expert_rows/pallas_call | solution.py:108
  81.2 2.7 %collective-permute-start.13 = (bf16[80,2048]{1,0:T(8,128)(2,1)S(1)}, bf16[80,2048]{1,0:T(8,128)(2,1)S(1)}, u32[]{:S(2)}, u32[]{:S(2)}) collective-permute-start(bf16[80,2048]{1,0:T(8,128)(2,1)S(1)} %collective-permute-done.11.refs_3_), channel_id=1, source_target_pairs={{0,224},{32,0},{64,32},{96,64},{128,96},{160,128},{192,160},{224,1... | collective-permute-start | bytes 983048 | tf_op jit(solution)/shard_map/while/body/ppermute | solution.py:197
  83.8 4.3 %collective-permute-done.8.refs_1_ = bf16[80,2048]{1,0:T(8,128)(2,1)S(1)} collective-permute-done((bf16[80,2048]{1,0:T(8,128)(2,1)S(1)}, bf16[80,2048]{1,0:T(8,128)(2,1)S(1)}, u32[]{:S(2)}, u32[]{:S(2)}) %collective-permute-start.8) | collective-permute-done | bytes 327712 | tf_op jit(solution)/shard_map/while/body/ppermute | solution.py:196
  88.2 3.8 %expert_rows.18 = (bf16[80,2048]{1,0:T(8,128)(2,1)S(1)}, f32[80,2048]{1,0:T(8,128)S(1)}, f32[80,2048]{1,0:T(8,128)S(1)}, bf16[80,2048]{1,0:T(8,128)(2,1)S(1)}) custom-call(bf16[88,2048]{1,0:T(8,128)(2,1)S(1)} %collective-permute-done.10.refs_0_, bf16[80,2048]{1,0:T(8,128)(2,1)S(1)} %collective-permute-done.8.refs_1_, ...), custom_call_target="tpu_custom_call" | custom-call | flops 2684354560 | bytes 12320768 | tf_op jit(solution)/shard_map/while/body/expert_rows/pallas_call | solution.py:108
  92.1 2.7 %collective-permute-start.17 = (bf16[80,2048]{1,0:T(8,128)(2,1)S(1)}, bf16[80,2048]{1,0:T(8,128)(2,1)S(1)}, u32[]{:S(2)}, u32[]{:S(2)}) collective-permute-start(bf16[80,2048]{1,0:T(8,128)(2,1)S(1)} %get-tuple-element.351), channel_id=1, source_target_pairs={{0,224},{32,0},{64,32},{96,64},{128,96},{160,128},{192,160},{224,1... | collective-permute-start | bytes 983048 | tf_op jit(solution)/shard_map/while/body/ppermute | solution.py:197
  95.9 3.8 %expert_rows.19 = (bf16[80,2048]{1,0:T(8,128)(2,1)S(1)}, f32[80,2048]{1,0:T(8,128)S(1)}, f32[80,2048]{1,0:T(8,128)S(1)}, bf16[80,2048]{1,0:T(8,128)(2,1)S(1)}) custom-call(bf16[88,2048]{1,0:T(8,128)(2,1)S(1)} %collective-permute-done.12.refs_0_, bf16[88,2048]{1,0:T(8,128)(2,1)S(1)} %pad_maximum_fusion.2.refs_1_, ...), custom_call_target="tpu_custom_call" | custom-call | flops 2684354560 | bytes 12320768 | tf_op jit(solution)/shard_map/while/body/expert_rows/pallas_call | solution.py:108
  99.8 2.7 %collective-permute-start.15 = (bf16[80,2048]{1,0:T(8,128)(2,1)S(1)}, bf16[80,2048]{1,0:T(8,128)(2,1)S(1)}, u32[]{:S(2)}, u32[]{:S(2)}) collective-permute-start(bf16[80,2048]{1,0:T(8,128)(2,1)S(1)} %get-tuple-element.357), channel_id=1, source_target_pairs={{0,224},{32,0},{64,32},{96,64},{128,96},{160,128},{192,160},{224,1... | collective-permute-start | bytes 983048 | tf_op jit(solution)/shard_map/while/body/ppermute | solution.py:197
  104.2 4.1 %collective-permute-done.14 = bf16[80,2048]{1,0:T(8,128)(2,1)S(1)} collective-permute-done((bf16[80,2048]{1,0:T(8,128)(2,1)S(1)}, bf16[80,2048]{1,0:T(8,128)(2,1)S(1)}, u32[]{:S(2)}, u32[]{:S(2)}) %collective-permute-start.14) | collective-permute-done | bytes 327712 | tf_op jit(solution)/shard_map/while/body/ppermute | solution.py:196
  111.2 4.2 %collective-permute-done.21 = bf16[80,2048]{1,0:T(8,128)(2,1)S(1)} collective-permute-done((bf16[80,2048]{1,0:T(8,128)(2,1)S(1)}, bf16[80,2048]{1,0:T(8,128)(2,1)S(1)}, u32[]{:S(2)}, u32[]{:S(2)}) %collective-permute-start.21) | collective-permute-done | bytes 327712 | tf_op jit(solution)/shard_map/while/body/ppermute | solution.py:197
  117.0 5.4 %collective-permute-done.19 = bf16[80,2048]{1,0:T(8,128)(2,1)S(1)} collective-permute-done((bf16[80,2048]{1,0:T(8,128)(2,1)S(1)}, bf16[80,2048]{1,0:T(8,128)(2,1)S(1)}, u32[]{:S(2)}, u32[]{:S(2)}) %collective-permute-start.19) | collective-permute-done | bytes 327712 | tf_op jit(solution)/shard_map/while/body/ppermute | solution.py:197
  127.3 2.7 %collective-permute-start.25 = (bf16[80,2048]{1,0:T(8,128)(2,1)}, bf16[80,2048]{1,0:T(8,128)(2,1)S(1)}, u32[]{:S(2)}, u32[]{:S(2)}) collective-permute-start(bf16[80,2048]{1,0:T(8,128)(2,1)} %add_convert_fusion.25), channel_id=1, source_target_pairs={{0,224},{32,0},{64,32},{96,64},{128,96},{160,128},{192,160},{224,1... | collective-permute-start | bytes 983048 | tf_op jit(solution)/shard_map/while/body/ppermute | solution.py:197
  130.3 3.6 %collective-permute-done.22 = bf16[80,2048]{1,0:T(8,128)(2,1)} collective-permute-done((bf16[80,2048]{1,0:T(8,128)(2,1)}, bf16[80,2048]{1,0:T(8,128)(2,1)}, u32[]{:S(2)}, u32[]{:S(2)}) %collective-permute-start.22) | collective-permute-done | bytes 327712 | tf_op jit(solution)/shard_map/while/body/ppermute | solution.py:196
  144.2 3.7 %collective-permute-done.24.refs_1_ = bf16[80,2048]{1,0:T(8,128)(2,1)S(1)} collective-permute-done((bf16[80,2048]{1,0:T(8,128)(2,1)}, bf16[80,2048]{1,0:T(8,128)(2,1)S(1)}, u32[]{:S(2)}, u32[]{:S(2)}) %collective-permute-start.24) | collective-permute-done | bytes 327712 | tf_op jit(solution)/shard_map/while/body/ppermute | solution.py:196
  151.1 26.7 %all_to_all.10 = bf16[32,8,2048]{2,1,0:T(8,128)(2,1)S(1)} all-to-all(bf16[32,8,2048]{2,1,0:T(8,128)(2,1)} %bitcast.21), channel_id=1, replica_groups=mesh['dp'=8,'expert_0'=4,'expert_1'=4,'expert_2'=2] {'expert_0','expert_..., dimensions={0} | all-to-all | bytes 2097152 | tf_op jit(solution)/shard_map/all_to_all | solution.py:303
  (97 shorter events, 48.4 us)
Async XLA Ops:
  4.6 26.5 %all-to-all-start = ((bf16[32,8,2176]{2,1,0:T(8,128)(2,1)}), bf16[32,8,2176]{2,1,0:T(8,128)(2,1)}, u32[]{:S(2)}, u32[]{:S(2)}) async-start(bf16[32,8,2176]{2,1,0:T(8,128)(2,1)} %bitcast.5), calls=%async_computation | async-start | bytes 2228224 | tf_op jit(solution)/shard_map/all_to_all | solution.py:255
  37.9 14.3 %collective-permute-start.2 = (bf16[88,2048]{1,0:T(8,128)(2,1)S(1)}, bf16[88,2048]{1,0:T(8,128)(2,1)S(1)}, u32[]{:S(2)}, u32[]{:S(2)}) collective-permute-start(bf16[88,2048]{1,0:T(8,128)(2,1)S(1)} %pad_maximum_fusion.2.refs_1_), channel_id=1, source_target_pairs={{0,32},{32,64},{64,96},{96,128},{128,160},{160,192},{192,224},{224... | collective-permute-start | bytes 1081352 | tf_op jit(solution)/shard_map/while/body/ppermute | solution.py:196
  39.6 11.0 %collective-permute-start.3 = (bf16[80,2048]{1,0:T(8,128)(2,1)S(1)}, bf16[80,2048]{1,0:T(8,128)(2,1)S(1)}, u32[]{:S(2)}, u32[]{:S(2)}) collective-permute-start(bf16[80,2048]{1,0:T(8,128)(2,1)S(1)} %get-tuple-element.328.refs_2_), channel_id=1, source_target_pairs={{0,224},{32,0},{64,32},{96,64},{128,96},{160,128},{192,160},{224,1... | collective-permute-start | bytes 983048 | tf_op jit(solution)/shard_map/while/body/ppermute | solution.py:197
  43.6 15.6 %collective-permute-start.1 = (bf16[88,2048]{1,0:T(8,128)(2,1)S(1)}, bf16[88,2048]{1,0:T(8,128)(2,1)S(1)}, u32[]{:S(2)}, u32[]{:S(2)}) collective-permute-start(bf16[88,2048]{1,0:T(8,128)(2,1)S(1)} %pad_maximum_fusion.2.refs_1_), channel_id=1, source_target_pairs={{0,224},{32,0},{64,32},{96,64},{128,96},{160,128},{192,160},{224,1... | collective-permute-start | bytes 1081352 | tf_op jit(solution)/shard_map/while/body/ppermute | solution.py:197
  45.0 14.2 %collective-permute-start = (bf16[80,2048]{1,0:T(8,128)(2,1)S(1)}, bf16[80,2048]{1,0:T(8,128)(2,1)S(1)}, u32[]{:S(2)}, u32[]{:S(2)}) collective-permute-start(bf16[80,2048]{1,0:T(8,128)(2,1)S(1)} %get-tuple-element.328.refs_2_), channel_id=1, source_target_pairs={{0,32},{32,64},{64,96},{96,128},{128,160},{160,192},{192,224},{224... | collective-permute-start | bytes 983048 | tf_op jit(solution)/shard_map/while/body/ppermute | solution.py:196
  52.2 16.7 %collective-permute-start.6 = (bf16[88,2048]{1,0:T(8,128)(2,1)S(1)}, bf16[88,2048]{1,0:T(8,128)(2,1)S(1)}, u32[]{:S(2)}, u32[]{:S(2)}) collective-permute-start(bf16[88,2048]{1,0:T(8,128)(2,1)S(1)} %collective-permute-done.2.refs_0_), channel_id=1, source_target_pairs={{0,32},{32,64},{64,96},{96,128},{128,160},{160,192},{192,224},{224... | collective-permute-start | bytes 1081352 | tf_op jit(solution)/shard_map/while/body/ppermute | solution.py:196
  52.2 16.7 %collective-permute-start.7 = (bf16[80,2048]{1,0:T(8,128)(2,1)S(1)}, bf16[80,2048]{1,0:T(8,128)(2,1)S(1)}, u32[]{:S(2)}, u32[]{:S(2)}) collective-permute-start(bf16[80,2048]{1,0:T(8,128)(2,1)S(1)} %collective-permute-done.3.refs_3_), channel_id=1, source_target_pairs={{0,224},{32,0},{64,32},{96,64},{128,96},{160,128},{192,160},{224,1... | collective-permute-start | bytes 983048 | tf_op jit(solution)/shard_map/while/body/ppermute | solution.py:197
  59.2 14.4 %collective-permute-start.5 = (bf16[88,2048]{1,0:T(8,128)(2,1)S(1)}, bf16[88,2048]{1,0:T(8,128)(2,1)S(1)}, u32[]{:S(2)}, u32[]{:S(2)}) collective-permute-start(bf16[88,2048]{1,0:T(8,128)(2,1)S(1)} %collective-permute-done.1.refs_2_), channel_id=1, source_target_pairs={{0,224},{32,0},{64,32},{96,64},{128,96},{160,128},{192,160},{224,1... | collective-permute-start | bytes 1081352 | tf_op jit(solution)/shard_map/while/body/ppermute | solution.py:197
  61.7 11.9 %collective-permute-start.4 = (bf16[80,2048]{1,0:T(8,128)(2,1)S(1)}, bf16[80,2048]{1,0:T(8,128)(2,1)S(1)}, u32[]{:S(2)}, u32[]{:S(2)}) collective-permute-start(bf16[80,2048]{1,0:T(8,128)(2,1)S(1)} %collective-permute-done.refs_1_), channel_id=1, source_target_pairs={{0,32},{32,64},{64,96},{96,128},{128,160},{160,192},{192,224},{224... | collective-permute-start | bytes 983048 | tf_op jit(solution)/shard_map/while/body/ppermute | solution.py:196
  68.9 12.2 %collective-permute-start.10 = (bf16[88,2048]{1,0:T(8,128)(2,1)S(1)}, bf16[88,2048]{1,0:T(8,128)(2,1)S(1)}, u32[]{:S(2)}, u32[]{:S(2)}) collective-permute-start(bf16[88,2048]{1,0:T(8,128)(2,1)S(1)} %collective-permute-done.6.refs_0_), channel_id=1, source_target_pairs={{0,32},{32,64},{64,96},{96,128},{128,160},{160,192},{192,224},{224... | collective-permute-start | bytes 1081352 | tf_op jit(solution)/shard_map/while/body/ppermute | solution.py:196
  68.9 11.4 %collective-permute-start.11 = (bf16[80,2048]{1,0:T(8,128)(2,1)S(1)}, bf16[80,2048]{1,0:T(8,128)(2,1)S(1)}, u32[]{:S(2)}, u32[]{:S(2)}) collective-permute-start(bf16[80,2048]{1,0:T(8,128)(2,1)S(1)} %collective-permute-done.7.refs_3_), channel_id=1, source_target_pairs={{0,224},{32,0},{64,32},{96,64},{128,96},{160,128},{192,160},{224,1... | collective-permute-start | bytes 983048 | tf_op jit(solution)/shard_map/while/body/ppermute | solution.py:197
  73.6 14.6 %collective-permute-start.9 = (bf16[88,2048]{1,0:T(8,128)(2,1)S(1)}, bf16[88,2048]{1,0:T(8,128)(2,1)S(1)}, u32[]{:S(2)}, u32[]{:S(2)}) collective-permute-start(bf16[88,2048]{1,0:T(8,128)(2,1)S(1)} %collective-permute-done.5.refs_2_), channel_id=1, source_target_pairs={{0,224},{32,0},{64,32},{96,64},{128,96},{160,128},{192,160},{224,1... | collective-permute-start | bytes 1081352 | tf_op jit(solution)/shard_map/while/body/ppermute | solution.py:197
  76.5 11.7 %collective-permute-start.8 = (bf16[80,2048]{1,0:T(8,128)(2,1)S(1)}, bf16[80,2048]{1,0:T(8,128)(2,1)S(1)}, u32[]{:S(2)}, u32[]{:S(2)}) collective-permute-start(bf16[80,2048]{1,0:T(8,128)(2,1)S(1)} %collective-permute-done.4.refs_1_), channel_id=1, source_target_pairs={{0,32},{32,64},{64,96},{96,128},{128,160},{160,192},{192,224},{224... | collective-permute-start | bytes 983048 | tf_op jit(solution)/shard_map/while/body/ppermute | solution.py:196
  81.1 14.7 %collective-permute-start.12 = (bf16[88,2048]{1,0:T(8,128)(2,1)S(1)}, bf16[88,2048]{1,0:T(8,128)(2,1)S(1)}, u32[]{:S(2)}, u32[]{:S(2)}) collective-permute-start(bf16[88,2048]{1,0:T(8,128)(2,1)S(1)} %collective-permute-done.10.refs_0_), channel_id=1, source_target_pairs={{0,32},{32,64},{64,96},{96,128},{128,160},{160,192},{192,224},{224... | collective-permute-start | bytes 1081352 | tf_op jit(solution)/shard_map/while/body/ppermute | solution.py:196
  81.2 13.6 %collective-permute-start.13 = (bf16[80,2048]{1,0:T(8,128)(2,1)S(1)}, bf16[80,2048]{1,0:T(8,128)(2,1)S(1)}, u32[]{:S(2)}, u32[]{:S(2)}) collective-permute-start(bf16[80,2048]{1,0:T(8,128)(2,1)S(1)} %collective-permute-done.11.refs_3_), channel_id=1, source_target_pairs={{0,224},{32,0},{64,32},{96,64},{128,96},{160,128},{192,160},{224,1... | collective-permute-start | bytes 983048 | tf_op jit(solution)/shard_map/while/body/ppermute | solution.py:197
  92.0 10.5 %collective-permute-start.16 = (bf16[80,2048]{1,0:T(8,128)(2,1)S(1)}, bf16[80,2048]{1,0:T(8,128)(2,1)S(1)}, u32[]{:S(2)}, u32[]{:S(2)}) collective-permute-start(bf16[80,2048]{1,0:T(8,128)(2,1)S(1)} %get-tuple-element.350), channel_id=1, source_target_pairs={{0,32},{32,64},{64,96},{96,128},{128,160},{160,192},{192,224},{224... | collective-permute-start | bytes 983048 | tf_op jit(solution)/shard_map/while/body/ppermute | solution.py:196
  92.1 10.4 %collective-permute-start.17 = (bf16[80,2048]{1,0:T(8,128)(2,1)S(1)}, bf16[80,2048]{1,0:T(8,128)(2,1)S(1)}, u32[]{:S(2)}, u32[]{:S(2)}) collective-permute-start(bf16[80,2048]{1,0:T(8,128)(2,1)S(1)} %get-tuple-element.351), channel_id=1, source_target_pairs={{0,224},{32,0},{64,32},{96,64},{128,96},{160,128},{192,160},{224,1... | collective-permute-start | bytes 983048 | tf_op jit(solution)/shard_map/while/body/ppermute | solution.py:197
  102.6 12.8 %collective-permute-start.21 = (bf16[80,2048]{1,0:T(8,128)(2,1)S(1)}, bf16[80,2048]{1,0:T(8,128)(2,1)S(1)}, u32[]{:S(2)}, u32[]{:S(2)}) collective-permute-start(bf16[80,2048]{1,0:T(8,128)(2,1)S(1)} %add_convert_fusion.21), channel_id=1, source_target_pairs={{0,224},{32,0},{64,32},{96,64},{128,96},{160,128},{192,160},{224,1... | collective-permute-start | bytes 983048 | tf_op jit(solution)/shard_map/while/body/ppermute | solution.py:197
  103.3 12.1 %collective-permute-start.20 = (bf16[80,2048]{1,0:T(8,128)(2,1)S(1)}, bf16[80,2048]{1,0:T(8,128)(2,1)S(1)}, u32[]{:S(2)}, u32[]{:S(2)}) collective-permute-start(bf16[80,2048]{1,0:T(8,128)(2,1)S(1)} %add_convert_fusion.20), channel_id=1, source_target_pairs={{0,32},{32,64},{64,96},{96,128},{128,160},{160,192},{192,224},{224... | collective-permute-start | bytes 983048 | tf_op jit(solution)/shard_map/while/body/ppermute | solution.py:196
  108.5 13.9 %collective-permute-start.19 = (bf16[80,2048]{1,0:T(8,128)(2,1)S(1)}, bf16[80,2048]{1,0:T(8,128)(2,1)S(1)}, u32[]{:S(2)}, u32[]{:S(2)}) collective-permute-start(bf16[80,2048]{1,0:T(8,128)(2,1)S(1)} %add_convert_fusion.23), channel_id=1, source_target_pairs={{0,224},{32,0},{64,32},{96,64},{128,96},{160,128},{192,160},{224,1... | collective-permute-start | bytes 983048 | tf_op jit(solution)/shard_map/while/body/ppermute | solution.py:197
  111.1 11.3 %collective-permute-start.18 = (bf16[80,2048]{1,0:T(8,128)(2,1)S(1)}, bf16[80,2048]{1,0:T(8,128)(2,1)S(1)}, u32[]{:S(2)}, u32[]{:S(2)}) collective-permute-start(bf16[80,2048]{1,0:T(8,128)(2,1)S(1)} %add_convert_fusion.22), channel_id=1, source_target_pairs={{0,32},{32,64},{64,96},{96,128},{128,160},{160,192},{192,224},{224... | collective-permute-start | bytes 983048 | tf_op jit(solution)/shard_map/while/body/ppermute | solution.py:196
  127.3 15.5 %collective-permute-start.25 = (bf16[80,2048]{1,0:T(8,128)(2,1)}, bf16[80,2048]{1,0:T(8,128)(2,1)S(1)}, u32[]{:S(2)}, u32[]{:S(2)}) collective-permute-start(bf16[80,2048]{1,0:T(8,128)(2,1)} %add_convert_fusion.25), channel_id=1, source_target_pairs={{0,224},{32,0},{64,32},{96,64},{128,96},{160,128},{192,160},{224,1... | collective-permute-start | bytes 983048 | tf_op jit(solution)/shard_map/while/body/ppermute | solution.py:197
  130.1 12.7 %collective-permute-start.26 = (bf16[80,2048]{1,0:T(8,128)(2,1)}, bf16[80,2048]{1,0:T(8,128)(2,1)}, u32[]{:S(2)}, u32[]{:S(2)}) collective-permute-start(bf16[80,2048]{1,0:T(8,128)(2,1)} %add_convert_fusion.24), channel_id=1, source_target_pairs={{0,32},{32,64},{64,96},{96,128},{128,160},{160,192},{192,224},{224... | collective-permute-start | bytes 983048 | tf_op jit(solution)/shard_map/while/body/ppermute | solution.py:196
  139.0 8.9 %collective-permute-start.24 = (bf16[80,2048]{1,0:T(8,128)(2,1)}, bf16[80,2048]{1,0:T(8,128)(2,1)S(1)}, u32[]{:S(2)}, u32[]{:S(2)}) collective-permute-start(bf16[80,2048]{1,0:T(8,128)(2,1)} %add_convert_fusion.28), channel_id=1, source_target_pairs={{0,32},{32,64},{64,96},{96,128},{128,160},{160,192},{192,224},{224... | collective-permute-start | bytes 983048 | tf_op jit(solution)/shard_map/while/body/ppermute | solution.py:196
  (13 other events, 116.4 us)

commit v6 on v5

--- a/solution.py
+++ b/solution.py
@@ -66,7 +66,7 @@
 
 
 def staged_expert_kernel(*refs):
-    *refs, rows_ref, hidden_ref, first_ref, second_ref, first_sems, second_sems = refs
+    *refs, first_ref, second_ref, rows_ref, hidden_ref, first_sems, second_sems = refs
     pieces, first_far, second_far, outs = split_refs(refs)
 
     def first_copy(i):
@@ -95,19 +95,19 @@
     width, hidden = first_weight.shape
     count = len(pieces) * half
     scratch = [pltpu.VMEM((count, width), jnp.bfloat16), pltpu.VMEM((count, hidden), jnp.bfloat16)]
+    out_shape = [jax.ShapeDtypeStruct((half, width), kind) for kind in kinds]
     specs = {}
     if staged:
         scratch += [
-            pltpu.VMEM(first_weight.shape, jnp.bfloat16),
-            pltpu.VMEM(second_weight.shape, jnp.bfloat16),
             pltpu.SemaphoreType.DMA((hidden // BLOCK,)),
             pltpu.SemaphoreType.DMA((width // BLOCK,)),
         ]
+        out_shape += [pltpu.VMEM(w.shape, w.dtype) for w in (first_weight, second_weight)]
         near, far = pl.BlockSpec(memory_space=pltpu.VMEM), pl.BlockSpec(memory_space=pl.ANY)
-        specs = {"in_specs": [near] * len(pieces) + [far] * 2}
+        specs = {"in_specs": [near] * len(pieces) + [far] * 2, "out_specs": [near] * len(out_shape)}
     return pl.pallas_call(
         staged_expert_kernel if staged else expert_kernel,
-        out_shape=[jax.ShapeDtypeStruct((half, width), kind) for kind in kinds],
+        out_shape=out_shape,
         scratch_shapes=scratch,
         compiler_params=pltpu.CompilerParams(vmem_limit_bytes=VMEM_LIMIT),
         cost_estimate=pl.CostEstimate(
@@ -159,36 +159,105 @@
     )(tokens, expert_ranks, capacity[:, None])
 
 
+def place_kernel(arrived_ref, step_ref, gates_ref, top_ref, bottom_ref, here_ref):
+    rows_all = arrived_ref.shape[0]
+    half, width = bottom_ref.shape
+    taken = arrived_ref[:, width:]
+    earlier = lax.broadcasted_iota(jnp.int32, (rows_all, rows_all), 1) < lax.broadcasted_iota(
+        jnp.int32, (rows_all, rows_all), 0
+    )
+    place = jnp.dot(
+        jnp.where(earlier, 1.0, 0.0).astype(jnp.bfloat16), taken, preferred_element_type=jnp.float32
+    )
+    here = jnp.where(wide(taken) > 0.0, place, -1.0) - (step_ref[0] * 2 * half).astype(jnp.float32)
+    here_ref[...] = here
+    slots = lax.broadcasted_iota(jnp.int32, (rows_all, 2 * half), 1).astype(jnp.float32)
+    table = jnp.where(here[:, :1] == slots, 1.0, 0.0).astype(jnp.bfloat16)
+    plane = lax.dot_general(
+        table, arrived_ref[:, :width], (((0,), (0,)), ((), ())), preferred_element_type=jnp.float32
+    )
+    count = place[rows_all - 1 :] + wide(taken[rows_all - 1 :])
+    gates = gates_ref.shape[1]
+    top_ref[:NOTE] = jnp.zeros((NOTE, width), top_ref.dtype)
+    top_ref[:NOTE, :gates] = jnp.broadcast_to(gates_ref[...], (NOTE, gates)).astype(top_ref.dtype)
+    top_ref[:NOTE, gates : gates + LANES] = jnp.broadcast_to(count, (NOTE, LANES)).astype(top_ref.dtype)
+    top_ref[NOTE:] = plane[:half].astype(top_ref.dtype)
+    bottom_ref[...] = plane[half:].astype(bottom_ref.dtype)
+
+
+def place(arrived, step, gate_pieces, half):
+    rows_all = arrived.shape[0]
+    width = arrived.shape[1] - LANES
+    near = pl.BlockSpec(memory_space=pltpu.VMEM)
+    return pl.pallas_call(
+        place_kernel,
+        in_specs=[near, pl.BlockSpec(memory_space=pltpu.SMEM), near],
+        out_shape=[
+            jax.ShapeDtypeStruct((NOTE + half, width), jnp.bfloat16),
+            jax.ShapeDtypeStruct((half, width), jnp.bfloat16),
+            jax.ShapeDtypeStruct((rows_all, LANES), jnp.float32),
+        ],
+        compiler_params=pltpu.CompilerParams(vmem_limit_bytes=VMEM_LIMIT),
+        name="place",
+    )(arrived, step, gate_pieces)
+
+
 def finish_kernel(*refs):
-    *parts, gates_ref, target_ref, kept_ref, out_ref, scaled_ref = refs
+    step_ref, own_ref, *refs, here_ref, kept_ref, out_ref, next_ref, most_ref, scaled_ref = refs
+    parts, notes = refs[:6], [note[...].astype(jnp.float32)[:1] for note in refs[6:]]
     half = parts[0].shape[0]
-    for i, (own, one, other) in enumerate((parts[:3], parts[3:])):
-        rows = slice(i * half, (i + 1) * half)
-        sums = own[...] + wide(one[...]) + wide(other[...])
-        scaled_ref[rows] = narrow(gates_ref[rows] * sums)
-    target = target_ref[:, :1]
     count = 2 * half
-    slots = lax.broadcasted_iota(jnp.int32, (target.shape[0], count), 1).astype(jnp.float32)
-    table = jnp.where(target == slots, 1.0, 0.0).astype(jnp.bfloat16)
+    own, step = own_ref[0], step_ref[0]
+    planes = [lax.rem(own + j, len(notes)) for j in range(len(notes))]
+    first = jnp.full((1, LANES), (step * count).astype(jnp.float32))
+    most = jnp.zeros((1, LANES), jnp.float32)
+    for plane, note in zip(planes, notes):
+        rows = note[:, 3 * LANES :]
+        first = first + jnp.where(plane < own, rows, 0.0)
+        most = jnp.maximum(most, rows)
+    next_ref[0] = step + 1
+    most_ref[0] = jnp.max(most).astype(jnp.int32)
+    slots = first + lax.broadcasted_iota(jnp.int32, (count, LANES), 0).astype(jnp.float32)
+    lanes = lax.broadcasted_iota(jnp.int32, (1, LANES), 1)
+    gates = jnp.zeros((count, LANES), jnp.float32)
+    for plane, note in zip(planes, notes):
+        gate = note[:, :LANES] + note[:, LANES : 2 * LANES] + note[:, 2 * LANES : 3 * LANES]
+        gates = gates + jnp.where(slots == (plane * LANES + lanes).astype(jnp.float32), gate, 0.0)
+    gates = jnp.sum(gates, axis=1, keepdims=True)
+    for i, (mine, one, other) in enumerate((parts[:3], parts[3:])):
+        sums = mine[...] + wide(one[...]) + wide(other[...])
+        scaled_ref[i * half : (i + 1) * half] = narrow(gates[i * half : (i + 1) * half] * sums)
+    here = here_ref[:, :1]
+    places = lax.broadcasted_iota(jnp.int32, (here.shape[0], count), 1).astype(jnp.float32)
+    table = jnp.where(here == places, 1.0, 0.0).astype(jnp.bfloat16)
     returned = jnp.dot(table, scaled_ref[...], preferred_element_type=jnp.float32)
-    here = jnp.logical_and(target >= 0.0, target < count)
-    out_ref[...] = narrow(jnp.where(here, returned, wide(kept_ref[...])))
-
-
-def finish(parts, gates, target, kept):
+    inside = jnp.logical_and(here >= 0.0, here < count)
+    out_ref[...] = narrow(jnp.where(inside, returned, wide(kept_ref[...])))
+
+
+def finish(step, own_dp, parts, notes, here, kept):
     half, width = parts[0].shape
+    near, scalar = pl.BlockSpec(memory_space=pltpu.VMEM), pl.BlockSpec(memory_space=pltpu.SMEM)
+    corner = pl.BlockSpec((NOTE, 4 * LANES), lambda i: (0, 0))
     return pl.pallas_call(
         finish_kernel,
-        out_shape=jax.ShapeDtypeStruct(kept.shape, kept.dtype),
+        grid=(1,),
+        in_specs=[scalar] * 2 + [near] * len(parts) + [corner] * len(notes) + [near] * 2,
+        out_specs=[near, scalar, scalar],
+        out_shape=[
+            jax.ShapeDtypeStruct(kept.shape, kept.dtype),
+            jax.ShapeDtypeStruct((1,), jnp.int32),
+            jax.ShapeDtypeStruct((1,), jnp.int32),
+        ],
         scratch_shapes=[pltpu.VMEM((2 * half, width), jnp.bfloat16)],
         compiler_params=pltpu.CompilerParams(vmem_limit_bytes=VMEM_LIMIT),
         name="finish",
-    )(*parts, gates, target, kept)
-
-
-def ring_experts(note, plane, first_weight, second_weight, dp_count):
+    )(step, own_dp, *parts, *notes, here, kept)
+
+
+def ring_experts(top, bottom, first_weight, second_weight, dp_count):
     far = dp_count // 2
-    half = plane.shape[0] // 2
+    half = bottom.shape[0]
     upward = [(i, (i + 1) % dp_count) for i in range(dp_count)]
     downward = [(i, (i - 1) % dp_count) for i in range(dp_count)]
 
@@ -204,27 +273,28 @@
     def after(rows, *others):
         return lax.optimization_barrier((rows, others))[0]
 
-    top, bottom = jnp.concatenate([note, plane[:half]]), plane[half:]
-    kept = 4 * LANES
-    notes = {0: note[:1, :kept]}
+    notes = {0: top}
     firsts = hop(top, bottom)
     seconds = hop(bottom, top)
     outs, done = {}, ()
     for k in range(1, far):
         firsts = after(firsts, *done)
         seconds = after(seconds, *firsts)
-        notes[-k % dp_count], notes[k] = firsts[0][:1, :kept], seconds[1][:1, :kept]
+        notes[-k % dp_count], notes[k] = firsts[0], seconds[1]
         next_firsts = hop(*firsts)
         if k < far - 1:
             next_seconds = hop(*seconds)
-        outs[k] = mlp(firsts[0], seconds[0], seconds[1], firsts[1], sent=(0, 3) if k == far - 1 else (), staged=k == 1)
-        done = *outs[k], notes[-k % dp_count], notes[k]
+        pieces = firsts[0], seconds[0], seconds[1], firsts[1]
+        outs[k] = mlp(*pieces, sent=(0, 3) if k == far - 1 else (), staged=k == 1)
+        if k == 1:
+            *outs[k], first_weight, second_weight = outs[k]
+        done = tuple(outs[k])
         firsts, seconds = next_firsts, next_seconds
 
     below_top, below_bottom, above_top, above_bottom = outs[far - 1]
     seconds = hop(above_bottom, below_top)
     firsts = after(firsts, above_bottom, below_top, *done)
-    notes[far] = firsts[0][:1, :kept]
+    notes[far] = firsts[0]
     last = mlp(firsts[0], top, bottom, firsts[1], sent=(0, 3))
     sends = last[0], last[3]
     firsts = hop(*sends)
@@ -239,7 +309,7 @@
         sends = narrow(wide(firsts[0]) + above_top), narrow(wide(firsts[1]) + below_bottom)
         firsts = hop(*sends)
     parts = last[1], firsts[0], seconds[1], last[2], seconds[0], firsts[1]
-    return parts, after([notes[j] for j in range(dp_count)], *sends)
+    return parts, [notes[j] for j in range(dp_count)]
 
 
 def on_device(tokens, expert_ranks, capacity, weight_in, weight_out, gate_weights):
@@ -255,50 +325,23 @@
     arrived = lax.all_to_all(
         packed.reshape(expert_count, MOST, width + LANES), EXPERT, split_axis=0, concat_axis=0, tiled=True
     ).reshape(rows_all, width + LANES)
-    taken = arrived[:, width:]
-
-    earlier = lax.broadcasted_iota(jnp.int32, (rows_all, rows_all), 1) < lax.broadcasted_iota(
-        jnp.int32, (rows_all, rows_all), 0
-    )
-    place = jnp.dot(earlier.astype(jnp.bfloat16), taken, preferred_element_type=jnp.float32)
-    target = jnp.where(taken > 0, place, -1.0)
-    plane_count = (place + wide(taken))[rows_all - 1 :]
-
     gate_high = lax.reduce_precision(gate_weights, 8, 7)
     gate_left = gate_weights - gate_high
     gate_middle = lax.reduce_precision(gate_left, 8, 7)
     gate_low = gate_left - gate_middle
-    note = jnp.concatenate([gate_high, gate_middle, gate_low, plane_count], axis=1).astype(jnp.bfloat16)
-    note = jnp.pad(note, ((0, NOTE - 1), (0, width - note.shape[1])))
+    gate_pieces = jnp.concatenate([gate_high, gate_middle, gate_low], axis=1)
 
     def experts(state):
         step, _, sent_back = state
-        first = step * round_rows
-        here = target - first.astype(jnp.float32)
-        slot_ids = lax.broadcasted_iota(jnp.int32, (rows_all, round_rows), 1)
-        place_table = (here[:, :1] == slot_ids.astype(jnp.float32)).astype(jnp.bfloat16)
-        plane = lax.dot_general(
-            place_table, arrived[:, :width], (((0,), (0,)), ((), ())), preferred_element_type=jnp.float32
-        ).astype(jnp.bfloat16)
-        parts, notes = ring_experts(note, plane, weight_in[0], weight_out[0], dp_count)
-        table = jnp.concatenate(notes).astype(jnp.float32)
-        table = lax.dynamic_slice_in_dim(
-            jnp.concatenate([table, table]), (dp_count - own_dp) % dp_count, dp_count, 0
-        )
-        gates = table[:, :slots_dp] + table[:, slots_dp : 2 * slots_dp] + table[:, 2 * slots_dp : 3 * slots_dp]
-        plane_counts = table[:, 3 * slots_dp].astype(jnp.int32)
-        first_slot = jnp.sum(
-            jnp.where(lax.broadcasted_iota(jnp.int32, (dp_count,), 0) < own_dp, plane_counts, 0)
-        )
-        gates = jnp.pad(gates.reshape(-1), (0, 2 * rows_all))
-        gates = lax.dynamic_slice_in_dim(gates, first_slot + first, round_rows, 0)
-        sent_back = finish(parts, gates[:, None], here, sent_back)
-        return step + 1, jnp.max(plane_counts), sent_back
+        top, bottom, here = place(arrived, step, gate_pieces, round_rows // 2)
+        parts, notes = ring_experts(top, bottom, weight_in[0], weight_out[0], dp_count)
+        sent_back, step, most = finish(step, own_dp.reshape(1), parts, notes, here, sent_back)
+        return step, most, sent_back
 
     _, _, sent_back = lax.while_loop(
-        lambda state: state[0] * round_rows < state[1],
+        lambda state: state[0][0] * round_rows < state[1][0],
         experts,
-        (jnp.int32(0), jnp.int32(1), blank),
+        (jnp.zeros((1,), jnp.int32), jnp.ones((1,), jnp.int32), blank),
     )
     results = lax.all_to_all(
         sent_back.reshape(expert_count, MOST, width), EXPERT, split_axis=0, concat_axis=0, tiled=True

time: 180 us -> 168 us (0.933)
  other arithmetic: 10.9 us -> 1.27 us
  waiting for transfers between devices: 60.1 us -> 68.5 us
  local copies, waits for them, and re-layouts: 6.93 us -> 2.83 us
  matrix products: 4.88 us -> 1.43 us
  blocking collectives: 26.7 us -> 24.2 us
    convert_element_type x10, other arithmetic: 7.09 us -> 0.6 us  [narrow(): return rows.astype(jnp.bfloat16)]
    ppermute x14, waiting for transfers between devices: 25.8 us -> 31.7 us  [hop(): up_rows = lax.ppermute(up_rows, 'dp', upward)]
    dot_general x2 -> x0, matrix products: 3.45 us -> none  [the longest x1 1.77 us: on_device(): jnp.dot(earlier.astype(jnp.bfloat16), taken, preferred_element_type=jnp.f...]
    ppermute x14, waiting for transfers between devices: 16.7 us -> 19.8 us  [hop(): down_rows = lax.ppermute(down_rows, 'dp', downward)]
    all_to_all x1, blocking collectives: 26.7 us -> 24.2 us  [on_device(): lax.all_to_all(sent_back.reshape(expert_count, MOST, width), EXPERT, spli...]
    ppermute x14, starting transfers between devices: 3.15 us -> 5.54 us  [hop(): up_rows = lax.ppermute(up_rows, 'dp', upward)]
    ppermute x14, starting transfers between devices: 34 us -> 32.1 us  [hop(): down_rows = lax.ppermute(down_rows, 'dp', downward)]
  transfers between devices with their start and end apart: 29 -> 29, of which waited for: 16 -> 15; matrix products, arithmetic and copies ran while one was open for 6% -> 1% of each run, Pallas kernels for 10% -> 10%
where the time goes in v6:
time: 168 us
  waiting for transfers between devices  68.5 us (41%)
  starting transfers between devices  46.2 us (28%)
  blocking collectives  24.2 us (14%)
  Pallas kernels  21.8 us (13%)
  local copies, waits for them, and re-layouts  2.83 us (2%)
    ppermute x14, starting transfers between devices, hop(): down_rows = lax.ppermute(down_rows, 'dp', downward)  32.1 us
    ppermute x14, waiting for transfers between devices, hop(): up_rows = lax.ppermute(up_rows, 'dp', upward)  31.7 us
    all_to_all x1, blocking collectives, on_device(): lax.all_to_all(sent_back.reshape(expert_count, MOST, width), EXPERT, spli...  24.2 us
    ppermute x14, waiting for transfers between devices, hop(): down_rows = lax.ppermute(down_rows, 'dp', downward)  19.8 us
    pallas_call x4, Pallas kernels, expert_rows(): pl.pallas_call(staged_expert_kernel if staged else expert_kernel, out_sha...  17.6 us
    all_to_all x1, waiting for transfers between devices, on_device(): lax.all_to_all(packed.reshape(expert_count, MOST, width + LANES), EXPERT,...  17 us
    all_to_all x1, starting transfers between devices, on_device(): lax.all_to_all(packed.reshape(expert_count, MOST, width + LANES), EXPERT,...  8.58 us
    ppermute x14, starting transfers between devices, hop(): up_rows = lax.ppermute(up_rows, 'dp', upward)  5.54 us
  transfers between devices with their start and end apart: 29, of which 15 were waited for; matrix products, arithmetic and copies ran while one was open for 1% of the time, Pallas kernels for 10%

profile of v6, /device:TPU:1, one launch (start us, length us, event | category | flops | bytes accessed | tf_op | source)
XLA Modules:
  0.0 167.7 jit_solution(16859501344864490680)
XLA Ops:
  4.6 8.6 %all-to-all-start = ((bf16[32,8,2176]{2,1,0:T(8,128)(2,1)}), bf16[32,8,2176]{2,1,0:T(8,128)(2,1)S(1)}, u32[]{:S(2)}, u32[]{:S(2)}) async-start(bf16[32,8,2176]{2,1,0:T(8,128)(2,1)} %bitcast.5), calls=%async_computation | async-start | bytes 2228224 | tf_op jit(solution)/shard_map/all_to_all | solution.py:325
  13.9 17.0 %all-to-all-done = bf16[32,8,2176]{2,1,0:T(8,128)(2,1)S(1)} async-done(((bf16[32,8,2176]{2,1,0:T(8,128)(2,1)}), bf16[32,8,2176]{2,1,0:T(8,128)(2,1)S(1)}, u32[]{:S(2)}, u32[]{:S(2)}) %all-to-all-start) | async-done | bytes 1114144 | tf_op jit(solution)/shard_map/all_to_all | solution.py:325
  30.8 111.2 %while.11 = (s32[1]{0:T(128)}, s32[1]{0:T(128)}, bf16[256,2048]{1,0:T(8,128)(2,1)}, s32[]{:T(128)}, bf16[256,2176]{1,0:T(8,128)(2,1)S(1)}, /*index=5*/f32[1,384]...) while((s32[1]{0:T(128)}, s32[1]{0:T(128)}, bf16[256,2048]{1,0:T(8,128)(2,1)}, s32[]{:T(128)}, ...), condition=%region_1.0_spmd, body=%region_0.0_spmd | while | flops 10742333440 | bytes 106300640 | solution.py:341
  33.2 4.0 %collective-permute-start.1 = (bf16[80,2048]{1,0:T(8,128)(2,1)S(1)}, bf16[80,2048]{1,0:T(8,128)(2,1)S(1)}, u32[]{:S(2)}, u32[]{:S(2)}) collective-permute-start(bf16[80,2048]{1,0:T(8,128)(2,1)S(1)} %get-tuple-element.42.refs_2_), channel_id=1, source_target_pairs={{0,224},{32,0},{64,32},{96,64},{128,96},{160,128},{192,160},{224,1... | collective-permute-start | bytes 983048 | tf_op jit(solution)/shard_map/while/body/ppermute | solution.py:266
  38.7 5.5 %collective-permute-done.1.refs_3_ = bf16[80,2048]{1,0:T(8,128)(2,1)S(1)} collective-permute-done((bf16[80,2048]{1,0:T(8,128)(2,1)S(1)}, bf16[80,2048]{1,0:T(8,128)(2,1)S(1)}, u32[]{:S(2)}, u32[]{:S(2)}) %collective-permute-start.1) | collective-permute-done | bytes 327712 | tf_op jit(solution)/shard_map/while/body/ppermute | solution.py:266
  45.8 2.7 %collective-permute-start.3 = (bf16[80,2048]{1,0:T(8,128)(2,1)S(1)}, bf16[80,2048]{1,0:T(8,128)(2,1)S(1)}, u32[]{:S(2)}, u32[]{:S(2)}) collective-permute-start(bf16[80,2048]{1,0:T(8,128)(2,1)S(1)} %collective-permute-done.1.refs_3_), channel_id=1, source_target_pairs={{0,224},{32,0},{64,32},{96,64},{128,96},{160,128},{192,160},{224,1... | collective-permute-start | bytes 983048 | tf_op jit(solution)/shard_map/while/body/ppermute | solution.py:266
  48.5 4.3 %collective-permute-done.4.refs_1_ = bf16[80,2048]{1,0:T(8,128)(2,1)S(1)} collective-permute-done((bf16[80,2048]{1,0:T(8,128)(2,1)S(1)}, bf16[80,2048]{1,0:T(8,128)(2,1)S(1)}, u32[]{:S(2)}, u32[]{:S(2)}) %collective-permute-start.4) | collective-permute-done | bytes 327712 | tf_op jit(solution)/shard_map/while/body/ppermute | solution.py:265
  55.3 6.1 %expert_rows.4 = (f32[80,2048]{1,0:T(8,128)S(1)}, f32[80,2048]{1,0:T(8,128)S(1)}, f32[80,2048]{1,0:T(8,128)S(1)}, f32[80,2048]{1,0:T(8,128)S(1)}, bf16[2048,1024...) custom-call(bf16[88,2048]{1,0:T(8,128)(2,1)S(1)} %collective-permute-done.refs_0_.refs_15_, ...), custom_call_target="tpu_custom_call" | custom-call | flops 2684354560 | bytes 12320768 | tf_op jit(solution)/shard_map/while/body/expert_rows/pallas_call | solution.py:108
  61.6 2.7 %collective-permute-start.7 = (bf16[80,2048]{1,0:T(8,128)(2,1)S(1)}, bf16[80,2048]{1,0:T(8,128)(2,1)S(1)}, u32[]{:S(2)}, u32[]{:S(2)}) collective-permute-start(bf16[80,2048]{1,0:T(8,128)(2,1)S(1)} %collective-permute-done.3.refs_3_), channel_id=1, source_target_pairs={{0,224},{32,0},{64,32},{96,64},{128,96},{160,128},{192,160},{224,1... | collective-permute-start | bytes 983048 | tf_op jit(solution)/shard_map/while/body/ppermute | solution.py:266
  64.3 2.9 %collective-permute-done.8.refs_1_ = bf16[80,2048]{1,0:T(8,128)(2,1)S(1)} collective-permute-done((bf16[80,2048]{1,0:T(8,128)(2,1)S(1)}, bf16[80,2048]{1,0:T(8,128)(2,1)S(1)}, u32[]{:S(2)}, u32[]{:S(2)}) %collective-permute-start.8) | collective-permute-done | bytes 327712 | tf_op jit(solution)/shard_map/while/body/ppermute | solution.py:265
  67.2 2.8 %collective-permute-start.13 = (bf16[88,2048]{1,0:T(8,128)(2,1)S(1)}, bf16[88,2048]{1,0:T(8,128)(2,1)S(1)}, u32[]{:S(2)}, u32[]{:S(2)}) collective-permute-start(bf16[88,2048]{1,0:T(8,128)(2,1)S(1)} %collective-permute-done.9.refs_2_.refs_10_), channel_id=1, source_target_pairs={{0,224},{32,0},{64,32},{96,64},{128,96},{160,128},{192,160},{224,1... | collective-permute-start | bytes 1081352 | tf_op jit(solution)/shard_map/while/body/ppermute | solution.py:266
  70.1 3.8 %expert_rows.5 = (f32[80,2048]{1,0:T(8,128)S(1)}, f32[80,2048]{1,0:T(8,128)S(1)}, f32[80,2048]{1,0:T(8,128)S(1)}, f32[80,2048]{1,0:T(8,128)S(1)}) custom-call(bf16[88,2048]{1,0:T(8,128)(2,1)S(1)} %collective-permute-done.2.refs_0_.refs_14_, bf16[80,2048]{1,0:T(8,128)(2,1)S(1)} %collective-permute-done.8.refs_1_, ...), custom_call_target="tpu_custom_call" | custom-call | flops 2684354560 | bytes 12320768 | tf_op jit(solution)/shard_map/while/body/expert_rows/pallas_call | solution.py:108
  75.0 2.7 %collective-permute-start.11 = (bf16[80,2048]{1,0:T(8,128)(2,1)S(1)}, bf16[80,2048]{1,0:T(8,128)(2,1)S(1)}, u32[]{:S(2)}, u32[]{:S(2)}) collective-permute-start(bf16[80,2048]{1,0:T(8,128)(2,1)S(1)} %collective-permute-done.7.refs_3_), channel_id=1, source_target_pairs={{0,224},{32,0},{64,32},{96,64},{128,96},{160,128},{192,160},{224,1... | collective-permute-start | bytes 983048 | tf_op jit(solution)/shard_map/while/body/ppermute | solution.py:266
  77.6 4.3 %collective-permute-done.12.refs_1_ = bf16[80,2048]{1,0:T(8,128)(2,1)S(1)} collective-permute-done((bf16[80,2048]{1,0:T(8,128)(2,1)S(1)}, bf16[80,2048]{1,0:T(8,128)(2,1)S(1)}, u32[]{:S(2)}, u32[]{:S(2)}) %collective-permute-start.12) | collective-permute-done | bytes 327712 | tf_op jit(solution)/shard_map/while/body/ppermute | solution.py:265
  82.0 3.8 %expert_rows.6 = (bf16[80,2048]{1,0:T(8,128)(2,1)S(1)}, f32[80,2048]{1,0:T(8,128)S(1)}, f32[80,2048]{1,0:T(8,128)S(1)}, bf16[80,2048]{1,0:T(8,128)(2,1)S(1)}) custom-call(bf16[88,2048]{1,0:T(8,128)(2,1)S(1)} %collective-permute-done.6.refs_0_.refs_13_, bf16[80,2048]{1,0:T(8,128)(2,1)S(1)} %collective-permute-done.12.refs_1_, ...), custom_call_target="tpu_custom_call" | custom-call | flops 2684354560 | bytes 12320768 | tf_op jit(solution)/shard_map/while/body/expert_rows/pallas_call | solution.py:108
  85.9 2.9 %collective-permute-start.17 = (bf16[80,2048]{1,0:T(8,128)(2,1)S(1)}, bf16[80,2048]{1,0:T(8,128)(2,1)S(1)}, u32[]{:S(2)}, u32[]{:S(2)}) collective-permute-start(bf16[80,2048]{1,0:T(8,128)(2,1)S(1)} %get-tuple-element.68), channel_id=1, source_target_pairs={{0,224},{32,0},{64,32},{96,64},{128,96},{160,128},{192,160},{224,1... | collective-permute-start | bytes 983048 | tf_op jit(solution)/shard_map/while/body/ppermute | solution.py:266
  89.7 3.8 %expert_rows.7 = (bf16[80,2048]{1,0:T(8,128)(2,1)S(1)}, f32[80,2048]{1,0:T(8,128)S(1)}, f32[80,2048]{1,0:T(8,128)S(1)}, bf16[80,2048]{1,0:T(8,128)(2,1)S(1)}) custom-call(bf16[88,2048]{1,0:T(8,128)(2,1)S(1)} %collective-permute-done.10.refs_0_.refs_12_, bf16[88,2048]{1,0:T(8,128)(2,1)S(1)} %get-tuple-element.41.refs_1_.refs_8_, ...), custom_call_target="tpu_custom_call" | custom-call | flops 2684354560 | bytes 12320768 | tf_op jit(solution)/shard_map/while/body/expert_rows/pallas_call | solution.py:108
  98.0 4.6 %collective-permute-done.14 = bf16[80,2048]{1,0:T(8,128)(2,1)S(1)} collective-permute-done((bf16[80,2048]{1,0:T(8,128)(2,1)S(1)}, bf16[80,2048]{1,0:T(8,128)(2,1)S(1)}, u32[]{:S(2)}, u32[]{:S(2)}) %collective-permute-start.14) | collective-permute-done | bytes 327712 | tf_op jit(solution)/shard_map/while/body/ppermute | solution.py:265
  105.6 3.0 %collective-permute-done.21 = bf16[80,2048]{1,0:T(8,128)(2,1)S(1)} collective-permute-done((bf16[80,2048]{1,0:T(8,128)(2,1)S(1)}, bf16[80,2048]{1,0:T(8,128)(2,1)S(1)}, u32[]{:S(2)}, u32[]{:S(2)}) %collective-permute-start.21) | collective-permute-done | bytes 327712 | tf_op jit(solution)/shard_map/while/body/ppermute | solution.py:266
  109.8 6.9 %collective-permute-done.18 = bf16[80,2048]{1,0:T(8,128)(2,1)S(1)} collective-permute-done((bf16[80,2048]{1,0:T(8,128)(2,1)S(1)}, bf16[80,2048]{1,0:T(8,128)(2,1)S(1)}, u32[]{:S(2)}, u32[]{:S(2)}) %collective-permute-start.18) | collective-permute-done | bytes 327712 | tf_op jit(solution)/shard_map/while/body/ppermute | solution.py:265
  121.1 4.0 %collective-permute-done.22 = bf16[80,2048]{1,0:T(8,128)(2,1)S(1)} collective-permute-done((bf16[80,2048]{1,0:T(8,128)(2,1)S(1)}, bf16[80,2048]{1,0:T(8,128)(2,1)S(1)}, u32[]{:S(2)}, u32[]{:S(2)}) %collective-permute-start.22) | collective-permute-done | bytes 327712 | tf_op jit(solution)/shard_map/while/body/ppermute | solution.py:265
  127.8 4.3 %collective-permute-done.25.refs_4_ = bf16[80,2048]{1,0:T(8,128)(2,1)S(1)} collective-permute-done((bf16[80,2048]{1,0:T(8,128)(2,1)S(1)}, bf16[80,2048]{1,0:T(8,128)(2,1)S(1)}, u32[]{:S(2)}, u32[]{:S(2)}) %collective-permute-start.25) | collective-permute-done | bytes 327712 | tf_op jit(solution)/shard_map/while/body/ppermute | solution.py:266
  132.1 7.0 %collective-permute-done.27.refs_7_ = bf16[80,2048]{1,0:T(8,128)(2,1)S(1)} collective-permute-done((bf16[80,2048]{1,0:T(8,128)(2,1)S(1)}, bf16[80,2048]{1,0:T(8,128)(2,1)S(1)}, u32[]{:S(2)}, u32[]{:S(2)}) %collective-permute-start.27) | collective-permute-done | bytes 327712 | tf_op jit(solution)/shard_map/while/body/ppermute | solution.py:266
  142.1 24.2 %all_to_all.10 = bf16[32,8,2048]{2,1,0:T(8,128)(2,1)S(1)} all-to-all(bf16[32,8,2048]{2,1,0:T(8,128)(2,1)} %bitcast.13), channel_id=1, replica_groups=mesh['dp'=8,'expert_0'=4,'expert_1'=4,'expert_2'=2] {'expert_0','expert_..., dimensions={0} | all-to-all | bytes 2097152 | tf_op jit(solution)/shard_map/all_to_all | solution.py:346
  (66 shorter events, 34.1 us)
Async XLA Ops:
  4.6 26.2 %all-to-all-start = ((bf16[32,8,2176]{2,1,0:T(8,128)(2,1)}), bf16[32,8,2176]{2,1,0:T(8,128)(2,1)S(1)}, u32[]{:S(2)}, u32[]{:S(2)}) async-start(bf16[32,8,2176]{2,1,0:T(8,128)(2,1)} %bitcast.5), calls=%async_computation | async-start | bytes 2228224 | tf_op jit(solution)/shard_map/all_to_all | solution.py:325
  31.5 14.3 %collective-permute-start = (bf16[88,2048]{1,0:T(8,128)(2,1)S(1)}, bf16[88,2048]{1,0:T(8,128)(2,1)S(1)}, u32[]{:S(2)}, u32[]{:S(2)}) collective-permute-start(bf16[88,2048]{1,0:T(8,128)(2,1)S(1)} %get-tuple-element.41.refs_1_.refs_8_), channel_id=1, source_target_pairs={{0,32},{32,64},{64,96},{96,128},{128,160},{160,192},{192,224},{224... | collective-permute-start | bytes 1081352 | tf_op jit(solution)/shard_map/while/body/ppermute | solution.py:265
  33.2 11.0 %collective-permute-start.1 = (bf16[80,2048]{1,0:T(8,128)(2,1)S(1)}, bf16[80,2048]{1,0:T(8,128)(2,1)S(1)}, u32[]{:S(2)}, u32[]{:S(2)}) collective-permute-start(bf16[80,2048]{1,0:T(8,128)(2,1)S(1)} %get-tuple-element.42.refs_2_), channel_id=1, source_target_pairs={{0,224},{32,0},{64,32},{96,64},{128,96},{160,128},{192,160},{224,1... | collective-permute-start | bytes 983048 | tf_op jit(solution)/shard_map/while/body/ppermute | solution.py:266
  37.2 15.6 %collective-permute-start.5 = (bf16[88,2048]{1,0:T(8,128)(2,1)S(1)}, bf16[88,2048]{1,0:T(8,128)(2,1)S(1)}, u32[]{:S(2)}, u32[]{:S(2)}) collective-permute-start(bf16[88,2048]{1,0:T(8,128)(2,1)S(1)} %get-tuple-element.41.refs_1_.refs_8_), channel_id=1, source_target_pairs={{0,224},{32,0},{64,32},{96,64},{128,96},{160,128},{192,160},{224,1... | collective-permute-start | bytes 1081352 | tf_op jit(solution)/shard_map/while/body/ppermute | solution.py:266
  38.6 14.2 %collective-permute-start.4 = (bf16[80,2048]{1,0:T(8,128)(2,1)S(1)}, bf16[80,2048]{1,0:T(8,128)(2,1)S(1)}, u32[]{:S(2)}, u32[]{:S(2)}) collective-permute-start(bf16[80,2048]{1,0:T(8,128)(2,1)S(1)} %get-tuple-element.42.refs_2_), channel_id=1, source_target_pairs={{0,32},{32,64},{64,96},{96,128},{128,160},{160,192},{192,224},{224... | collective-permute-start | bytes 983048 | tf_op jit(solution)/shard_map/while/body/ppermute | solution.py:265
  45.8 15.7 %collective-permute-start.2 = (bf16[88,2048]{1,0:T(8,128)(2,1)S(1)}, bf16[88,2048]{1,0:T(8,128)(2,1)S(1)}, u32[]{:S(2)}, u32[]{:S(2)}) collective-permute-start(bf16[88,2048]{1,0:T(8,128)(2,1)S(1)} %collective-permute-done.refs_0_.refs_15_), channel_id=1, source_target_pairs={{0,32},{32,64},{64,96},{96,128},{128,160},{160,192},{192,224},{224... | collective-permute-start | bytes 1081352 | tf_op jit(solution)/shard_map/while/body/ppermute | solution.py:265
  45.8 15.7 %collective-permute-start.3 = (bf16[80,2048]{1,0:T(8,128)(2,1)S(1)}, bf16[80,2048]{1,0:T(8,128)(2,1)S(1)}, u32[]{:S(2)}, u32[]{:S(2)}) collective-permute-start(bf16[80,2048]{1,0:T(8,128)(2,1)S(1)} %collective-permute-done.1.refs_3_), channel_id=1, source_target_pairs={{0,224},{32,0},{64,32},{96,64},{128,96},{160,128},{192,160},{224,1... | collective-permute-start | bytes 983048 | tf_op jit(solution)/shard_map/while/body/ppermute | solution.py:266
  52.9 14.4 %collective-permute-start.9 = (bf16[88,2048]{1,0:T(8,128)(2,1)S(1)}, bf16[88,2048]{1,0:T(8,128)(2,1)S(1)}, u32[]{:S(2)}, u32[]{:S(2)}) collective-permute-start(bf16[88,2048]{1,0:T(8,128)(2,1)S(1)} %collective-permute-done.5.refs_2_.refs_9_), channel_id=1, source_target_pairs={{0,224},{32,0},{64,32},{96,64},{128,96},{160,128},{192,160},{224,1... | collective-permute-start | bytes 1081352 | tf_op jit(solution)/shard_map/while/body/ppermute | solution.py:266
  55.3 11.9 %collective-permute-start.8 = (bf16[80,2048]{1,0:T(8,128)(2,1)S(1)}, bf16[80,2048]{1,0:T(8,128)(2,1)S(1)}, u32[]{:S(2)}, u32[]{:S(2)}) collective-permute-start(bf16[80,2048]{1,0:T(8,128)(2,1)S(1)} %collective-permute-done.4.refs_1_), channel_id=1, source_target_pairs={{0,32},{32,64},{64,96},{96,128},{128,160},{160,192},{192,224},{224... | collective-permute-start | bytes 983048 | tf_op jit(solution)/shard_map/while/body/ppermute | solution.py:265
  61.5 13.4 %collective-permute-start.6 = (bf16[88,2048]{1,0:T(8,128)(2,1)S(1)}, bf16[88,2048]{1,0:T(8,128)(2,1)S(1)}, u32[]{:S(2)}, u32[]{:S(2)}) collective-permute-start(bf16[88,2048]{1,0:T(8,128)(2,1)S(1)} %collective-permute-done.2.refs_0_.refs_14_), channel_id=1, source_target_pairs={{0,32},{32,64},{64,96},{96,128},{128,160},{160,192},{192,224},{224... | collective-permute-start | bytes 1081352 | tf_op jit(solution)/shard_map/while/body/ppermute | solution.py:265
  61.6 12.3 %collective-permute-start.7 = (bf16[80,2048]{1,0:T(8,128)(2,1)S(1)}, bf16[80,2048]{1,0:T(8,128)(2,1)S(1)}, u32[]{:S(2)}, u32[]{:S(2)}) collective-permute-start(bf16[80,2048]{1,0:T(8,128)(2,1)S(1)} %collective-permute-done.3.refs_3_), channel_id=1, source_target_pairs={{0,224},{32,0},{64,32},{96,64},{128,96},{160,128},{192,160},{224,1... | collective-permute-start | bytes 983048 | tf_op jit(solution)/shard_map/while/body/ppermute | solution.py:266
  67.2 14.7 %collective-permute-start.13 = (bf16[88,2048]{1,0:T(8,128)(2,1)S(1)}, bf16[88,2048]{1,0:T(8,128)(2,1)S(1)}, u32[]{:S(2)}, u32[]{:S(2)}) collective-permute-start(bf16[88,2048]{1,0:T(8,128)(2,1)S(1)} %collective-permute-done.9.refs_2_.refs_10_), channel_id=1, source_target_pairs={{0,224},{32,0},{64,32},{96,64},{128,96},{160,128},{192,160},{224,1... | collective-permute-start | bytes 1081352 | tf_op jit(solution)/shard_map/while/body/ppermute | solution.py:266
  70.1 11.9 %collective-permute-start.12 = (bf16[80,2048]{1,0:T(8,128)(2,1)S(1)}, bf16[80,2048]{1,0:T(8,128)(2,1)S(1)}, u32[]{:S(2)}, u32[]{:S(2)}) collective-permute-start(bf16[80,2048]{1,0:T(8,128)(2,1)S(1)} %collective-permute-done.8.refs_1_), channel_id=1, source_target_pairs={{0,32},{32,64},{64,96},{96,128},{128,160},{160,192},{192,224},{224... | collective-permute-start | bytes 983048 | tf_op jit(solution)/shard_map/while/body/ppermute | solution.py:265
  75.0 14.7 %collective-permute-start.10 = (bf16[88,2048]{1,0:T(8,128)(2,1)S(1)}, bf16[88,2048]{1,0:T(8,128)(2,1)S(1)}, u32[]{:S(2)}, u32[]{:S(2)}) collective-permute-start(bf16[88,2048]{1,0:T(8,128)(2,1)S(1)} %collective-permute-done.6.refs_0_.refs_13_), channel_id=1, source_target_pairs={{0,32},{32,64},{64,96},{96,128},{128,160},{160,192},{192,224},{224... | collective-permute-start | bytes 1081352 | tf_op jit(solution)/shard_map/while/body/ppermute | solution.py:265
  75.0 13.9 %collective-permute-start.11 = (bf16[80,2048]{1,0:T(8,128)(2,1)S(1)}, bf16[80,2048]{1,0:T(8,128)(2,1)S(1)}, u32[]{:S(2)}, u32[]{:S(2)}) collective-permute-start(bf16[80,2048]{1,0:T(8,128)(2,1)S(1)} %collective-permute-done.7.refs_3_), channel_id=1, source_target_pairs={{0,224},{32,0},{64,32},{96,64},{128,96},{160,128},{192,160},{224,1... | collective-permute-start | bytes 983048 | tf_op jit(solution)/shard_map/while/body/ppermute | solution.py:266
  85.8 10.5 %collective-permute-start.16 = (bf16[80,2048]{1,0:T(8,128)(2,1)S(1)}, bf16[80,2048]{1,0:T(8,128)(2,1)S(1)}, u32[]{:S(2)}, u32[]{:S(2)}) collective-permute-start(bf16[80,2048]{1,0:T(8,128)(2,1)S(1)} %get-tuple-element.67), channel_id=1, source_target_pairs={{0,32},{32,64},{64,96},{96,128},{128,160},{160,192},{192,224},{224... | collective-permute-start | bytes 983048 | tf_op jit(solution)/shard_map/while/body/ppermute | solution.py:265
  96.4 12.3 %collective-permute-start.21 = (bf16[80,2048]{1,0:T(8,128)(2,1)S(1)}, bf16[80,2048]{1,0:T(8,128)(2,1)S(1)}, u32[]{:S(2)}, u32[]{:S(2)}) collective-permute-start(bf16[80,2048]{1,0:T(8,128)(2,1)S(1)} %add_convert_fusion.8), channel_id=1, source_target_pairs={{0,224},{32,0},{64,32},{96,64},{128,96},{160,128},{192,160},{224,1... | collective-permute-start | bytes 983048 | tf_op jit(solution)/shard_map/while/body/ppermute | solution.py:266
  97.8 11.9 %collective-permute-start.20 = (bf16[80,2048]{1,0:T(8,128)(2,1)S(1)}, bf16[80,2048]{1,0:T(8,128)(2,1)S(1)}, u32[]{:S(2)}, u32[]{:S(2)}) collective-permute-start(bf16[80,2048]{1,0:T(8,128)(2,1)S(1)} %add_convert_fusion.9), channel_id=1, source_target_pairs={{0,32},{32,64},{64,96},{96,128},{128,160},{160,192},{192,224},{224... | collective-permute-start | bytes 983048 | tf_op jit(solution)/shard_map/while/body/ppermute | solution.py:265
  102.7 14.0 %collective-permute-start.18 = (bf16[80,2048]{1,0:T(8,128)(2,1)S(1)}, bf16[80,2048]{1,0:T(8,128)(2,1)S(1)}, u32[]{:S(2)}, u32[]{:S(2)}) collective-permute-start(bf16[80,2048]{1,0:T(8,128)(2,1)S(1)} %add_convert_fusion.7), channel_id=1, source_target_pairs={{0,32},{32,64},{64,96},{96,128},{128,160},{160,192},{192,224},{224... | collective-permute-start | bytes 983048 | tf_op jit(solution)/shard_map/while/body/ppermute | solution.py:265
  104.3 12.4 %collective-permute-start.19 = (bf16[80,2048]{1,0:T(8,128)(2,1)S(1)}, bf16[80,2048]{1,0:T(8,128)(2,1)S(1)}, u32[]{:S(2)}, u32[]{:S(2)}) collective-permute-start(bf16[80,2048]{1,0:T(8,128)(2,1)S(1)} %add_convert_fusion.6), channel_id=1, source_target_pairs={{0,224},{32,0},{64,32},{96,64},{128,96},{160,128},{192,160},{224,1... | collective-permute-start | bytes 983048 | tf_op jit(solution)/shard_map/while/body/ppermute | solution.py:266
  119.6 12.5 %collective-permute-start.25 = (bf16[80,2048]{1,0:T(8,128)(2,1)S(1)}, bf16[80,2048]{1,0:T(8,128)(2,1)S(1)}, u32[]{:S(2)}, u32[]{:S(2)}) collective-permute-start(bf16[80,2048]{1,0:T(8,128)(2,1)S(1)} %add_convert_fusion.4), channel_id=1, source_target_pairs={{0,224},{32,0},{64,32},{96,64},{128,96},{160,128},{192,160},{224,1... | collective-permute-start | bytes 983048 | tf_op jit(solution)/shard_map/while/body/ppermute | solution.py:266
  120.8 11.4 %collective-permute-start.26 = (bf16[80,2048]{1,0:T(8,128)(2,1)S(1)}, bf16[80,2048]{1,0:T(8,128)(2,1)S(1)}, u32[]{:S(2)}, u32[]{:S(2)}) collective-permute-start(bf16[80,2048]{1,0:T(8,128)(2,1)S(1)} %add_convert_fusion.5), channel_id=1, source_target_pairs={{0,32},{32,64},{64,96},{96,128},{128,160},{160,192},{192,224},{224... | collective-permute-start | bytes 983048 | tf_op jit(solution)/shard_map/while/body/ppermute | solution.py:265
  125.2 13.9 %collective-permute-start.27 = (bf16[80,2048]{1,0:T(8,128)(2,1)S(1)}, bf16[80,2048]{1,0:T(8,128)(2,1)S(1)}, u32[]{:S(2)}, u32[]{:S(2)}) collective-permute-start(bf16[80,2048]{1,0:T(8,128)(2,1)S(1)} %add_convert_fusion), channel_id=1, source_target_pairs={{0,224},{32,0},{64,32},{96,64},{128,96},{160,128},{192,160},{224,1... | collective-permute-start | bytes 983048 | tf_op jit(solution)/shard_map/while/body/ppermute | solution.py:266
  127.7 11.4 %collective-permute-start.24 = (bf16[80,2048]{1,0:T(8,128)(2,1)S(1)}, bf16[80,2048]{1,0:T(8,128)(2,1)S(1)}, u32[]{:S(2)}, u32[]{:S(2)}) collective-permute-start(bf16[80,2048]{1,0:T(8,128)(2,1)S(1)} %add_convert_fusion.1), channel_id=1, source_target_pairs={{0,32},{32,64},{64,96},{96,128},{128,160},{160,192},{192,224},{224... | collective-permute-start | bytes 983048 | tf_op jit(solution)/shard_map/while/body/ppermute | solution.py:265
  (9 other events, 204.5 us)

commit v7 on v6

--- a/solution.py
+++ b/solution.py
@@ -123,7 +123,11 @@
 def pack_kernel(tokens_ref, ranks_ref, capacity_ref, packed_ref, table_ref, blank_ref):
     experts, count = ranks_ref.shape
     width = tokens_ref.shape[1]
-    chosen = ranks_ref[...] < capacity_ref[...]
+    square = (experts, experts)
+    diagonal = lax.broadcasted_iota(jnp.int32, square, 0) == lax.broadcasted_iota(jnp.int32, square, 1)
+    limits = jnp.broadcast_to(capacity_ref[...].astype(jnp.float32), square)
+    limits = jnp.sum(jnp.where(diagonal, limits, 0.0), axis=1, keepdims=True)
+    chosen = ranks_ref[...].astype(jnp.float32) < limits
     earlier = lax.broadcasted_iota(jnp.int32, (count, count), 0) < lax.broadcasted_iota(
         jnp.int32, (count, count), 1
     )
@@ -156,7 +160,7 @@
         ],
         compiler_params=pltpu.CompilerParams(vmem_limit_bytes=VMEM_LIMIT),
         name="pack",
-    )(tokens, expert_ranks, capacity[:, None])
+    )(tokens, expert_ranks, capacity[None, :])
 
 
 def place_kernel(arrived_ref, step_ref, gates_ref, top_ref, bottom_ref, here_ref):
@@ -276,7 +280,8 @@
     notes = {0: top}
     firsts = hop(top, bottom)
     seconds = hop(bottom, top)
-    outs, done = {}, ()
+    *own, first_weight, second_weight = mlp(top, bottom, staged=True)
+    below, above, done = {}, {}, own
     for k in range(1, far):
         firsts = after(firsts, *done)
         seconds = after(seconds, *firsts)
@@ -284,31 +289,31 @@
         next_firsts = hop(*firsts)
         if k < far - 1:
             next_seconds = hop(*seconds)
-        pieces = firsts[0], seconds[0], seconds[1], firsts[1]
-        outs[k] = mlp(*pieces, sent=(0, 3) if k == far - 1 else (), staged=k == 1)
-        if k == 1:
-            *outs[k], first_weight, second_weight = outs[k]
-        done = tuple(outs[k])
-        firsts, seconds = next_firsts, next_seconds
-
-    below_top, below_bottom, above_top, above_bottom = outs[far - 1]
-    seconds = hop(above_bottom, below_top)
-    firsts = after(firsts, above_bottom, below_top, *done)
+            done = mlp(firsts[0], seconds[0], seconds[1], firsts[1])
+            below[k], above[k] = done[:2], done[2:]
+            seconds = next_seconds
+        else:
+            below_top, above_bottom = mlp(*firsts, sent=(0, 1))
+            seconds_back = hop(above_bottom, below_top)
+            seconds = after(seconds, above_bottom, below_top)
+            below_bottom, above_top = mlp(*seconds)
+            below[k], above[k] = (below_top, below_bottom), (above_top, above_bottom)
+        firsts = next_firsts
+
+    firsts = after(firsts, below_bottom, above_top)
     notes[far] = firsts[0]
-    last = mlp(firsts[0], top, bottom, firsts[1], sent=(0, 3))
-    sends = last[0], last[3]
+    sends = tuple(mlp(*firsts, sent=(0, 1)))
+    seconds = seconds_back
     firsts = hop(*sends)
     for k in range(far - 1, 0, -1):
         if k > 1:
-            below_top, _, _, above_bottom = outs[k - 1]
             seconds = after(seconds, *sends)
-            sends = narrow(wide(seconds[0]) + above_bottom), narrow(wide(seconds[1]) + below_top)
+            sends = narrow(wide(seconds[0]) + above[k - 1][1]), narrow(wide(seconds[1]) + below[k - 1][0])
             seconds = hop(*sends)
-        _, below_bottom, above_top, _ = outs[k]
         firsts = after(firsts, *sends)
-        sends = narrow(wide(firsts[0]) + above_top), narrow(wide(firsts[1]) + below_bottom)
+        sends = narrow(wide(firsts[0]) + above[k][0]), narrow(wide(firsts[1]) + below[k][1])
         firsts = hop(*sends)
-    parts = last[1], firsts[0], seconds[1], last[2], seconds[0], firsts[1]
+    parts = own[0], firsts[0], seconds[1], own[1], seconds[0], firsts[1]
     return parts, [notes[j] for j in range(dp_count)]
 
 

time: 168 us -> 172 us (1.024)
  Pallas kernels: 21.8 us -> 25.9 us
  waiting for transfers between devices: 68.5 us -> 70.4 us
    ppermute x14, waiting for transfers between devices: 31.7 us -> 39.3 us  [hop(): up_rows = lax.ppermute(up_rows, 'dp', upward)]
    ppermute x14, waiting for transfers between devices: 19.8 us -> 14.1 us  [hop(): down_rows = lax.ppermute(down_rows, 'dp', downward)]
    pallas_call x4 -> x6, Pallas kernels: 17.6 us -> 20.3 us  [expert_rows(): pl.pallas_call(staged_expert_kernel if staged else expert_kernel, out_sha...]
    ppermute x14, starting transfers between devices: 5.54 us -> 3.34 us  [hop(): up_rows = lax.ppermute(up_rows, 'dp', upward)]
  transfers between devices with their start and end apart: 29 -> 29, of which waited for: 15 -> 20; matrix products, arithmetic and copies ran while one was open for 1% -> 1% of each run, Pallas kernels for 10% -> 12%
where the time goes in v7:
time: 172 us; the launch traced here: 171 us
  waiting for transfers between devices  70.4 us (41%)
  starting transfers between devices  44.8 us (26%)
  Pallas kernels  25.9 us (15%)
  blocking collectives  23.3 us (14%)
  local copies, waits for them, and re-layouts  2.75 us (2%)
    ppermute x14, waiting for transfers between devices, hop(): up_rows = lax.ppermute(up_rows, 'dp', upward)  39.3 us
    ppermute x14, starting transfers between devices, hop(): down_rows = lax.ppermute(down_rows, 'dp', downward)  32.8 us
    all_to_all x1, blocking collectives, on_device(): lax.all_to_all(sent_back.reshape(expert_count, MOST, width), EXPERT, spli...  23.3 us
    pallas_call x6, Pallas kernels, expert_rows(): pl.pallas_call(staged_expert_kernel if staged else expert_kernel, out_sha...  20.3 us
    all_to_all x1, waiting for transfers between devices, on_device(): lax.all_to_all(packed.reshape(expert_count, MOST, width + LANES), EXPERT,...  17 us
    ppermute x14, waiting for transfers between devices, hop(): down_rows = lax.ppermute(down_rows, 'dp', downward)  14.1 us
    all_to_all x1, starting transfers between devices, on_device(): lax.all_to_all(packed.reshape(expert_count, MOST, width + LANES), EXPERT,...  8.63 us
  transfers between devices with their start and end apart: 29, of which 20 were waited for; matrix products, arithmetic and copies ran while one was open for 1% of the time, Pallas kernels for 12%

profile of v7, /device:TPU:1, one launch (start us, length us, event | category | flops | bytes accessed | tf_op | source)
XLA Modules:
  0.0 171.3 jit_solution(4048751106234373215)
XLA Ops:
  4.7 8.6 %all-to-all-start = ((bf16[32,8,2176]{2,1,0:T(8,128)(2,1)}), bf16[32,8,2176]{2,1,0:T(8,128)(2,1)}, u32[]{:S(2)}, u32[]{:S(2)}) async-start(bf16[32,8,2176]{2,1,0:T(8,128)(2,1)} %bitcast.5), calls=%async_computation | async-start | bytes 2228224 | tf_op jit(solution)/shard_map/all_to_all | solution.py:330
  14.0 17.0 %all-to-all-done = bf16[32,8,2176]{2,1,0:T(8,128)(2,1)} async-done(((bf16[32,8,2176]{2,1,0:T(8,128)(2,1)}), bf16[32,8,2176]{2,1,0:T(8,128)(2,1)}, u32[]{:S(2)}, u32[]{:S(2)}) %all-to-all-start) | async-done | bytes 1114144 | tf_op jit(solution)/shard_map/all_to_all | solution.py:330
  31.0 115.6 %while.11 = (s32[1]{0:T(128)}, s32[1]{0:T(128)}, bf16[256,2048]{1,0:T(8,128)(2,1)}, s32[]{:T(128)}, bf16[256,2176]{1,0:T(8,128)(2,1)}, /*index=5*/f32[1,384]{1,0...) while((s32[1]{0:T(128)}, s32[1]{0:T(128)}, bf16[256,2048]{1,0:T(8,128)(2,1)}, s32[]{:T(128)}, ...), condition=%region_1.0_spmd, body=%region_0.0_spmd | while | flops 10742333440 | bytes 123077856 | solution.py:346
  34.6 4.0 %collective-permute-start.1 = (bf16[80,2048]{1,0:T(8,128)(2,1)S(1)}, bf16[80,2048]{1,0:T(8,128)(2,1)S(1)}, u32[]{:S(2)}, u32[]{:S(2)}) collective-permute-start(bf16[80,2048]{1,0:T(8,128)(2,1)S(1)} %get-tuple-element.42.refs_1_), channel_id=1, source_target_pairs={{0,224},{32,0},{64,32},{96,64},{128,96},{160,128},{192,160},{224,1... | collective-permute-start | bytes 983048 | tf_op jit(solution)/shard_map/while/body/ppermute | solution.py:270
  40.1 5.2 %expert_rows.6 = (f32[80,2048]{1,0:T(8,128)S(1)}, f32[80,2048]{1,0:T(8,128)S(1)}, bf16[2048,1024]{1,0:T(8,128)(2,1)S(1)}, bf16[1024,2048]{1,0:T(8,128)(2,1)S(1)}) custom-call(bf16[88,2048]{1,0:T(8,128)(2,1)S(1)} %get-tuple-element.41.refs_0_.refs_8_, bf16[80,2048]{1,0:T(8,128)(2,1)S(1)} %get-tuple-element.42.refs_1_, bf16[2048,1024]{1,0:T(8,128)(2,1)} %bitcast.13, ...), custom_call_target="tpu_custom_call" | custom-call | flops 1342177280 | bytes 10354688 | tf_op jit(solution)/shard_map/while/body/expert_rows/pallas_call | solution.py:108
  47.3 2.7 %collective-permute-start.3 = (bf16[80,2048]{1,0:T(8,128)(2,1)S(1)}, bf16[80,2048]{1,0:T(8,128)(2,1)S(1)}, u32[]{:S(2)}, u32[]{:S(2)}) collective-permute-start(bf16[80,2048]{1,0:T(8,128)(2,1)S(1)} %collective-permute-done.1.refs_3_), channel_id=1, source_target_pairs={{0,224},{32,0},{64,32},{96,64},{128,96},{160,128},{192,160},{224,1... | collective-permute-start | bytes 983048 | tf_op jit(solution)/shard_map/while/body/ppermute | solution.py:270
  49.9 4.3 %collective-permute-done.4.refs_1_ = bf16[80,2048]{1,0:T(8,128)(2,1)S(1)} collective-permute-done((bf16[80,2048]{1,0:T(8,128)(2,1)S(1)}, bf16[80,2048]{1,0:T(8,128)(2,1)S(1)}, u32[]{:S(2)}, u32[]{:S(2)}) %collective-permute-start.4) | collective-permute-done | bytes 327712 | tf_op jit(solution)/shard_map/while/body/ppermute | solution.py:269
  54.3 2.7 %collective-permute-start.9 = (bf16[88,2048]{1,0:T(8,128)(2,1)S(1)}, bf16[88,2048]{1,0:T(8,128)(2,1)S(1)}, u32[]{:S(2)}, u32[]{:S(2)}) collective-permute-start(bf16[88,2048]{1,0:T(8,128)(2,1)S(1)} %collective-permute-done.5.refs_2_.refs_9_), channel_id=1, source_target_pairs={{0,224},{32,0},{64,32},{96,64},{128,96},{160,128},{192,160},{224,1... | collective-permute-start | bytes 1081352 | tf_op jit(solution)/shard_map/while/body/ppermute | solution.py:270
  57.0 3.8 %expert_rows.7 = (f32[80,2048]{1,0:T(8,128)S(1)}, f32[80,2048]{1,0:T(8,128)S(1)}, f32[80,2048]{1,0:T(8,128)S(1)}, f32[80,2048]{1,0:T(8,128)S(1)}) custom-call(bf16[88,2048]{1,0:T(8,128)(2,1)S(1)} %collective-permute-done.refs_0_.refs_15_, bf16[80,2048]{1,0:T(8,128)(2,1)S(1)} %collective-permute-done.4.refs_1_, ...), custom_call_target="tpu_custom_call" | custom-call | flops 2684354560 | bytes 12320768 | tf_op jit(solution)/shard_map/while/body/expert_rows/pallas_call | solution.py:108
  64.7 4.3 %collective-permute-done.8.refs_1_ = bf16[80,2048]{1,0:T(8,128)(2,1)S(1)} collective-permute-done((bf16[80,2048]{1,0:T(8,128)(2,1)S(1)}, bf16[80,2048]{1,0:T(8,128)(2,1)S(1)}, u32[]{:S(2)}, u32[]{:S(2)}) %collective-permute-start.8) | collective-permute-done | bytes 327712 | tf_op jit(solution)/shard_map/while/body/ppermute | solution.py:269
  69.0 2.7 %collective-permute-start.13 = (bf16[88,2048]{1,0:T(8,128)(2,1)S(1)}, bf16[88,2048]{1,0:T(8,128)(2,1)S(1)}, u32[]{:S(2)}, u32[]{:S(2)}) collective-permute-start(bf16[88,2048]{1,0:T(8,128)(2,1)S(1)} %collective-permute-done.9.refs_2_.refs_10_), channel_id=1, source_target_pairs={{0,224},{32,0},{64,32},{96,64},{128,96},{160,128},{192,160},{224,1... | collective-permute-start | bytes 1081352 | tf_op jit(solution)/shard_map/while/body/ppermute | solution.py:270
  71.7 3.8 %expert_rows.8 = (f32[80,2048]{1,0:T(8,128)S(1)}, f32[80,2048]{1,0:T(8,128)S(1)}, f32[80,2048]{1,0:T(8,128)S(1)}, f32[80,2048]{1,0:T(8,128)S(1)}) custom-call(bf16[88,2048]{1,0:T(8,128)(2,1)S(1)} %collective-permute-done.2.refs_0_.refs_14_, bf16[80,2048]{1,0:T(8,128)(2,1)S(1)} %collective-permute-done.8.refs_1_, ...), custom_call_target="tpu_custom_call" | custom-call | flops 2684354560 | bytes 12320768 | tf_op jit(solution)/shard_map/while/body/expert_rows/pallas_call | solution.py:108
  98.8 2.7 %collective-permute-start.21 = (bf16[80,2048]{1,0:T(8,128)(2,1)S(1)}, bf16[80,2048]{1,0:T(8,128)(2,1)S(1)}, u32[]{:S(2)}, u32[]{:S(2)}) collective-permute-start(bf16[80,2048]{1,0:T(8,128)(2,1)S(1)} %add_convert_fusion.8), channel_id=1, source_target_pairs={{0,224},{32,0},{64,32},{96,64},{128,96},{160,128},{192,160},{224,1... | collective-permute-start | bytes 983048 | tf_op jit(solution)/shard_map/while/body/ppermute | solution.py:270
  101.5 3.7 %collective-permute-done.14 = bf16[80,2048]{1,0:T(8,128)(2,1)S(1)} collective-permute-done((bf16[80,2048]{1,0:T(8,128)(2,1)S(1)}, bf16[80,2048]{1,0:T(8,128)(2,1)S(1)}, u32[]{:S(2)}, u32[]{:S(2)}) %collective-permute-start.14) | collective-permute-done | bytes 327712 | tf_op jit(solution)/shard_map/while/body/ppermute | solution.py:269
  107.0 5.2 %collective-permute-done.20 = bf16[80,2048]{1,0:T(8,128)(2,1)S(1)} collective-permute-done((bf16[80,2048]{1,0:T(8,128)(2,1)S(1)}, bf16[80,2048]{1,0:T(8,128)(2,1)S(1)}, u32[]{:S(2)}, u32[]{:S(2)}) %collective-permute-start.20) | collective-permute-done | bytes 327712 | tf_op jit(solution)/shard_map/while/body/ppermute | solution.py:269
  112.4 4.6 %collective-permute-done.19 = bf16[80,2048]{1,0:T(8,128)(2,1)S(1)} collective-permute-done((bf16[80,2048]{1,0:T(8,128)(2,1)S(1)}, bf16[80,2048]{1,0:T(8,128)(2,1)S(1)}, u32[]{:S(2)}, u32[]{:S(2)}) %collective-permute-start.19) | collective-permute-done | bytes 327712 | tf_op jit(solution)/shard_map/while/body/ppermute | solution.py:270
  118.1 2.9 %collective-permute-start.23 = (bf16[80,2048]{1,0:T(8,128)(2,1)S(1)}, bf16[80,2048]{1,0:T(8,128)(2,1)S(1)}, u32[]{:S(2)}, u32[]{:S(2)}) collective-permute-start(bf16[80,2048]{1,0:T(8,128)(2,1)S(1)} %add_convert_fusion.2), channel_id=1, source_target_pairs={{0,224},{32,0},{64,32},{96,64},{128,96},{160,128},{192,160},{224,1... | collective-permute-start | bytes 983048 | tf_op jit(solution)/shard_map/while/body/ppermute | solution.py:270
  121.0 2.7 %collective-permute-start.25 = (bf16[80,2048]{1,0:T(8,128)(2,1)S(1)}, bf16[80,2048]{1,0:T(8,128)(2,1)S(1)}, u32[]{:S(2)}, u32[]{:S(2)}) collective-permute-start(bf16[80,2048]{1,0:T(8,128)(2,1)S(1)} %add_convert_fusion.4), channel_id=1, source_target_pairs={{0,224},{32,0},{64,32},{96,64},{128,96},{160,128},{192,160},{224,1... | collective-permute-start | bytes 983048 | tf_op jit(solution)/shard_map/while/body/ppermute | solution.py:270
  123.7 2.8 %collective-permute-done.23 = bf16[80,2048]{1,0:T(8,128)(2,1)S(1)} collective-permute-done((bf16[80,2048]{1,0:T(8,128)(2,1)S(1)}, bf16[80,2048]{1,0:T(8,128)(2,1)S(1)}, u32[]{:S(2)}, u32[]{:S(2)}) %collective-permute-start.23) | collective-permute-done | bytes 327712 | tf_op jit(solution)/shard_map/while/body/ppermute | solution.py:270
  126.5 3.1 %collective-permute-done.22 = bf16[80,2048]{1,0:T(8,128)(2,1)S(1)} collective-permute-done((bf16[80,2048]{1,0:T(8,128)(2,1)S(1)}, bf16[80,2048]{1,0:T(8,128)(2,1)S(1)}, u32[]{:S(2)}, u32[]{:S(2)}) %collective-permute-start.22) | collective-permute-done | bytes 327712 | tf_op jit(solution)/shard_map/while/body/ppermute | solution.py:269
  131.4 5.2 %collective-permute-done.26.refs_6_ = bf16[80,2048]{1,0:T(8,128)(2,1)S(1)} collective-permute-done((bf16[80,2048]{1,0:T(8,128)(2,1)S(1)}, bf16[80,2048]{1,0:T(8,128)(2,1)S(1)}, u32[]{:S(2)}, u32[]{:S(2)}) %collective-permute-start.26) | collective-permute-done | bytes 327712 | tf_op jit(solution)/shard_map/while/body/ppermute | solution.py:269
  136.6 3.9 %collective-permute-done.27.refs_7_ = bf16[80,2048]{1,0:T(8,128)(2,1)S(1)} collective-permute-done((bf16[80,2048]{1,0:T(8,128)(2,1)S(1)}, bf16[80,2048]{1,0:T(8,128)(2,1)S(1)}, u32[]{:S(2)}, u32[]{:S(2)}) %collective-permute-start.27) | collective-permute-done | bytes 327712 | tf_op jit(solution)/shard_map/while/body/ppermute | solution.py:270
  140.5 3.1 %collective-permute-done.24.refs_3_ = bf16[80,2048]{1,0:T(8,128)(2,1)S(1)} collective-permute-done((bf16[80,2048]{1,0:T(8,128)(2,1)S(1)}, bf16[80,2048]{1,0:T(8,128)(2,1)S(1)}, u32[]{:S(2)}, u32[]{:S(2)}) %collective-permute-start.24) | collective-permute-done | bytes 327712 | tf_op jit(solution)/shard_map/while/body/ppermute | solution.py:269
  146.6 23.3 %all_to_all.10 = bf16[32,8,2048]{2,1,0:T(8,128)(2,1)S(1)} all-to-all(bf16[32,8,2048]{2,1,0:T(8,128)(2,1)} %bitcast.15), channel_id=1, replica_groups=mesh['dp'=8,'expert_0'=4,'expert_1'=4,'expert_2'=2] {'expert_0','expert_..., dimensions={0} | all-to-all | bytes 2097152 | tf_op jit(solution)/shard_map/all_to_all | solution.py:351
  (69 shorter events, 47.2 us)
Async XLA Ops:
  4.7 26.3 %all-to-all-start = ((bf16[32,8,2176]{2,1,0:T(8,128)(2,1)}), bf16[32,8,2176]{2,1,0:T(8,128)(2,1)}, u32[]{:S(2)}, u32[]{:S(2)}) async-start(bf16[32,8,2176]{2,1,0:T(8,128)(2,1)} %bitcast.5), calls=%async_computation | async-start | bytes 2228224 | tf_op jit(solution)/shard_map/all_to_all | solution.py:330
  32.9 14.3 %collective-permute-start = (bf16[88,2048]{1,0:T(8,128)(2,1)S(1)}, bf16[88,2048]{1,0:T(8,128)(2,1)S(1)}, u32[]{:S(2)}, u32[]{:S(2)}) collective-permute-start(bf16[88,2048]{1,0:T(8,128)(2,1)S(1)} %get-tuple-element.41.refs_0_.refs_8_), channel_id=1, source_target_pairs={{0,32},{32,64},{64,96},{96,128},{128,160},{160,192},{192,224},{224... | collective-permute-start | bytes 1081352 | tf_op jit(solution)/shard_map/while/body/ppermute | solution.py:269
  38.7 15.6 %collective-permute-start.5 = (bf16[88,2048]{1,0:T(8,128)(2,1)S(1)}, bf16[88,2048]{1,0:T(8,128)(2,1)S(1)}, u32[]{:S(2)}, u32[]{:S(2)}) collective-permute-start(bf16[88,2048]{1,0:T(8,128)(2,1)S(1)} %get-tuple-element.41.refs_0_.refs_8_), channel_id=1, source_target_pairs={{0,224},{32,0},{64,32},{96,64},{128,96},{160,128},{192,160},{224,1... | collective-permute-start | bytes 1081352 | tf_op jit(solution)/shard_map/while/body/ppermute | solution.py:270
  40.0 14.2 %collective-permute-start.4 = (bf16[80,2048]{1,0:T(8,128)(2,1)S(1)}, bf16[80,2048]{1,0:T(8,128)(2,1)S(1)}, u32[]{:S(2)}, u32[]{:S(2)}) collective-permute-start(bf16[80,2048]{1,0:T(8,128)(2,1)S(1)} %get-tuple-element.42.refs_1_), channel_id=1, source_target_pairs={{0,32},{32,64},{64,96},{96,128},{128,160},{160,192},{192,224},{224... | collective-permute-start | bytes 983048 | tf_op jit(solution)/shard_map/while/body/ppermute | solution.py:269
  47.3 14.7 %collective-permute-start.2 = (bf16[88,2048]{1,0:T(8,128)(2,1)S(1)}, bf16[88,2048]{1,0:T(8,128)(2,1)S(1)}, u32[]{:S(2)}, u32[]{:S(2)}) collective-permute-start(bf16[88,2048]{1,0:T(8,128)(2,1)S(1)} %collective-permute-done.refs_0_.refs_15_), channel_id=1, source_target_pairs={{0,32},{32,64},{64,96},{96,128},{128,160},{160,192},{192,224},{224... | collective-permute-start | bytes 1081352 | tf_op jit(solution)/shard_map/while/body/ppermute | solution.py:269
  47.3 13.5 %collective-permute-start.3 = (bf16[80,2048]{1,0:T(8,128)(2,1)S(1)}, bf16[80,2048]{1,0:T(8,128)(2,1)S(1)}, u32[]{:S(2)}, u32[]{:S(2)}) collective-permute-start(bf16[80,2048]{1,0:T(8,128)(2,1)S(1)} %collective-permute-done.1.refs_3_), channel_id=1, source_target_pairs={{0,224},{32,0},{64,32},{96,64},{128,96},{160,128},{192,160},{224,1... | collective-permute-start | bytes 983048 | tf_op jit(solution)/shard_map/while/body/ppermute | solution.py:270
  54.3 14.7 %collective-permute-start.8 = (bf16[80,2048]{1,0:T(8,128)(2,1)S(1)}, bf16[80,2048]{1,0:T(8,128)(2,1)S(1)}, u32[]{:S(2)}, u32[]{:S(2)}) collective-permute-start(bf16[80,2048]{1,0:T(8,128)(2,1)S(1)} %collective-permute-done.4.refs_1_), channel_id=1, source_target_pairs={{0,32},{32,64},{64,96},{96,128},{128,160},{160,192},{192,224},{224... | collective-permute-start | bytes 983048 | tf_op jit(solution)/shard_map/while/body/ppermute | solution.py:269
  54.3 14.7 %collective-permute-start.9 = (bf16[88,2048]{1,0:T(8,128)(2,1)S(1)}, bf16[88,2048]{1,0:T(8,128)(2,1)S(1)}, u32[]{:S(2)}, u32[]{:S(2)}) collective-permute-start(bf16[88,2048]{1,0:T(8,128)(2,1)S(1)} %collective-permute-done.5.refs_2_.refs_9_), channel_id=1, source_target_pairs={{0,224},{32,0},{64,32},{96,64},{128,96},{160,128},{192,160},{224,1... | collective-permute-start | bytes 1081352 | tf_op jit(solution)/shard_map/while/body/ppermute | solution.py:270
  62.0 14.7 %collective-permute-start.6 = (bf16[88,2048]{1,0:T(8,128)(2,1)S(1)}, bf16[88,2048]{1,0:T(8,128)(2,1)S(1)}, u32[]{:S(2)}, u32[]{:S(2)}) collective-permute-start(bf16[88,2048]{1,0:T(8,128)(2,1)S(1)} %collective-permute-done.2.refs_0_.refs_14_), channel_id=1, source_target_pairs={{0,32},{32,64},{64,96},{96,128},{128,160},{160,192},{192,224},{224... | collective-permute-start | bytes 1081352 | tf_op jit(solution)/shard_map/while/body/ppermute | solution.py:269
  62.0 13.5 %collective-permute-start.7 = (bf16[80,2048]{1,0:T(8,128)(2,1)S(1)}, bf16[80,2048]{1,0:T(8,128)(2,1)S(1)}, u32[]{:S(2)}, u32[]{:S(2)}) collective-permute-start(bf16[80,2048]{1,0:T(8,128)(2,1)S(1)} %collective-permute-done.3.refs_3_), channel_id=1, source_target_pairs={{0,224},{32,0},{64,32},{96,64},{128,96},{160,128},{192,160},{224,1... | collective-permute-start | bytes 983048 | tf_op jit(solution)/shard_map/while/body/ppermute | solution.py:270
  69.0 14.7 %collective-permute-start.12 = (bf16[80,2048]{1,0:T(8,128)(2,1)S(1)}, bf16[80,2048]{1,0:T(8,128)(2,1)S(1)}, u32[]{:S(2)}, u32[]{:S(2)}) collective-permute-start(bf16[80,2048]{1,0:T(8,128)(2,1)S(1)} %collective-permute-done.8.refs_1_), channel_id=1, source_target_pairs={{0,32},{32,64},{64,96},{96,128},{128,160},{160,192},{192,224},{224... | collective-permute-start | bytes 983048 | tf_op jit(solution)/shard_map/while/body/ppermute | solution.py:269
  69.0 15.9 %collective-permute-start.13 = (bf16[88,2048]{1,0:T(8,128)(2,1)S(1)}, bf16[88,2048]{1,0:T(8,128)(2,1)S(1)}, u32[]{:S(2)}, u32[]{:S(2)}) collective-permute-start(bf16[88,2048]{1,0:T(8,128)(2,1)S(1)} %collective-permute-done.9.refs_2_.refs_10_), channel_id=1, source_target_pairs={{0,224},{32,0},{64,32},{96,64},{128,96},{160,128},{192,160},{224,1... | collective-permute-start | bytes 1081352 | tf_op jit(solution)/shard_map/while/body/ppermute | solution.py:270
  76.8 14.7 %collective-permute-start.10 = (bf16[88,2048]{1,0:T(8,128)(2,1)S(1)}, bf16[88,2048]{1,0:T(8,128)(2,1)S(1)}, u32[]{:S(2)}, u32[]{:S(2)}) collective-permute-start(bf16[88,2048]{1,0:T(8,128)(2,1)S(1)} %collective-permute-done.6.refs_0_.refs_13_), channel_id=1, source_target_pairs={{0,32},{32,64},{64,96},{96,128},{128,160},{160,192},{192,224},{224... | collective-permute-start | bytes 1081352 | tf_op jit(solution)/shard_map/while/body/ppermute | solution.py:269
  76.8 13.1 %collective-permute-start.11 = (bf16[80,2048]{1,0:T(8,128)(2,1)S(1)}, bf16[80,2048]{1,0:T(8,128)(2,1)S(1)}, u32[]{:S(2)}, u32[]{:S(2)}) collective-permute-start(bf16[80,2048]{1,0:T(8,128)(2,1)S(1)} %collective-permute-done.7.refs_1_), channel_id=1, source_target_pairs={{0,224},{32,0},{64,32},{96,64},{128,96},{160,128},{192,160},{224,1... | collective-permute-start | bytes 983048 | tf_op jit(solution)/shard_map/while/body/ppermute | solution.py:270
  81.9 16.6 %collective-permute-start.16 = (bf16[80,2048]{1,0:T(8,128)(2,1)S(1)}, bf16[80,2048]{1,0:T(8,128)(2,1)S(1)}, u32[]{:S(2)}, u32[]{:S(2)}) collective-permute-start(bf16[80,2048]{1,0:T(8,128)(2,1)S(1)} %get-tuple-element.69), channel_id=1, source_target_pairs={{0,32},{32,64},{64,96},{96,128},{128,160},{160,192},{192,224},{224... | collective-permute-start | bytes 983048 | tf_op jit(solution)/shard_map/while/body/ppermute | solution.py:269
  83.8 14.7 %collective-permute-start.17 = (bf16[80,2048]{1,0:T(8,128)(2,1)S(1)}, bf16[80,2048]{1,0:T(8,128)(2,1)S(1)}, u32[]{:S(2)}, u32[]{:S(2)}) collective-permute-start(bf16[80,2048]{1,0:T(8,128)(2,1)S(1)} %get-tuple-element.70), channel_id=1, source_target_pairs={{0,224},{32,0},{64,32},{96,64},{128,96},{160,128},{192,160},{224,1... | collective-permute-start | bytes 983048 | tf_op jit(solution)/shard_map/while/body/ppermute | solution.py:270
  94.0 11.2 %collective-permute-start.14 = (bf16[80,2048]{1,0:T(8,128)(2,1)S(1)}, bf16[80,2048]{1,0:T(8,128)(2,1)S(1)}, u32[]{:S(2)}, u32[]{:S(2)}) collective-permute-start(bf16[80,2048]{1,0:T(8,128)(2,1)S(1)} %get-tuple-element.77), channel_id=1, source_target_pairs={{0,32},{32,64},{64,96},{96,128},{128,160},{160,192},{192,224},{224... | collective-permute-start | bytes 983048 | tf_op jit(solution)/shard_map/while/body/ppermute | solution.py:269
  94.1 11.2 %collective-permute-start.15 = (bf16[80,2048]{1,0:T(8,128)(2,1)S(1)}, bf16[80,2048]{1,0:T(8,128)(2,1)S(1)}, u32[]{:S(2)}, u32[]{:S(2)}) collective-permute-start(bf16[80,2048]{1,0:T(8,128)(2,1)S(1)} %get-tuple-element.78), channel_id=1, source_target_pairs={{0,224},{32,0},{64,32},{96,64},{128,96},{160,128},{192,160},{224,1... | collective-permute-start | bytes 983048 | tf_op jit(solution)/shard_map/while/body/ppermute | solution.py:270
  98.6 13.7 %collective-permute-start.20 = (bf16[80,2048]{1,0:T(8,128)(2,1)S(1)}, bf16[80,2048]{1,0:T(8,128)(2,1)S(1)}, u32[]{:S(2)}, u32[]{:S(2)}) collective-permute-start(bf16[80,2048]{1,0:T(8,128)(2,1)S(1)} %add_convert_fusion.9), channel_id=1, source_target_pairs={{0,32},{32,64},{64,96},{96,128},{128,160},{160,192},{192,224},{224... | collective-permute-start | bytes 983048 | tf_op jit(solution)/shard_map/while/body/ppermute | solution.py:269
  98.8 13.5 %collective-permute-start.21 = (bf16[80,2048]{1,0:T(8,128)(2,1)S(1)}, bf16[80,2048]{1,0:T(8,128)(2,1)S(1)}, u32[]{:S(2)}, u32[]{:S(2)}) collective-permute-start(bf16[80,2048]{1,0:T(8,128)(2,1)S(1)} %add_convert_fusion.8), channel_id=1, source_target_pairs={{0,224},{32,0},{64,32},{96,64},{128,96},{160,128},{192,160},{224,1... | collective-permute-start | bytes 983048 | tf_op jit(solution)/shard_map/while/body/ppermute | solution.py:270
  105.3 11.7 %collective-permute-start.19 = (bf16[80,2048]{1,0:T(8,128)(2,1)S(1)}, bf16[80,2048]{1,0:T(8,128)(2,1)S(1)}, u32[]{:S(2)}, u32[]{:S(2)}) collective-permute-start(bf16[80,2048]{1,0:T(8,128)(2,1)S(1)} %add_convert_fusion.6), channel_id=1, source_target_pairs={{0,224},{32,0},{64,32},{96,64},{128,96},{160,128},{192,160},{224,1... | collective-permute-start | bytes 983048 | tf_op jit(solution)/shard_map/while/body/ppermute | solution.py:270
  121.0 15.7 %collective-permute-start.26 = (bf16[80,2048]{1,0:T(8,128)(2,1)S(1)}, bf16[80,2048]{1,0:T(8,128)(2,1)S(1)}, u32[]{:S(2)}, u32[]{:S(2)}) collective-permute-start(bf16[80,2048]{1,0:T(8,128)(2,1)S(1)} %add_convert_fusion.5), channel_id=1, source_target_pairs={{0,32},{32,64},{64,96},{96,128},{128,160},{160,192},{192,224},{224... | collective-permute-start | bytes 983048 | tf_op jit(solution)/shard_map/while/body/ppermute | solution.py:269
  121.0 15.7 %collective-permute-start.25 = (bf16[80,2048]{1,0:T(8,128)(2,1)S(1)}, bf16[80,2048]{1,0:T(8,128)(2,1)S(1)}, u32[]{:S(2)}, u32[]{:S(2)}) collective-permute-start(bf16[80,2048]{1,0:T(8,128)(2,1)S(1)} %add_convert_fusion.4), channel_id=1, source_target_pairs={{0,224},{32,0},{64,32},{96,64},{128,96},{160,128},{192,160},{224,1... | collective-permute-start | bytes 983048 | tf_op jit(solution)/shard_map/while/body/ppermute | solution.py:270
  130.1 13.6 %collective-permute-start.24 = (bf16[80,2048]{1,0:T(8,128)(2,1)S(1)}, bf16[80,2048]{1,0:T(8,128)(2,1)S(1)}, u32[]{:S(2)}, u32[]{:S(2)}) collective-permute-start(bf16[80,2048]{1,0:T(8,128)(2,1)S(1)} %add_convert_fusion.1), channel_id=1, source_target_pairs={{0,32},{32,64},{64,96},{96,128},{128,160},{160,192},{192,224},{224... | collective-permute-start | bytes 983048 | tf_op jit(solution)/shard_map/while/body/ppermute | solution.py:269
  (10 other events, 215.6 us)

commit v8 on v7

--- a/solution.py
+++ b/solution.py
@@ -173,19 +173,18 @@
     place = jnp.dot(
         jnp.where(earlier, 1.0, 0.0).astype(jnp.bfloat16), taken, preferred_element_type=jnp.float32
     )
-    here = jnp.where(wide(taken) > 0.0, place, -1.0) - (step_ref[0] * 2 * half).astype(jnp.float32)
+    here = jnp.where(wide(taken) > 0.0, place, -1.0) - (step_ref[0] * (2 * half - 1)).astype(jnp.float32)
     here_ref[...] = here
     slots = lax.broadcasted_iota(jnp.int32, (rows_all, 2 * half), 1).astype(jnp.float32)
-    table = jnp.where(here[:, :1] == slots, 1.0, 0.0).astype(jnp.bfloat16)
+    table = jnp.where(here[:, :1] + 1.0 == slots, 1.0, 0.0).astype(jnp.bfloat16)
     plane = lax.dot_general(
         table, arrived_ref[:, :width], (((0,), (0,)), ((), ())), preferred_element_type=jnp.float32
     )
     count = place[rows_all - 1 :] + wide(taken[rows_all - 1 :])
-    gates = gates_ref.shape[1]
-    top_ref[:NOTE] = jnp.zeros((NOTE, width), top_ref.dtype)
-    top_ref[:NOTE, :gates] = jnp.broadcast_to(gates_ref[...], (NOTE, gates)).astype(top_ref.dtype)
-    top_ref[:NOTE, gates : gates + LANES] = jnp.broadcast_to(count, (NOTE, LANES)).astype(top_ref.dtype)
-    top_ref[NOTE:] = plane[:half].astype(top_ref.dtype)
+    blank = jnp.zeros((1, width - gates_ref.shape[1] - LANES), jnp.float32)
+    note = jnp.concatenate([gates_ref[...], count, blank], axis=1)
+    row = lax.broadcasted_iota(jnp.int32, (half, width), 0)
+    top_ref[...] = jnp.where(row == 0, jnp.broadcast_to(note, (half, width)), plane[:half]).astype(top_ref.dtype)
     bottom_ref[...] = plane[half:].astype(bottom_ref.dtype)
 
 
@@ -197,7 +196,7 @@
         place_kernel,
         in_specs=[near, pl.BlockSpec(memory_space=pltpu.SMEM), near],
         out_shape=[
-            jax.ShapeDtypeStruct((NOTE + half, width), jnp.bfloat16),
+            jax.ShapeDtypeStruct((half, width), jnp.bfloat16),
             jax.ShapeDtypeStruct((half, width), jnp.bfloat16),
             jax.ShapeDtypeStruct((rows_all, LANES), jnp.float32),
         ],
@@ -208,12 +207,12 @@
 
 def finish_kernel(*refs):
     step_ref, own_ref, *refs, here_ref, kept_ref, out_ref, next_ref, most_ref, scaled_ref = refs
-    parts, notes = refs[:6], [note[...].astype(jnp.float32)[:1] for note in refs[6:]]
+    parts, notes = refs[:8], [note[...].astype(jnp.float32)[:1] for note in refs[8:]]
     half = parts[0].shape[0]
     count = 2 * half
     own, step = own_ref[0], step_ref[0]
     planes = [lax.rem(own + j, len(notes)) for j in range(len(notes))]
-    first = jnp.full((1, LANES), (step * count).astype(jnp.float32))
+    first = jnp.full((1, LANES), (step * (count - 1) - 1).astype(jnp.float32))
     most = jnp.zeros((1, LANES), jnp.float32)
     for plane, note in zip(planes, notes):
         rows = note[:, 3 * LANES :]
@@ -228,14 +227,18 @@
         gate = note[:, :LANES] + note[:, LANES : 2 * LANES] + note[:, 2 * LANES : 3 * LANES]
         gates = gates + jnp.where(slots == (plane * LANES + lanes).astype(jnp.float32), gate, 0.0)
     gates = jnp.sum(gates, axis=1, keepdims=True)
-    for i, (mine, one, other) in enumerate((parts[:3], parts[3:])):
-        sums = mine[...] + wide(one[...]) + wide(other[...])
-        scaled_ref[i * half : (i + 1) * half] = narrow(gates[i * half : (i + 1) * half] * sums)
+    quarter = half // 2
+    for i, (mine, near, *fars) in enumerate((parts[:4], parts[4:])):
+        for j, far in enumerate(fars):
+            rows = slice(j * quarter, (j + 1) * quarter)
+            sums = mine[rows] + wide(near[rows]) + wide(far[...])
+            part = slice(i * half + j * quarter, i * half + (j + 1) * quarter)
+            scaled_ref[part] = narrow(gates[part] * sums)
     here = here_ref[:, :1]
     places = lax.broadcasted_iota(jnp.int32, (here.shape[0], count), 1).astype(jnp.float32)
-    table = jnp.where(here == places, 1.0, 0.0).astype(jnp.bfloat16)
+    table = jnp.where(here + 1.0 == places, 1.0, 0.0).astype(jnp.bfloat16)
     returned = jnp.dot(table, scaled_ref[...], preferred_element_type=jnp.float32)
-    inside = jnp.logical_and(here >= 0.0, here < count)
+    inside = jnp.logical_and(here >= 0.0, here < count - 1)
     out_ref[...] = narrow(jnp.where(inside, returned, wide(kept_ref[...])))
 
 
@@ -305,15 +308,25 @@
     sends = tuple(mlp(*firsts, sent=(0, 1)))
     seconds = seconds_back
     firsts = hop(*sends)
-    for k in range(far - 1, 0, -1):
-        if k > 1:
-            seconds = after(seconds, *sends)
-            sends = narrow(wide(seconds[0]) + above[k - 1][1]), narrow(wide(seconds[1]) + below[k - 1][0])
-            seconds = hop(*sends)
+    for k in range(far - 1, 1, -1):
+        seconds = after(seconds, *sends)
+        sends = narrow(wide(seconds[0]) + above[k - 1][1]), narrow(wide(seconds[1]) + below[k - 1][0])
+        seconds = hop(*sends)
         firsts = after(firsts, *sends)
-        sends = narrow(wide(firsts[0]) + above[k][0]), narrow(wide(firsts[1]) + below[k][1])
-        firsts = hop(*sends)
-    parts = own[0], firsts[0], seconds[1], own[1], seconds[0], firsts[1]
+        if k > 2:
+            sends = narrow(wide(firsts[0]) + above[k][0]), narrow(wide(firsts[1]) + below[k][1])
+            firsts = hop(*sends)
+    quarters = [slice(0, half // 2), slice(half // 2, half)]
+    hops = []
+    for part in quarters:
+        sends = narrow(wide(firsts[0][part]) + above[2][0][part]), narrow(wide(firsts[1][part]) + below[2][1][part])
+        hops.append(hop(*sends))
+    fars = []
+    for j, part in enumerate(quarters):
+        firsts = after(hops[j], *sends)
+        sends = narrow(wide(firsts[0]) + above[1][0][part]), narrow(wide(firsts[1]) + below[1][1][part])
+        fars.append(hop(*sends))
+    parts = own[0], seconds[1], fars[0][0], fars[1][0], own[1], seconds[0], fars[0][1], fars[1][1]
     return parts, [notes[j] for j in range(dp_count)]
 
 
@@ -323,7 +336,8 @@
     width = tokens.shape[1]
     slots_dp = gate_weights.shape[1]
     rows_all = expert_count * MOST
-    round_rows = slots_dp + slots_dp // 4
+    half = (slots_dp + slots_dp // 4) // 2
+    round_rows = 2 * half - 1
     own_dp = lax.axis_index("dp")
 
     packed, pack_table, blank = pack(tokens, expert_ranks, capacity)
@@ -338,7 +352,7 @@
 
     def experts(state):
         step, _, sent_back = state
-        top, bottom, here = place(arrived, step, gate_pieces, round_rows // 2)
+        top, bottom, here = place(arrived, step, gate_pieces, half)
         parts, notes = ring_experts(top, bottom, weight_in[0], weight_out[0], dp_count)
         sent_back, step, most = finish(step, own_dp.reshape(1), parts, notes, here, sent_back)
         return step, most, sent_back

time: 172 us -> 170 us (0.988)
    ppermute x14 -> x16, waiting for transfers between devices: 14.1 us -> 4.09 us  [hop(): down_rows = lax.ppermute(down_rows, 'dp', downward)]
    ppermute x14 -> x16, waiting for transfers between devices: 39.3 us -> 49.3 us  [hop(): up_rows = lax.ppermute(up_rows, 'dp', upward)]
    ppermute x14 -> x16, starting transfers between devices: 32.8 us -> 28.2 us  [hop(): down_rows = lax.ppermute(down_rows, 'dp', downward)]
    ppermute x14 -> x16, starting transfers between devices: 3.34 us -> 7.19 us  [hop(): up_rows = lax.ppermute(up_rows, 'dp', upward)]
  transfers between devices with their start and end apart: 29 -> 33, of which waited for: 20 -> 18; matrix products, arithmetic and copies ran while one was open for 1% -> 1% of each run, Pallas kernels for 12% -> 12%
where the time goes in v8:
time: 170 us
  waiting for transfers between devices  70.3 us (41%)
  starting transfers between devices  44 us (26%)
  Pallas kernels  24.7 us (15%)
  blocking collectives  23.8 us (14%)
  local copies, waits for them, and re-layouts  2.75 us (2%)
    ppermute x16, waiting for transfers between devices, hop(): up_rows = lax.ppermute(up_rows, 'dp', upward)  49.3 us
    ppermute x16, starting transfers between devices, hop(): down_rows = lax.ppermute(down_rows, 'dp', downward)  28.2 us
    all_to_all x1, blocking collectives, on_device(): lax.all_to_all(sent_back.reshape(expert_count, MOST, width), EXPERT, spli...  23.8 us
    pallas_call x6, Pallas kernels, expert_rows(): pl.pallas_call(staged_expert_kernel if staged else expert_kernel, out_sha...  20.3 us
    all_to_all x1, waiting for transfers between devices, on_device(): lax.all_to_all(packed.reshape(expert_count, MOST, width + LANES), EXPERT,...  17 us
    all_to_all x1, starting transfers between devices, on_device(): lax.all_to_all(packed.reshape(expert_count, MOST, width + LANES), EXPERT,...  8.58 us
    ppermute x16, starting transfers between devices, hop(): up_rows = lax.ppermute(up_rows, 'dp', upward)  7.19 us
    ppermute x16, waiting for transfers between devices, hop(): down_rows = lax.ppermute(down_rows, 'dp', downward)  4.09 us
  transfers between devices with their start and end apart: 33, of which 18 were waited for; matrix products, arithmetic and copies ran while one was open for 1% of the time, Pallas kernels for 12%

profile of v8, /device:TPU:1, one launch (start us, length us, event | category | flops | bytes accessed | tf_op | source)
XLA Modules:
  0.0 169.9 jit_solution(5713028244821799399)
XLA Ops:
  4.7 8.6 %all-to-all-start = ((bf16[32,8,2176]{2,1,0:T(8,128)(2,1)}), bf16[32,8,2176]{2,1,0:T(8,128)(2,1)S(1)}, u32[]{:S(2)}, u32[]{:S(2)}) async-start(bf16[32,8,2176]{2,1,0:T(8,128)(2,1)} %bitcast.5), calls=%async_computation | async-start | bytes 2228224 | tf_op jit(solution)/shard_map/all_to_all | solution.py:344
  14.0 17.0 %all-to-all-done = bf16[32,8,2176]{2,1,0:T(8,128)(2,1)S(1)} async-done(((bf16[32,8,2176]{2,1,0:T(8,128)(2,1)}), bf16[32,8,2176]{2,1,0:T(8,128)(2,1)S(1)}, u32[]{:S(2)}, u32[]{:S(2)}) %all-to-all-start) | async-done | bytes 1114144 | tf_op jit(solution)/shard_map/all_to_all | solution.py:344
  30.9 113.7 %while.11 = (s32[1]{0:T(128)}, s32[1]{0:T(128)}, bf16[256,2048]{1,0:T(8,128)(2,1)}, s32[]{:T(128)}, bf16[256,2176]{1,0:T(8,128)(2,1)S(1)}, /*index=5*/f32[1,384]...) while((s32[1]{0:T(128)}, s32[1]{0:T(128)}, bf16[256,2048]{1,0:T(8,128)(2,1)}, s32[]{:T(128)}, ...), condition=%region_1.0_spmd, body=%region_0.0_spmd | while | flops 10742333440 | bytes 122160512 | solution.py:360
  31.6 5.7 %collective-permute-start.1 = (bf16[80,2048]{1,0:T(8,128)(2,1)S(1)}, bf16[80,2048]{1,0:T(8,128)(2,1)S(1)}, u32[]{:S(2)}, u32[]{:S(2)}) collective-permute-start(bf16[80,2048]{1,0:T(8,128)(2,1)S(1)} %get-tuple-element.42.refs_1_), channel_id=1, source_target_pairs={{0,224},{32,0},{64,32},{96,64},{128,96},{160,128},{192,160},{224,1... | collective-permute-start | bytes 983048 | tf_op jit(solution)/shard_map/while/body/ppermute | solution.py:273
  37.2 2.7 %collective-permute-start.5 = (bf16[80,2048]{1,0:T(8,128)(2,1)S(1)}, bf16[80,2048]{1,0:T(8,128)(2,1)S(1)}, u32[]{:S(2)}, u32[]{:S(2)}) collective-permute-start(bf16[80,2048]{1,0:T(8,128)(2,1)S(1)} %get-tuple-element.41.refs_0_.refs_10_), channel_id=1, source_target_pairs={{0,224},{32,0},{64,32},{96,64},{128,96},{160,128},{192,160},{224,1... | collective-permute-start | bytes 983048 | tf_op jit(solution)/shard_map/while/body/ppermute | solution.py:273
  39.9 5.2 %expert_rows.6 = (f32[80,2048]{1,0:T(8,128)S(1)}, f32[80,2048]{1,0:T(8,128)S(1)}, bf16[2048,1024]{1,0:T(8,128)(2,1)S(1)}, bf16[1024,2048]{1,0:T(8,128)(2,1)S(1)}) custom-call(bf16[80,2048]{1,0:T(8,128)(2,1)S(1)} %get-tuple-element.41.refs_0_.refs_10_, bf16[80,2048]{1,0:T(8,128)(2,1)S(1)} %get-tuple-element.42.refs_1_, bf16[2048,1024]{1,0:T(8,128)(2,1)} %bitcast.13, ...), custom_call_target="tpu_custom_call" | custom-call | flops 1342177280 | bytes 10354688 | tf_op jit(solution)/shard_map/while/body/expert_rows/pallas_call | solution.py:108
  48.8 5.6 %collective-permute-done.4.refs_1_ = bf16[80,2048]{1,0:T(8,128)(2,1)S(1)} collective-permute-done((bf16[80,2048]{1,0:T(8,128)(2,1)S(1)}, bf16[80,2048]{1,0:T(8,128)(2,1)S(1)}, u32[]{:S(2)}, u32[]{:S(2)}) %collective-permute-start.4) | collective-permute-done | bytes 327712 | tf_op jit(solution)/shard_map/while/body/ppermute | solution.py:272
  54.3 2.7 %collective-permute-start.9 = (bf16[80,2048]{1,0:T(8,128)(2,1)S(1)}, bf16[80,2048]{1,0:T(8,128)(2,1)S(1)}, u32[]{:S(2)}, u32[]{:S(2)}) collective-permute-start(bf16[80,2048]{1,0:T(8,128)(2,1)S(1)} %collective-permute-done.5.refs_2_.refs_11_), channel_id=1, source_target_pairs={{0,224},{32,0},{64,32},{96,64},{128,96},{160,128},{192,160},{224,1... | collective-permute-start | bytes 983048 | tf_op jit(solution)/shard_map/while/body/ppermute | solution.py:273
  57.0 3.8 %expert_rows.7 = (f32[80,2048]{1,0:T(8,128)S(1)}, f32[80,2048]{1,0:T(8,128)S(1)}, f32[80,2048]{1,0:T(8,128)S(1)}, f32[80,2048]{1,0:T(8,128)S(1)}) custom-call(bf16[80,2048]{1,0:T(8,128)(2,1)S(1)} %collective-permute-done.refs_0_.refs_17_, bf16[80,2048]{1,0:T(8,128)(2,1)S(1)} %collective-permute-done.4.refs_1_, ...), custom_call_target="tpu_custom_call" | custom-call | flops 2684354560 | bytes 12320768 | tf_op jit(solution)/shard_map/while/body/expert_rows/pallas_call | solution.py:108
  62.8 5.6 %collective-permute-done.8.refs_1_ = bf16[80,2048]{1,0:T(8,128)(2,1)S(1)} collective-permute-done((bf16[80,2048]{1,0:T(8,128)(2,1)S(1)}, bf16[80,2048]{1,0:T(8,128)(2,1)S(1)}, u32[]{:S(2)}, u32[]{:S(2)}) %collective-permute-start.8) | collective-permute-done | bytes 327712 | tf_op jit(solution)/shard_map/while/body/ppermute | solution.py:272
  68.4 2.7 %collective-permute-start.15 = (bf16[80,2048]{1,0:T(8,128)(2,1)S(1)}, bf16[80,2048]{1,0:T(8,128)(2,1)S(1)}, u32[]{:S(2)}, u32[]{:S(2)}) collective-permute-start(bf16[80,2048]{1,0:T(8,128)(2,1)S(1)} %collective-permute-done.9.refs_2_.refs_12_), channel_id=1, source_target_pairs={{0,224},{32,0},{64,32},{96,64},{128,96},{160,128},{192,160},{224,1... | collective-permute-start | bytes 983048 | tf_op jit(solution)/shard_map/while/body/ppermute | solution.py:273
  71.1 3.8 %expert_rows.8 = (f32[80,2048]{1,0:T(8,128)S(1)}, f32[80,2048]{1,0:T(8,128)S(1)}, f32[80,2048]{1,0:T(8,128)S(1)}, f32[80,2048]{1,0:T(8,128)S(1)}) custom-call(bf16[80,2048]{1,0:T(8,128)(2,1)S(1)} %collective-permute-done.2.refs_0_.refs_16_, bf16[80,2048]{1,0:T(8,128)(2,1)S(1)} %collective-permute-done.8.refs_1_, ...), custom_call_target="tpu_custom_call" | custom-call | flops 2684354560 | bytes 12320768 | tf_op jit(solution)/shard_map/while/body/expert_rows/pallas_call | solution.py:108
  79.5 3.0 %collective-permute-done.14.refs_0_ = bf16[80,2048]{1,0:T(8,128)(2,1)S(1)} collective-permute-done((bf16[80,2048]{1,0:T(8,128)(2,1)S(1)}, bf16[80,2048]{1,0:T(8,128)(2,1)S(1)}, u32[]{:S(2)}, u32[]{:S(2)}) %collective-permute-start.14) | collective-permute-done | bytes 327712 | tf_op jit(solution)/shard_map/while/body/ppermute | solution.py:272
  85.3 4.1 %collective-permute-done.12.refs_0_.refs_14_ = bf16[80,2048]{1,0:T(8,128)(2,1)S(1)} collective-permute-done((bf16[80,2048]{1,0:T(8,128)(2,1)S(1)}, bf16[80,2048]{1,0:T(8,128)(2,1)S(1)}, u32[]{:S(2)}, u32[]{:S(2)}) %collective-permute-start.12) | collective-permute-done | bytes 327712 | tf_op jit(solution)/shard_map/while/body/ppermute | solution.py:272
  92.0 2.7 %collective-permute-start.19 = (bf16[80,2048]{1,0:T(8,128)(2,1)S(1)}, bf16[80,2048]{1,0:T(8,128)(2,1)S(1)}, u32[]{:S(2)}, u32[]{:S(2)}) collective-permute-start(bf16[80,2048]{1,0:T(8,128)(2,1)S(1)} %get-tuple-element.78), channel_id=1, source_target_pairs={{0,224},{32,0},{64,32},{96,64},{128,96},{160,128},{192,160},{224,1... | collective-permute-start | bytes 983048 | tf_op jit(solution)/shard_map/while/body/ppermute | solution.py:273
  96.7 2.7 %collective-permute-start.17 = (bf16[80,2048]{1,0:T(8,128)(2,1)S(1)}, bf16[80,2048]{1,0:T(8,128)(2,1)S(1)}, u32[]{:S(2)}, u32[]{:S(2)}) collective-permute-start(bf16[80,2048]{1,0:T(8,128)(2,1)S(1)} %add_convert_fusion.4), channel_id=1, source_target_pairs={{0,224},{32,0},{64,32},{96,64},{128,96},{160,128},{192,160},{224,1... | collective-permute-start | bytes 983048 | tf_op jit(solution)/shard_map/while/body/ppermute | solution.py:273
  99.5 3.7 %collective-permute-done.18 = bf16[80,2048]{1,0:T(8,128)(2,1)S(1)} collective-permute-done((bf16[80,2048]{1,0:T(8,128)(2,1)S(1)}, bf16[80,2048]{1,0:T(8,128)(2,1)S(1)}, u32[]{:S(2)}, u32[]{:S(2)}) %collective-permute-start.18) | collective-permute-done | bytes 327712 | tf_op jit(solution)/shard_map/while/body/ppermute | solution.py:272
  105.0 5.2 %collective-permute-done.16 = bf16[80,2048]{1,0:T(8,128)(2,1)S(1)} collective-permute-done((bf16[80,2048]{1,0:T(8,128)(2,1)S(1)}, bf16[80,2048]{1,0:T(8,128)(2,1)S(1)}, u32[]{:S(2)}, u32[]{:S(2)}) %collective-permute-start.16) | collective-permute-done | bytes 327712 | tf_op jit(solution)/shard_map/while/body/ppermute | solution.py:272
  110.4 3.7 %collective-permute-done.22 = bf16[80,2048]{1,0:T(8,128)(2,1)S(1)} collective-permute-done((bf16[80,2048]{1,0:T(8,128)(2,1)S(1)}, bf16[80,2048]{1,0:T(8,128)(2,1)S(1)}, u32[]{:S(2)}, u32[]{:S(2)}) %collective-permute-start.22) | collective-permute-done | bytes 327712 | tf_op jit(solution)/shard_map/while/body/ppermute | solution.py:273
  116.7 2.7 %collective-permute-start.24 = (bf16[40,2048]{1,0:T(8,128)(2,1)S(1)}, bf16[40,2048]{1,0:T(8,128)(2,1)S(1)}, u32[]{:S(2)}, u32[]{:S(2)}) collective-permute-start(bf16[40,2048]{1,0:T(8,128)(2,1)S(1)} %get-tuple-element.123), channel_id=1, source_target_pairs={{0,224},{32,0},{64,32},{96,64},{128,96},{160,128},{192,160},{224,1... | collective-permute-start | bytes 491528 | tf_op jit(solution)/shard_map/while/body/ppermute | solution.py:273
  125.0 8.6 %collective-permute-done.26 = bf16[40,2048]{1,0:T(8,128)(2,1)S(1)} collective-permute-done((bf16[40,2048]{1,0:T(8,128)(2,1)S(1)}, bf16[40,2048]{1,0:T(8,128)(2,1)S(1)}, u32[]{:S(2)}, u32[]{:S(2)}) %collective-permute-start.26) | collective-permute-done | bytes 163872 | tf_op jit(solution)/shard_map/while/body/ppermute | solution.py:272
  133.8 2.7 %collective-permute-start.31 = (bf16[40,2048]{1,0:T(8,128)(2,1)S(1)}, bf16[40,2048]{1,0:T(8,128)(2,1)S(1)}, u32[]{:S(2)}, u32[]{:S(2)}) collective-permute-start(bf16[40,2048]{1,0:T(8,128)(2,1)S(1)} %add_convert_fusion.6), channel_id=1, source_target_pairs={{0,224},{32,0},{64,32},{96,64},{128,96},{160,128},{192,160},{224,1... | collective-permute-start | bytes 491528 | tf_op jit(solution)/shard_map/while/body/ppermute | solution.py:273
  139.0 2.7 %collective-permute-done.28.refs_5_ = bf16[40,2048]{1,0:T(8,128)(2,1)S(1)} collective-permute-done((bf16[40,2048]{1,0:T(8,128)(2,1)S(1)}, bf16[40,2048]{1,0:T(8,128)(2,1)S(1)}, u32[]{:S(2)}, u32[]{:S(2)}) %collective-permute-start.28) | collective-permute-done | bytes 163872 | tf_op jit(solution)/shard_map/while/body/ppermute | solution.py:272
  144.6 23.8 %all_to_all.10 = bf16[32,8,2048]{2,1,0:T(8,128)(2,1)S(1)} all-to-all(bf16[32,8,2048]{2,1,0:T(8,128)(2,1)} %bitcast.16), channel_id=1, replica_groups=mesh['dp'=8,'expert_0'=4,'expert_1'=4,'expert_2'=2] {'expert_0','expert_..., dimensions={0} | all-to-all | bytes 2097152 | tf_op jit(solution)/shard_map/all_to_all | solution.py:365
  (79 shorter events, 39.5 us)
Async XLA Ops:
  4.7 26.2 %all-to-all-start = ((bf16[32,8,2176]{2,1,0:T(8,128)(2,1)}), bf16[32,8,2176]{2,1,0:T(8,128)(2,1)S(1)}, u32[]{:S(2)}, u32[]{:S(2)}) async-start(bf16[32,8,2176]{2,1,0:T(8,128)(2,1)} %bitcast.5), calls=%async_computation | async-start | bytes 2228224 | tf_op jit(solution)/shard_map/all_to_all | solution.py:344
  31.6 13.6 %collective-permute-start.1 = (bf16[80,2048]{1,0:T(8,128)(2,1)S(1)}, bf16[80,2048]{1,0:T(8,128)(2,1)S(1)}, u32[]{:S(2)}, u32[]{:S(2)}) collective-permute-start(bf16[80,2048]{1,0:T(8,128)(2,1)S(1)} %get-tuple-element.42.refs_1_), channel_id=1, source_target_pairs={{0,224},{32,0},{64,32},{96,64},{128,96},{160,128},{192,160},{224,1... | collective-permute-start | bytes 983048 | tf_op jit(solution)/shard_map/while/body/ppermute | solution.py:273
  37.2 17.1 %collective-permute-start.4 = (bf16[80,2048]{1,0:T(8,128)(2,1)S(1)}, bf16[80,2048]{1,0:T(8,128)(2,1)S(1)}, u32[]{:S(2)}, u32[]{:S(2)}) collective-permute-start(bf16[80,2048]{1,0:T(8,128)(2,1)S(1)} %get-tuple-element.42.refs_1_), channel_id=1, source_target_pairs={{0,32},{32,64},{64,96},{96,128},{128,160},{160,192},{192,224},{224... | collective-permute-start | bytes 983048 | tf_op jit(solution)/shard_map/while/body/ppermute | solution.py:272
  37.2 17.1 %collective-permute-start.5 = (bf16[80,2048]{1,0:T(8,128)(2,1)S(1)}, bf16[80,2048]{1,0:T(8,128)(2,1)S(1)}, u32[]{:S(2)}, u32[]{:S(2)}) collective-permute-start(bf16[80,2048]{1,0:T(8,128)(2,1)S(1)} %get-tuple-element.41.refs_0_.refs_10_), channel_id=1, source_target_pairs={{0,224},{32,0},{64,32},{96,64},{128,96},{160,128},{192,160},{224,1... | collective-permute-start | bytes 983048 | tf_op jit(solution)/shard_map/while/body/ppermute | solution.py:273
  47.3 13.5 %collective-permute-start.3 = (bf16[80,2048]{1,0:T(8,128)(2,1)S(1)}, bf16[80,2048]{1,0:T(8,128)(2,1)S(1)}, u32[]{:S(2)}, u32[]{:S(2)}) collective-permute-start(bf16[80,2048]{1,0:T(8,128)(2,1)S(1)} %collective-permute-done.1.refs_3_), channel_id=1, source_target_pairs={{0,224},{32,0},{64,32},{96,64},{128,96},{160,128},{192,160},{224,1... | collective-permute-start | bytes 983048 | tf_op jit(solution)/shard_map/while/body/ppermute | solution.py:273
  47.6 13.8 %collective-permute-start.2 = (bf16[80,2048]{1,0:T(8,128)(2,1)S(1)}, bf16[80,2048]{1,0:T(8,128)(2,1)S(1)}, u32[]{:S(2)}, u32[]{:S(2)}) collective-permute-start(bf16[80,2048]{1,0:T(8,128)(2,1)S(1)} %collective-permute-done.refs_0_.refs_17_), channel_id=1, source_target_pairs={{0,32},{32,64},{64,96},{96,128},{128,160},{160,192},{192,224},{224... | collective-permute-start | bytes 983048 | tf_op jit(solution)/shard_map/while/body/ppermute | solution.py:272
  54.3 14.0 %collective-permute-start.8 = (bf16[80,2048]{1,0:T(8,128)(2,1)S(1)}, bf16[80,2048]{1,0:T(8,128)(2,1)S(1)}, u32[]{:S(2)}, u32[]{:S(2)}) collective-permute-start(bf16[80,2048]{1,0:T(8,128)(2,1)S(1)} %collective-permute-done.4.refs_1_), channel_id=1, source_target_pairs={{0,32},{32,64},{64,96},{96,128},{128,160},{160,192},{192,224},{224... | collective-permute-start | bytes 983048 | tf_op jit(solution)/shard_map/while/body/ppermute | solution.py:272
  54.3 14.0 %collective-permute-start.9 = (bf16[80,2048]{1,0:T(8,128)(2,1)S(1)}, bf16[80,2048]{1,0:T(8,128)(2,1)S(1)}, u32[]{:S(2)}, u32[]{:S(2)}) collective-permute-start(bf16[80,2048]{1,0:T(8,128)(2,1)S(1)} %collective-permute-done.5.refs_2_.refs_11_), channel_id=1, source_target_pairs={{0,224},{32,0},{64,32},{96,64},{128,96},{160,128},{192,160},{224,1... | collective-permute-start | bytes 983048 | tf_op jit(solution)/shard_map/while/body/ppermute | solution.py:273
  61.4 13.5 %collective-permute-start.7 = (bf16[80,2048]{1,0:T(8,128)(2,1)S(1)}, bf16[80,2048]{1,0:T(8,128)(2,1)S(1)}, u32[]{:S(2)}, u32[]{:S(2)}) collective-permute-start(bf16[80,2048]{1,0:T(8,128)(2,1)S(1)} %collective-permute-done.3.refs_3_), channel_id=1, source_target_pairs={{0,224},{32,0},{64,32},{96,64},{128,96},{160,128},{192,160},{224,1... | collective-permute-start | bytes 983048 | tf_op jit(solution)/shard_map/while/body/ppermute | solution.py:273
  61.6 13.8 %collective-permute-start.6 = (bf16[80,2048]{1,0:T(8,128)(2,1)S(1)}, bf16[80,2048]{1,0:T(8,128)(2,1)S(1)}, u32[]{:S(2)}, u32[]{:S(2)}) collective-permute-start(bf16[80,2048]{1,0:T(8,128)(2,1)S(1)} %collective-permute-done.2.refs_0_.refs_16_), channel_id=1, source_target_pairs={{0,32},{32,64},{64,96},{96,128},{128,160},{160,192},{192,224},{224... | collective-permute-start | bytes 983048 | tf_op jit(solution)/shard_map/while/body/ppermute | solution.py:272
  68.4 14.0 %collective-permute-start.14 = (bf16[80,2048]{1,0:T(8,128)(2,1)S(1)}, bf16[80,2048]{1,0:T(8,128)(2,1)S(1)}, u32[]{:S(2)}, u32[]{:S(2)}) collective-permute-start(bf16[80,2048]{1,0:T(8,128)(2,1)S(1)} %collective-permute-done.8.refs_1_), channel_id=1, source_target_pairs={{0,32},{32,64},{64,96},{96,128},{128,160},{160,192},{192,224},{224... | collective-permute-start | bytes 983048 | tf_op jit(solution)/shard_map/while/body/ppermute | solution.py:272
  68.4 14.0 %collective-permute-start.15 = (bf16[80,2048]{1,0:T(8,128)(2,1)S(1)}, bf16[80,2048]{1,0:T(8,128)(2,1)S(1)}, u32[]{:S(2)}, u32[]{:S(2)}) collective-permute-start(bf16[80,2048]{1,0:T(8,128)(2,1)S(1)} %collective-permute-done.9.refs_2_.refs_12_), channel_id=1, source_target_pairs={{0,224},{32,0},{64,32},{96,64},{128,96},{160,128},{192,160},{224,1... | collective-permute-start | bytes 983048 | tf_op jit(solution)/shard_map/while/body/ppermute | solution.py:273
  75.4 14.0 %collective-permute-start.12 = (bf16[80,2048]{1,0:T(8,128)(2,1)S(1)}, bf16[80,2048]{1,0:T(8,128)(2,1)S(1)}, u32[]{:S(2)}, u32[]{:S(2)}) collective-permute-start(bf16[80,2048]{1,0:T(8,128)(2,1)S(1)} %collective-permute-done.6.refs_0_.refs_15_), channel_id=1, source_target_pairs={{0,32},{32,64},{64,96},{96,128},{128,160},{160,192},{192,224},{224... | collective-permute-start | bytes 983048 | tf_op jit(solution)/shard_map/while/body/ppermute | solution.py:272
  79.4 17.1 %collective-permute-start.10 = (bf16[80,2048]{1,0:T(8,128)(2,1)S(1)}, bf16[80,2048]{1,0:T(8,128)(2,1)S(1)}, u32[]{:S(2)}, u32[]{:S(2)}) collective-permute-start(bf16[80,2048]{1,0:T(8,128)(2,1)S(1)} %get-tuple-element.67), channel_id=1, source_target_pairs={{0,32},{32,64},{64,96},{96,128},{128,160},{160,192},{192,224},{224... | collective-permute-start | bytes 983048 | tf_op jit(solution)/shard_map/while/body/ppermute | solution.py:272
  82.4 14.0 %collective-permute-start.11 = (bf16[80,2048]{1,0:T(8,128)(2,1)S(1)}, bf16[80,2048]{1,0:T(8,128)(2,1)S(1)}, u32[]{:S(2)}, u32[]{:S(2)}) collective-permute-start(bf16[80,2048]{1,0:T(8,128)(2,1)S(1)} %get-tuple-element.68), channel_id=1, source_target_pairs={{0,224},{32,0},{64,32},{96,64},{128,96},{160,128},{192,160},{224,1... | collective-permute-start | bytes 983048 | tf_op jit(solution)/shard_map/while/body/ppermute | solution.py:273
  91.9 11.2 %collective-permute-start.18 = (bf16[80,2048]{1,0:T(8,128)(2,1)S(1)}, bf16[80,2048]{1,0:T(8,128)(2,1)S(1)}, u32[]{:S(2)}, u32[]{:S(2)}) collective-permute-start(bf16[80,2048]{1,0:T(8,128)(2,1)S(1)} %get-tuple-element.77), channel_id=1, source_target_pairs={{0,32},{32,64},{64,96},{96,128},{128,160},{160,192},{192,224},{224... | collective-permute-start | bytes 983048 | tf_op jit(solution)/shard_map/while/body/ppermute | solution.py:272
  96.6 13.6 %collective-permute-start.16 = (bf16[80,2048]{1,0:T(8,128)(2,1)S(1)}, bf16[80,2048]{1,0:T(8,128)(2,1)S(1)}, u32[]{:S(2)}, u32[]{:S(2)}) collective-permute-start(bf16[80,2048]{1,0:T(8,128)(2,1)S(1)} %add_convert_fusion.5), channel_id=1, source_target_pairs={{0,32},{32,64},{64,96},{96,128},{128,160},{160,192},{192,224},{224... | collective-permute-start | bytes 983048 | tf_op jit(solution)/shard_map/while/body/ppermute | solution.py:272
  96.7 13.5 %collective-permute-start.17 = (bf16[80,2048]{1,0:T(8,128)(2,1)S(1)}, bf16[80,2048]{1,0:T(8,128)(2,1)S(1)}, u32[]{:S(2)}, u32[]{:S(2)}) collective-permute-start(bf16[80,2048]{1,0:T(8,128)(2,1)S(1)} %add_convert_fusion.4), channel_id=1, source_target_pairs={{0,224},{32,0},{64,32},{96,64},{128,96},{160,128},{192,160},{224,1... | collective-permute-start | bytes 983048 | tf_op jit(solution)/shard_map/while/body/ppermute | solution.py:273
  103.4 13.0 %collective-permute-start.21 = (bf16[80,2048]{1,0:T(8,128)(2,1)S(1)}, bf16[80,2048]{1,0:T(8,128)(2,1)S(1)}, u32[]{:S(2)}, u32[]{:S(2)}) collective-permute-start(bf16[80,2048]{1,0:T(8,128)(2,1)S(1)} %add_convert_fusion.3), channel_id=1, source_target_pairs={{0,32},{32,64},{64,96},{96,128},{128,160},{160,192},{192,224},{224... | collective-permute-start | bytes 983048 | tf_op jit(solution)/shard_map/while/body/ppermute | solution.py:272
  119.4 14.4 %collective-permute-start.20 = (bf16[80,2048]{1,0:T(8,128)(2,1)S(1)}, bf16[80,2048]{1,0:T(8,128)(2,1)S(1)}, u32[]{:S(2)}, u32[]{:S(2)}) collective-permute-start(bf16[80,2048]{1,0:T(8,128)(2,1)S(1)} %add_convert_fusion.1), channel_id=1, source_target_pairs={{0,224},{32,0},{64,32},{96,64},{128,96},{160,128},{192,160},{224,1... | collective-permute-start | bytes 983048 | tf_op jit(solution)/shard_map/while/body/ppermute | solution.py:273
  119.5 17.1 %collective-permute-start.29 = (bf16[80,2048]{1,0:T(8,128)(2,1)S(1)}, bf16[80,2048]{1,0:T(8,128)(2,1)S(1)}, u32[]{:S(2)}, u32[]{:S(2)}) collective-permute-start(bf16[80,2048]{1,0:T(8,128)(2,1)S(1)} %add_convert_fusion), channel_id=1, source_target_pairs={{0,32},{32,64},{64,96},{96,128},{128,160},{160,192},{192,224},{224... | collective-permute-start | bytes 983048 | tf_op jit(solution)/shard_map/while/body/ppermute | solution.py:272
  120.9 12.7 %collective-permute-start.26 = (bf16[40,2048]{1,0:T(8,128)(2,1)S(1)}, bf16[40,2048]{1,0:T(8,128)(2,1)S(1)}, u32[]{:S(2)}, u32[]{:S(2)}) collective-permute-start(bf16[40,2048]{1,0:T(8,128)(2,1)S(1)} %get-tuple-element.124), channel_id=1, source_target_pairs={{0,32},{32,64},{64,96},{96,128},{128,160},{160,192},{192,224},{224... | collective-permute-start | bytes 491528 | tf_op jit(solution)/shard_map/while/body/ppermute | solution.py:272
  122.0 11.6 %collective-permute-start.27 = (bf16[40,2048]{1,0:T(8,128)(2,1)S(1)}, bf16[40,2048]{1,0:T(8,128)(2,1)S(1)}, u32[]{:S(2)}, u32[]{:S(2)}) collective-permute-start(bf16[40,2048]{1,0:T(8,128)(2,1)S(1)} %get-tuple-element.122), channel_id=1, source_target_pairs={{0,224},{32,0},{64,32},{96,64},{128,96},{160,128},{192,160},{224,1... | collective-permute-start | bytes 491528 | tf_op jit(solution)/shard_map/while/body/ppermute | solution.py:273
  123.7 13.0 %collective-permute-start.30 = (bf16[40,2048]{1,0:T(8,128)(2,1)S(1)}, bf16[40,2048]{1,0:T(8,128)(2,1)S(1)}, u32[]{:S(2)}, u32[]{:S(2)}) collective-permute-start(bf16[40,2048]{1,0:T(8,128)(2,1)S(1)} %add_convert_fusion.8), channel_id=1, source_target_pairs={{0,224},{32,0},{64,32},{96,64},{128,96},{160,128},{192,160},{224,1... | collective-permute-start | bytes 491528 | tf_op jit(solution)/shard_map/while/body/ppermute | solution.py:273
  (14 other events, 248.8 us)

commit v9 on v8

--- a/solution.py
+++ b/solution.py
@@ -12,6 +12,7 @@
 NOTE = 8
 BLOCK = 512
 VMEM_LIMIT = 20 * 1024 * 1024
+PACK_LIMIT = 60 * 1024 * 1024
 EXPERT = ("expert_0", "expert_1", "expert_2")
 DP_EXPERT = ("dp", "expert_0", "expert_1", "expert_2")
 
@@ -120,9 +121,19 @@
     )(*pieces, first_weight, second_weight)
 
 
-def pack_kernel(tokens_ref, ranks_ref, capacity_ref, packed_ref, table_ref, blank_ref):
+def pack_kernel(tokens_far, ranks_far, capacity_far, packed_ref, table_ref, blank_ref, *scratch):
+    tokens_ref, ranks_ref, capacity_ref, sems = scratch
     experts, count = ranks_ref.shape
     width = tokens_ref.shape[1]
+    capacity_copy = pltpu.make_async_copy(capacity_far, capacity_ref, sems.at[0])
+    ranks_copy = pltpu.make_async_copy(ranks_far, ranks_ref, sems.at[1])
+    tokens_copy = pltpu.make_async_copy(tokens_far, tokens_ref, sems.at[2])
+    capacity_copy.start()
+    ranks_copy.start()
+    tokens_copy.start()
+    blank_ref[...] = jnp.zeros(blank_ref.shape, blank_ref.dtype)
+    capacity_copy.wait()
+    ranks_copy.wait()
     square = (experts, experts)
     diagonal = lax.broadcasted_iota(jnp.int32, square, 0) == lax.broadcasted_iota(jnp.int32, square, 1)
     limits = jnp.broadcast_to(capacity_ref[...].astype(jnp.float32), square)
@@ -141,9 +152,9 @@
     for e in range(experts):
         table_ref[e * MOST : (e + 1) * MOST] = jnp.where(place[e : e + 1] == row, 1.0, 0.0).astype(jnp.bfloat16)
     table = table_ref[...]
+    tokens_copy.wait()
     packed = jnp.dot(table, tokens_ref[...], preferred_element_type=jnp.float32)
     packed_ref[:, :width] = packed.astype(jnp.bfloat16)
-    blank_ref[...] = jnp.zeros(blank_ref.shape, blank_ref.dtype)
     ones = jnp.ones((count, LANES), jnp.bfloat16)
     packed_ref[:, width:] = jnp.dot(table, ones, preferred_element_type=jnp.float32).astype(jnp.bfloat16)
 
@@ -158,7 +169,14 @@
             pltpu.HBM((rows_all, count), jnp.bfloat16),
             pltpu.HBM((rows_all, width), jnp.bfloat16),
         ],
-        compiler_params=pltpu.CompilerParams(vmem_limit_bytes=VMEM_LIMIT),
+        in_specs=[pl.BlockSpec(memory_space=pl.ANY)] * 3,
+        scratch_shapes=[
+            pltpu.VMEM(tokens.shape, tokens.dtype),
+            pltpu.VMEM(expert_ranks.shape, expert_ranks.dtype),
+            pltpu.VMEM((1, *capacity.shape), capacity.dtype),
+            pltpu.SemaphoreType.DMA((3,)),
+        ],
+        compiler_params=pltpu.CompilerParams(vmem_limit_bytes=PACK_LIMIT),
         name="pack",
     )(tokens, expert_ranks, capacity[None, :])
 

time: 170 us -> 168 us (0.988)
  local copies, waits for them, and re-layouts: 2.75 us -> 0.11 us
    unnamed x8 -> x2, local copies, waits for them, and re-layouts: 2.64 us -> 0.01 us
where the time goes in v9:
time: 168 us
  waiting for transfers between devices  70.3 us (42%)
  starting transfers between devices  44 us (26%)
  Pallas kernels  25.4 us (15%)
  blocking collectives  23.8 us (14%)
    ppermute x16, waiting for transfers between devices, hop(): up_rows = lax.ppermute(up_rows, 'dp', upward)  49.3 us
    ppermute x16, starting transfers between devices, hop(): down_rows = lax.ppermute(down_rows, 'dp', downward)  28.2 us
    all_to_all x1, blocking collectives, on_device(): lax.all_to_all(sent_back.reshape(expert_count, MOST, width), EXPERT, spli...  23.8 us
    pallas_call x6, Pallas kernels, expert_rows(): pl.pallas_call(staged_expert_kernel if staged else expert_kernel, out_sha...  20.3 us
    all_to_all x1, waiting for transfers between devices, on_device(): lax.all_to_all(packed.reshape(expert_count, MOST, width + LANES), EXPERT,...  17 us
    all_to_all x1, starting transfers between devices, on_device(): lax.all_to_all(packed.reshape(expert_count, MOST, width + LANES), EXPERT,...  8.59 us
    ppermute x16, starting transfers between devices, hop(): up_rows = lax.ppermute(up_rows, 'dp', upward)  7.18 us
    ppermute x16, waiting for transfers between devices, hop(): down_rows = lax.ppermute(down_rows, 'dp', downward)  4.08 us
  transfers between devices with their start and end apart: 33, of which 18 were waited for; matrix products, arithmetic and copies ran while one was open for 1% of the time, Pallas kernels for 12%

profile of v9, /device:TPU:1, one launch (start us, length us, event | category | flops | bytes accessed | tf_op | source)
XLA Modules:
  0.0 168.0 jit_solution(18150329415095469923)
XLA Ops:
  0.0 2.8 %pack.1 = (bf16[256,2176]{1,0:T(8,128)(2,1)}, bf16[256,256]{1,0:T(8,128)(2,1)}, bf16[256,2048]{1,0:T(8,128)(2,1)}) custom-call(bf16[256,2048]{1,0:T(8,128)(2,1)} %tokens_far.1, s32[32,256]{1,0:T(8,128)} %ranks_far.1, s32[1,32]{1,0:T(1,128)} %bitcast.17), custom_call_target="tpu_custom_call" | custom-call | tf_op jit(solution)/shard_map/pack/pallas_call | solution.py:165
  2.8 8.6 %all-to-all-start = ((bf16[32,8,2176]{2,1,0:T(8,128)(2,1)}), bf16[32,8,2176]{2,1,0:T(8,128)(2,1)S(1)}, u32[]{:S(2)}, u32[]{:S(2)}) async-start(bf16[32,8,2176]{2,1,0:T(8,128)(2,1)} %bitcast.16), calls=%async_computation | async-start | bytes 2228224 | tf_op jit(solution)/shard_map/all_to_all | solution.py:362
  12.1 17.0 %all-to-all-done = bf16[32,8,2176]{2,1,0:T(8,128)(2,1)S(1)} async-done(((bf16[32,8,2176]{2,1,0:T(8,128)(2,1)}), bf16[32,8,2176]{2,1,0:T(8,128)(2,1)S(1)}, u32[]{:S(2)}, u32[]{:S(2)}) %all-to-all-start) | async-done | bytes 1114144 | tf_op jit(solution)/shard_map/all_to_all | solution.py:362
  29.0 113.7 %while.11 = (s32[1]{0:T(128)}, s32[1]{0:T(128)}, bf16[256,2048]{1,0:T(8,128)(2,1)}, s32[]{:T(128)}, bf16[256,2176]{1,0:T(8,128)(2,1)S(1)}, /*index=5*/f32[1,384]...) while((s32[1]{0:T(128)}, s32[1]{0:T(128)}, bf16[256,2048]{1,0:T(8,128)(2,1)}, s32[]{:T(128)}, ...), condition=%region_1.0_spmd, body=%region_0.0_spmd | while | flops 10742333440 | bytes 122160512 | solution.py:378
  29.7 5.7 %collective-permute-start.1 = (bf16[80,2048]{1,0:T(8,128)(2,1)S(1)}, bf16[80,2048]{1,0:T(8,128)(2,1)S(1)}, u32[]{:S(2)}, u32[]{:S(2)}) collective-permute-start(bf16[80,2048]{1,0:T(8,128)(2,1)S(1)} %get-tuple-element.42.refs_1_), channel_id=1, source_target_pairs={{0,224},{32,0},{64,32},{96,64},{128,96},{160,128},{192,160},{224,1... | collective-permute-start | bytes 983048 | tf_op jit(solution)/shard_map/while/body/ppermute | solution.py:291
  35.4 2.7 %collective-permute-start.5 = (bf16[80,2048]{1,0:T(8,128)(2,1)S(1)}, bf16[80,2048]{1,0:T(8,128)(2,1)S(1)}, u32[]{:S(2)}, u32[]{:S(2)}) collective-permute-start(bf16[80,2048]{1,0:T(8,128)(2,1)S(1)} %get-tuple-element.41.refs_0_.refs_10_), channel_id=1, source_target_pairs={{0,224},{32,0},{64,32},{96,64},{128,96},{160,128},{192,160},{224,1... | collective-permute-start | bytes 983048 | tf_op jit(solution)/shard_map/while/body/ppermute | solution.py:291
  38.0 5.2 %expert_rows.6 = (f32[80,2048]{1,0:T(8,128)S(1)}, f32[80,2048]{1,0:T(8,128)S(1)}, bf16[2048,1024]{1,0:T(8,128)(2,1)S(1)}, bf16[1024,2048]{1,0:T(8,128)(2,1)S(1)}) custom-call(bf16[80,2048]{1,0:T(8,128)(2,1)S(1)} %get-tuple-element.41.refs_0_.refs_10_, bf16[80,2048]{1,0:T(8,128)(2,1)S(1)} %get-tuple-element.42.refs_1_, bf16[2048,1024]{1,0:T(8,128)(2,1)} %bitcast.12, ...), custom_call_target="tpu_custom_call" | custom-call | flops 1342177280 | bytes 10354688 | tf_op jit(solution)/shard_map/while/body/expert_rows/pallas_call | solution.py:109
  46.9 5.6 %collective-permute-done.4.refs_1_ = bf16[80,2048]{1,0:T(8,128)(2,1)S(1)} collective-permute-done((bf16[80,2048]{1,0:T(8,128)(2,1)S(1)}, bf16[80,2048]{1,0:T(8,128)(2,1)S(1)}, u32[]{:S(2)}, u32[]{:S(2)}) %collective-permute-start.4) | collective-permute-done | bytes 327712 | tf_op jit(solution)/shard_map/while/body/ppermute | solution.py:290
  52.5 2.7 %collective-permute-start.9 = (bf16[80,2048]{1,0:T(8,128)(2,1)S(1)}, bf16[80,2048]{1,0:T(8,128)(2,1)S(1)}, u32[]{:S(2)}, u32[]{:S(2)}) collective-permute-start(bf16[80,2048]{1,0:T(8,128)(2,1)S(1)} %collective-permute-done.5.refs_2_.refs_11_), channel_id=1, source_target_pairs={{0,224},{32,0},{64,32},{96,64},{128,96},{160,128},{192,160},{224,1... | collective-permute-start | bytes 983048 | tf_op jit(solution)/shard_map/while/body/ppermute | solution.py:291
  55.1 3.8 %expert_rows.7 = (f32[80,2048]{1,0:T(8,128)S(1)}, f32[80,2048]{1,0:T(8,128)S(1)}, f32[80,2048]{1,0:T(8,128)S(1)}, f32[80,2048]{1,0:T(8,128)S(1)}) custom-call(bf16[80,2048]{1,0:T(8,128)(2,1)S(1)} %collective-permute-done.refs_0_.refs_17_, bf16[80,2048]{1,0:T(8,128)(2,1)S(1)} %collective-permute-done.4.refs_1_, ...), custom_call_target="tpu_custom_call" | custom-call | flops 2684354560 | bytes 12320768 | tf_op jit(solution)/shard_map/while/body/expert_rows/pallas_call | solution.py:109
  61.0 5.6 %collective-permute-done.8.refs_1_ = bf16[80,2048]{1,0:T(8,128)(2,1)S(1)} collective-permute-done((bf16[80,2048]{1,0:T(8,128)(2,1)S(1)}, bf16[80,2048]{1,0:T(8,128)(2,1)S(1)}, u32[]{:S(2)}, u32[]{:S(2)}) %collective-permute-start.8) | collective-permute-done | bytes 327712 | tf_op jit(solution)/shard_map/while/body/ppermute | solution.py:290
  66.5 2.7 %collective-permute-start.15 = (bf16[80,2048]{1,0:T(8,128)(2,1)S(1)}, bf16[80,2048]{1,0:T(8,128)(2,1)S(1)}, u32[]{:S(2)}, u32[]{:S(2)}) collective-permute-start(bf16[80,2048]{1,0:T(8,128)(2,1)S(1)} %collective-permute-done.9.refs_2_.refs_12_), channel_id=1, source_target_pairs={{0,224},{32,0},{64,32},{96,64},{128,96},{160,128},{192,160},{224,1... | collective-permute-start | bytes 983048 | tf_op jit(solution)/shard_map/while/body/ppermute | solution.py:291
  69.2 3.8 %expert_rows.8 = (f32[80,2048]{1,0:T(8,128)S(1)}, f32[80,2048]{1,0:T(8,128)S(1)}, f32[80,2048]{1,0:T(8,128)S(1)}, f32[80,2048]{1,0:T(8,128)S(1)}) custom-call(bf16[80,2048]{1,0:T(8,128)(2,1)S(1)} %collective-permute-done.2.refs_0_.refs_16_, bf16[80,2048]{1,0:T(8,128)(2,1)S(1)} %collective-permute-done.8.refs_1_, ...), custom_call_target="tpu_custom_call" | custom-call | flops 2684354560 | bytes 12320768 | tf_op jit(solution)/shard_map/while/body/expert_rows/pallas_call | solution.py:109
  77.6 3.0 %collective-permute-done.14.refs_0_ = bf16[80,2048]{1,0:T(8,128)(2,1)S(1)} collective-permute-done((bf16[80,2048]{1,0:T(8,128)(2,1)S(1)}, bf16[80,2048]{1,0:T(8,128)(2,1)S(1)}, u32[]{:S(2)}, u32[]{:S(2)}) %collective-permute-start.14) | collective-permute-done | bytes 327712 | tf_op jit(solution)/shard_map/while/body/ppermute | solution.py:290
  83.4 4.1 %collective-permute-done.12.refs_0_.refs_14_ = bf16[80,2048]{1,0:T(8,128)(2,1)S(1)} collective-permute-done((bf16[80,2048]{1,0:T(8,128)(2,1)S(1)}, bf16[80,2048]{1,0:T(8,128)(2,1)S(1)}, u32[]{:S(2)}, u32[]{:S(2)}) %collective-permute-start.12) | collective-permute-done | bytes 327712 | tf_op jit(solution)/shard_map/while/body/ppermute | solution.py:290
  94.9 2.7 %collective-permute-start.17 = (bf16[80,2048]{1,0:T(8,128)(2,1)S(1)}, bf16[80,2048]{1,0:T(8,128)(2,1)S(1)}, u32[]{:S(2)}, u32[]{:S(2)}) collective-permute-start(bf16[80,2048]{1,0:T(8,128)(2,1)S(1)} %add_convert_fusion.4), channel_id=1, source_target_pairs={{0,224},{32,0},{64,32},{96,64},{128,96},{160,128},{192,160},{224,1... | collective-permute-start | bytes 983048 | tf_op jit(solution)/shard_map/while/body/ppermute | solution.py:291
  97.6 3.7 %collective-permute-done.18 = bf16[80,2048]{1,0:T(8,128)(2,1)S(1)} collective-permute-done((bf16[80,2048]{1,0:T(8,128)(2,1)S(1)}, bf16[80,2048]{1,0:T(8,128)(2,1)S(1)}, u32[]{:S(2)}, u32[]{:S(2)}) %collective-permute-start.18) | collective-permute-done | bytes 327712 | tf_op jit(solution)/shard_map/while/body/ppermute | solution.py:290
  103.1 5.2 %collective-permute-done.16 = bf16[80,2048]{1,0:T(8,128)(2,1)S(1)} collective-permute-done((bf16[80,2048]{1,0:T(8,128)(2,1)S(1)}, bf16[80,2048]{1,0:T(8,128)(2,1)S(1)}, u32[]{:S(2)}, u32[]{:S(2)}) %collective-permute-start.16) | collective-permute-done | bytes 327712 | tf_op jit(solution)/shard_map/while/body/ppermute | solution.py:290
  108.5 3.6 %collective-permute-done.22 = bf16[80,2048]{1,0:T(8,128)(2,1)S(1)} collective-permute-done((bf16[80,2048]{1,0:T(8,128)(2,1)S(1)}, bf16[80,2048]{1,0:T(8,128)(2,1)S(1)}, u32[]{:S(2)}, u32[]{:S(2)}) %collective-permute-start.22) | collective-permute-done | bytes 327712 | tf_op jit(solution)/shard_map/while/body/ppermute | solution.py:291
  114.8 2.7 %collective-permute-start.24 = (bf16[40,2048]{1,0:T(8,128)(2,1)S(1)}, bf16[40,2048]{1,0:T(8,128)(2,1)S(1)}, u32[]{:S(2)}, u32[]{:S(2)}) collective-permute-start(bf16[40,2048]{1,0:T(8,128)(2,1)S(1)} %get-tuple-element.123), channel_id=1, source_target_pairs={{0,224},{32,0},{64,32},{96,64},{128,96},{160,128},{192,160},{224,1... | collective-permute-start | bytes 491528 | tf_op jit(solution)/shard_map/while/body/ppermute | solution.py:291
  123.1 8.6 %collective-permute-done.26 = bf16[40,2048]{1,0:T(8,128)(2,1)S(1)} collective-permute-done((bf16[40,2048]{1,0:T(8,128)(2,1)S(1)}, bf16[40,2048]{1,0:T(8,128)(2,1)S(1)}, u32[]{:S(2)}, u32[]{:S(2)}) %collective-permute-start.26) | collective-permute-done | bytes 163872 | tf_op jit(solution)/shard_map/while/body/ppermute | solution.py:290
  131.9 2.7 %collective-permute-start.31 = (bf16[40,2048]{1,0:T(8,128)(2,1)S(1)}, bf16[40,2048]{1,0:T(8,128)(2,1)S(1)}, u32[]{:S(2)}, u32[]{:S(2)}) collective-permute-start(bf16[40,2048]{1,0:T(8,128)(2,1)S(1)} %add_convert_fusion.6), channel_id=1, source_target_pairs={{0,224},{32,0},{64,32},{96,64},{128,96},{160,128},{192,160},{224,1... | collective-permute-start | bytes 491528 | tf_op jit(solution)/shard_map/while/body/ppermute | solution.py:291
  137.1 2.7 %collective-permute-done.28.refs_5_ = bf16[40,2048]{1,0:T(8,128)(2,1)S(1)} collective-permute-done((bf16[40,2048]{1,0:T(8,128)(2,1)S(1)}, bf16[40,2048]{1,0:T(8,128)(2,1)S(1)}, u32[]{:S(2)}, u32[]{:S(2)}) %collective-permute-start.28) | collective-permute-done | bytes 163872 | tf_op jit(solution)/shard_map/while/body/ppermute | solution.py:290
  142.8 23.8 %all_to_all.10 = bf16[32,8,2048]{2,1,0:T(8,128)(2,1)S(1)} all-to-all(bf16[32,8,2048]{2,1,0:T(8,128)(2,1)} %bitcast.15), channel_id=1, replica_groups=mesh['dp'=8,'expert_0'=4,'expert_1'=4,'expert_2'=2] {'expert_0','expert_..., dimensions={0} | all-to-all | bytes 2097152 | tf_op jit(solution)/shard_map/all_to_all | solution.py:383
  (73 shorter events, 37.5 us)
Async XLA Ops:
  2.8 26.2 %all-to-all-start = ((bf16[32,8,2176]{2,1,0:T(8,128)(2,1)}), bf16[32,8,2176]{2,1,0:T(8,128)(2,1)S(1)}, u32[]{:S(2)}, u32[]{:S(2)}) async-start(bf16[32,8,2176]{2,1,0:T(8,128)(2,1)} %bitcast.16), calls=%async_computation | async-start | bytes 2228224 | tf_op jit(solution)/shard_map/all_to_all | solution.py:362
  29.7 13.5 %collective-permute-start.1 = (bf16[80,2048]{1,0:T(8,128)(2,1)S(1)}, bf16[80,2048]{1,0:T(8,128)(2,1)S(1)}, u32[]{:S(2)}, u32[]{:S(2)}) collective-permute-start(bf16[80,2048]{1,0:T(8,128)(2,1)S(1)} %get-tuple-element.42.refs_1_), channel_id=1, source_target_pairs={{0,224},{32,0},{64,32},{96,64},{128,96},{160,128},{192,160},{224,1... | collective-permute-start | bytes 983048 | tf_op jit(solution)/shard_map/while/body/ppermute | solution.py:291
  35.4 17.1 %collective-permute-start.4 = (bf16[80,2048]{1,0:T(8,128)(2,1)S(1)}, bf16[80,2048]{1,0:T(8,128)(2,1)S(1)}, u32[]{:S(2)}, u32[]{:S(2)}) collective-permute-start(bf16[80,2048]{1,0:T(8,128)(2,1)S(1)} %get-tuple-element.42.refs_1_), channel_id=1, source_target_pairs={{0,32},{32,64},{64,96},{96,128},{128,160},{160,192},{192,224},{224... | collective-permute-start | bytes 983048 | tf_op jit(solution)/shard_map/while/body/ppermute | solution.py:290
  35.4 17.1 %collective-permute-start.5 = (bf16[80,2048]{1,0:T(8,128)(2,1)S(1)}, bf16[80,2048]{1,0:T(8,128)(2,1)S(1)}, u32[]{:S(2)}, u32[]{:S(2)}) collective-permute-start(bf16[80,2048]{1,0:T(8,128)(2,1)S(1)} %get-tuple-element.41.refs_0_.refs_10_), channel_id=1, source_target_pairs={{0,224},{32,0},{64,32},{96,64},{128,96},{160,128},{192,160},{224,1... | collective-permute-start | bytes 983048 | tf_op jit(solution)/shard_map/while/body/ppermute | solution.py:291
  45.4 13.5 %collective-permute-start.3 = (bf16[80,2048]{1,0:T(8,128)(2,1)S(1)}, bf16[80,2048]{1,0:T(8,128)(2,1)S(1)}, u32[]{:S(2)}, u32[]{:S(2)}) collective-permute-start(bf16[80,2048]{1,0:T(8,128)(2,1)S(1)} %collective-permute-done.1.refs_3_), channel_id=1, source_target_pairs={{0,224},{32,0},{64,32},{96,64},{128,96},{160,128},{192,160},{224,1... | collective-permute-start | bytes 983048 | tf_op jit(solution)/shard_map/while/body/ppermute | solution.py:291
  45.7 13.8 %collective-permute-start.2 = (bf16[80,2048]{1,0:T(8,128)(2,1)S(1)}, bf16[80,2048]{1,0:T(8,128)(2,1)S(1)}, u32[]{:S(2)}, u32[]{:S(2)}) collective-permute-start(bf16[80,2048]{1,0:T(8,128)(2,1)S(1)} %collective-permute-done.refs_0_.refs_17_), channel_id=1, source_target_pairs={{0,32},{32,64},{64,96},{96,128},{128,160},{160,192},{192,224},{224... | collective-permute-start | bytes 983048 | tf_op jit(solution)/shard_map/while/body/ppermute | solution.py:290
  52.5 14.0 %collective-permute-start.8 = (bf16[80,2048]{1,0:T(8,128)(2,1)S(1)}, bf16[80,2048]{1,0:T(8,128)(2,1)S(1)}, u32[]{:S(2)}, u32[]{:S(2)}) collective-permute-start(bf16[80,2048]{1,0:T(8,128)(2,1)S(1)} %collective-permute-done.4.refs_1_), channel_id=1, source_target_pairs={{0,32},{32,64},{64,96},{96,128},{128,160},{160,192},{192,224},{224... | collective-permute-start | bytes 983048 | tf_op jit(solution)/shard_map/while/body/ppermute | solution.py:290
  52.5 14.0 %collective-permute-start.9 = (bf16[80,2048]{1,0:T(8,128)(2,1)S(1)}, bf16[80,2048]{1,0:T(8,128)(2,1)S(1)}, u32[]{:S(2)}, u32[]{:S(2)}) collective-permute-start(bf16[80,2048]{1,0:T(8,128)(2,1)S(1)} %collective-permute-done.5.refs_2_.refs_11_), channel_id=1, source_target_pairs={{0,224},{32,0},{64,32},{96,64},{128,96},{160,128},{192,160},{224,1... | collective-permute-start | bytes 983048 | tf_op jit(solution)/shard_map/while/body/ppermute | solution.py:291
  59.5 13.5 %collective-permute-start.7 = (bf16[80,2048]{1,0:T(8,128)(2,1)S(1)}, bf16[80,2048]{1,0:T(8,128)(2,1)S(1)}, u32[]{:S(2)}, u32[]{:S(2)}) collective-permute-start(bf16[80,2048]{1,0:T(8,128)(2,1)S(1)} %collective-permute-done.3.refs_3_), channel_id=1, source_target_pairs={{0,224},{32,0},{64,32},{96,64},{128,96},{160,128},{192,160},{224,1... | collective-permute-start | bytes 983048 | tf_op jit(solution)/shard_map/while/body/ppermute | solution.py:291
  59.8 13.8 %collective-permute-start.6 = (bf16[80,2048]{1,0:T(8,128)(2,1)S(1)}, bf16[80,2048]{1,0:T(8,128)(2,1)S(1)}, u32[]{:S(2)}, u32[]{:S(2)}) collective-permute-start(bf16[80,2048]{1,0:T(8,128)(2,1)S(1)} %collective-permute-done.2.refs_0_.refs_16_), channel_id=1, source_target_pairs={{0,32},{32,64},{64,96},{96,128},{128,160},{160,192},{192,224},{224... | collective-permute-start | bytes 983048 | tf_op jit(solution)/shard_map/while/body/ppermute | solution.py:290
  66.5 14.0 %collective-permute-start.14 = (bf16[80,2048]{1,0:T(8,128)(2,1)S(1)}, bf16[80,2048]{1,0:T(8,128)(2,1)S(1)}, u32[]{:S(2)}, u32[]{:S(2)}) collective-permute-start(bf16[80,2048]{1,0:T(8,128)(2,1)S(1)} %collective-permute-done.8.refs_1_), channel_id=1, source_target_pairs={{0,32},{32,64},{64,96},{96,128},{128,160},{160,192},{192,224},{224... | collective-permute-start | bytes 983048 | tf_op jit(solution)/shard_map/while/body/ppermute | solution.py:290
  66.5 14.0 %collective-permute-start.15 = (bf16[80,2048]{1,0:T(8,128)(2,1)S(1)}, bf16[80,2048]{1,0:T(8,128)(2,1)S(1)}, u32[]{:S(2)}, u32[]{:S(2)}) collective-permute-start(bf16[80,2048]{1,0:T(8,128)(2,1)S(1)} %collective-permute-done.9.refs_2_.refs_12_), channel_id=1, source_target_pairs={{0,224},{32,0},{64,32},{96,64},{128,96},{160,128},{192,160},{224,1... | collective-permute-start | bytes 983048 | tf_op jit(solution)/shard_map/while/body/ppermute | solution.py:291
  73.5 14.0 %collective-permute-start.12 = (bf16[80,2048]{1,0:T(8,128)(2,1)S(1)}, bf16[80,2048]{1,0:T(8,128)(2,1)S(1)}, u32[]{:S(2)}, u32[]{:S(2)}) collective-permute-start(bf16[80,2048]{1,0:T(8,128)(2,1)S(1)} %collective-permute-done.6.refs_0_.refs_15_), channel_id=1, source_target_pairs={{0,32},{32,64},{64,96},{96,128},{128,160},{160,192},{192,224},{224... | collective-permute-start | bytes 983048 | tf_op jit(solution)/shard_map/while/body/ppermute | solution.py:290
  77.5 17.1 %collective-permute-start.10 = (bf16[80,2048]{1,0:T(8,128)(2,1)S(1)}, bf16[80,2048]{1,0:T(8,128)(2,1)S(1)}, u32[]{:S(2)}, u32[]{:S(2)}) collective-permute-start(bf16[80,2048]{1,0:T(8,128)(2,1)S(1)} %get-tuple-element.67), channel_id=1, source_target_pairs={{0,32},{32,64},{64,96},{96,128},{128,160},{160,192},{192,224},{224... | collective-permute-start | bytes 983048 | tf_op jit(solution)/shard_map/while/body/ppermute | solution.py:290
  80.6 14.0 %collective-permute-start.11 = (bf16[80,2048]{1,0:T(8,128)(2,1)S(1)}, bf16[80,2048]{1,0:T(8,128)(2,1)S(1)}, u32[]{:S(2)}, u32[]{:S(2)}) collective-permute-start(bf16[80,2048]{1,0:T(8,128)(2,1)S(1)} %get-tuple-element.68), channel_id=1, source_target_pairs={{0,224},{32,0},{64,32},{96,64},{128,96},{160,128},{192,160},{224,1... | collective-permute-start | bytes 983048 | tf_op jit(solution)/shard_map/while/body/ppermute | solution.py:291
  90.1 11.2 %collective-permute-start.18 = (bf16[80,2048]{1,0:T(8,128)(2,1)S(1)}, bf16[80,2048]{1,0:T(8,128)(2,1)S(1)}, u32[]{:S(2)}, u32[]{:S(2)}) collective-permute-start(bf16[80,2048]{1,0:T(8,128)(2,1)S(1)} %get-tuple-element.77), channel_id=1, source_target_pairs={{0,32},{32,64},{64,96},{96,128},{128,160},{160,192},{192,224},{224... | collective-permute-start | bytes 983048 | tf_op jit(solution)/shard_map/while/body/ppermute | solution.py:290
  94.7 13.6 %collective-permute-start.16 = (bf16[80,2048]{1,0:T(8,128)(2,1)S(1)}, bf16[80,2048]{1,0:T(8,128)(2,1)S(1)}, u32[]{:S(2)}, u32[]{:S(2)}) collective-permute-start(bf16[80,2048]{1,0:T(8,128)(2,1)S(1)} %add_convert_fusion.5), channel_id=1, source_target_pairs={{0,32},{32,64},{64,96},{96,128},{128,160},{160,192},{192,224},{224... | collective-permute-start | bytes 983048 | tf_op jit(solution)/shard_map/while/body/ppermute | solution.py:290
  94.9 13.5 %collective-permute-start.17 = (bf16[80,2048]{1,0:T(8,128)(2,1)S(1)}, bf16[80,2048]{1,0:T(8,128)(2,1)S(1)}, u32[]{:S(2)}, u32[]{:S(2)}) collective-permute-start(bf16[80,2048]{1,0:T(8,128)(2,1)S(1)} %add_convert_fusion.4), channel_id=1, source_target_pairs={{0,224},{32,0},{64,32},{96,64},{128,96},{160,128},{192,160},{224,1... | collective-permute-start | bytes 983048 | tf_op jit(solution)/shard_map/while/body/ppermute | solution.py:291
  101.6 13.0 %collective-permute-start.21 = (bf16[80,2048]{1,0:T(8,128)(2,1)S(1)}, bf16[80,2048]{1,0:T(8,128)(2,1)S(1)}, u32[]{:S(2)}, u32[]{:S(2)}) collective-permute-start(bf16[80,2048]{1,0:T(8,128)(2,1)S(1)} %add_convert_fusion.3), channel_id=1, source_target_pairs={{0,32},{32,64},{64,96},{96,128},{128,160},{160,192},{192,224},{224... | collective-permute-start | bytes 983048 | tf_op jit(solution)/shard_map/while/body/ppermute | solution.py:290
  117.6 14.4 %collective-permute-start.20 = (bf16[80,2048]{1,0:T(8,128)(2,1)S(1)}, bf16[80,2048]{1,0:T(8,128)(2,1)S(1)}, u32[]{:S(2)}, u32[]{:S(2)}) collective-permute-start(bf16[80,2048]{1,0:T(8,128)(2,1)S(1)} %add_convert_fusion.1), channel_id=1, source_target_pairs={{0,224},{32,0},{64,32},{96,64},{128,96},{160,128},{192,160},{224,1... | collective-permute-start | bytes 983048 | tf_op jit(solution)/shard_map/while/body/ppermute | solution.py:291
  117.6 17.1 %collective-permute-start.29 = (bf16[80,2048]{1,0:T(8,128)(2,1)S(1)}, bf16[80,2048]{1,0:T(8,128)(2,1)S(1)}, u32[]{:S(2)}, u32[]{:S(2)}) collective-permute-start(bf16[80,2048]{1,0:T(8,128)(2,1)S(1)} %add_convert_fusion), channel_id=1, source_target_pairs={{0,32},{32,64},{64,96},{96,128},{128,160},{160,192},{192,224},{224... | collective-permute-start | bytes 983048 | tf_op jit(solution)/shard_map/while/body/ppermute | solution.py:290
  119.0 12.7 %collective-permute-start.26 = (bf16[40,2048]{1,0:T(8,128)(2,1)S(1)}, bf16[40,2048]{1,0:T(8,128)(2,1)S(1)}, u32[]{:S(2)}, u32[]{:S(2)}) collective-permute-start(bf16[40,2048]{1,0:T(8,128)(2,1)S(1)} %get-tuple-element.124), channel_id=1, source_target_pairs={{0,32},{32,64},{64,96},{96,128},{128,160},{160,192},{192,224},{224... | collective-permute-start | bytes 491528 | tf_op jit(solution)/shard_map/while/body/ppermute | solution.py:290
  120.1 11.6 %collective-permute-start.27 = (bf16[40,2048]{1,0:T(8,128)(2,1)S(1)}, bf16[40,2048]{1,0:T(8,128)(2,1)S(1)}, u32[]{:S(2)}, u32[]{:S(2)}) collective-permute-start(bf16[40,2048]{1,0:T(8,128)(2,1)S(1)} %get-tuple-element.122), channel_id=1, source_target_pairs={{0,224},{32,0},{64,32},{96,64},{128,96},{160,128},{192,160},{224,1... | collective-permute-start | bytes 491528 | tf_op jit(solution)/shard_map/while/body/ppermute | solution.py:291
  121.8 13.0 %collective-permute-start.30 = (bf16[40,2048]{1,0:T(8,128)(2,1)S(1)}, bf16[40,2048]{1,0:T(8,128)(2,1)S(1)}, u32[]{:S(2)}, u32[]{:S(2)}) collective-permute-start(bf16[40,2048]{1,0:T(8,128)(2,1)S(1)} %add_convert_fusion.8), channel_id=1, source_target_pairs={{0,224},{32,0},{64,32},{96,64},{128,96},{160,128},{192,160},{224,1... | collective-permute-start | bytes 491528 | tf_op jit(solution)/shard_map/while/body/ppermute | solution.py:291
  (11 other events, 246.2 us)
